TPU v7x, 32 devices: a whole 2x2x4 slice. The times are simulated.
32 devices in a mesh: surf: 8 (over z, y), pair: 4 (over x, core).
Axes of the slice: x: 2, y: 2, z: 4, core: 2. Of those that a mesh axis runs over, the one named last changes fastest.
Arguments:
- left_panel: bfloat16 [64, 4, 128, 192], P(('surf', 'pair')), may hold values from -0.5 to 0.5
- right_panel: bfloat16 [64, 4, 128, 192], P(('surf', 'pair')), may hold values from -6 to 6
- inverse: bfloat16 [64, 128, 128], P(('surf', 'pair')), may hold values from -0.5 to 0.5
- target: int32 [64, 4, 4], P(('surf', 'pair')), may hold values from 0 to 127, as said below
- blocks: float32 [128, 192, 192], P(('surf', 'pair')), may hold values from -12 to 12
- weights: bfloat16 [128, 192, 512], P('surf', None, 'pair'), may hold values from -0.109375 to 0.109375
Outputs:
- updated: float32 [128, 192, 192], P(('surf', 'pair'))
- coarse_panel: float32 [1536, 512], P('surf', 'pair')
Inputs may be any that keep to these rules, and one draw needn't show every extreme that they name: target[b, k, l] = target[b, l, k]. Pair block p lies on device p // 4 of the joined axes; the block of every term lies on a device with the same index along pair as the box's device, whose index along surf differs from the box's device's by at most 2 along the closed loop of 8 tiles. From the boxes of one device at most 8 unordered neighbour pairs (k <= l) go to any one tile, and every device sends exactly 8 to some tile in every draw.
All inputs are finite; a program needn't handle non-finite values.
Results may differ from a plain program's by a relative error of at most 0.0055.
Values may be sent and summed in bfloat16 or wider, within the bound.
No kernel may reach another device: no remote copies, remote signals or barrier semaphores. Data moves between devices by JAX's collectives and lax.ppermute only.
A program may use at most 64 MiB of HBM per device.

v0:
```python
import jax
import jax.numpy as jnp
import numpy as np
from jax import lax
from jax.sharding import PartitionSpec as P

REACH = 2


def from_behind(shard, axis, by):
    count = lax.axis_size(axis)
    return lax.ppermute(shard, axis, [(i, (i + by) % count) for i in range(count)])


def unit_tables(neighbours):
    firsts = []
    seconds = []
    for first in range(neighbours):
        for second in range(first, neighbours):
            firsts.append(first)
            seconds.append(second)
    return (np.array(firsts, np.int32), np.array(seconds, np.int32))


def body(left_panel, right_panel, inverse, target, blocks, weights):
    box_count, neighbours, redundant, skeleton = left_panel.shape
    surf_count = lax.axis_size("surf")
    pair_count = lax.axis_size("pair")
    local_pairs = blocks.shape[0]
    spots = 2 * REACH + 1
    solved = jnp.einsum(
        "bij,bkjc->bkic", inverse, right_panel, preferred_element_type=jnp.float32
    ).astype(jnp.bfloat16)
    firsts, seconds = unit_tables(neighbours)
    per_box = firsts.shape[0]
    item_count = box_count * per_box
    unit_target = target[:, firsts, seconds].reshape(-1)
    dest_tile = unit_target // (local_pairs * pair_count)
    block_slot = unit_target % local_pairs
    relative = (dest_tile - lax.axis_index("surf") + surf_count) % surf_count
    spot = jnp.where(relative <= REACH, relative, relative - surf_count) + REACH
    products = (
        jnp.einsum("bkri,blrj->bklij", left_panel, solved, preferred_element_type=jnp.float32)
        .astype(jnp.bfloat16)
        .reshape(box_count * neighbours * neighbours, skeleton, skeleton)
    )
    item_box = jnp.arange(item_count, dtype=jnp.int32) // per_box
    item_first = jnp.tile(jnp.asarray(firsts), box_count)
    item_second = jnp.tile(jnp.asarray(seconds), box_count)
    direct_terms = products[(item_box * neighbours + item_first) * neighbours + item_second]
    swapped_terms = products[(item_box * neighbours + item_second) * neighbours + item_first]
    destination = spot * local_pairs + block_slot
    selector = jnp.arange(spots * local_pairs)[:, None] == destination[None, :]
    direct_pick = selector.astype(jnp.bfloat16)
    swapped_pick = (selector & (item_first != item_second)[None, :]).astype(jnp.bfloat16)
    grouped = jnp.einsum(
        "ps,sij->pij", direct_pick, direct_terms, preferred_element_type=jnp.float32
    )
    grouped = grouped + jnp.einsum(
        "ps,sji->pij", swapped_pick, swapped_terms, preferred_element_type=jnp.float32
    )
    grouped = grouped.reshape(spots, local_pairs, skeleton, skeleton)
    total = jnp.zeros((local_pairs, skeleton, skeleton), jnp.float32)
    for offset in range(-REACH, REACH + 1):
        piece = grouped[offset + REACH]
        if offset != 0:
            piece = from_behind(piece, "surf", offset)
        total = total + piece
    updated = blocks - total
    rounded = updated.astype(jnp.bfloat16)
    coarse_panel = jnp.einsum(
        "pij,pjc->ic",
        lax.all_gather(rounded, "pair", axis=0, tiled=True),
        weights,
        preferred_element_type=jnp.float32,
    )
    return (updated, coarse_panel)


def solution(mesh):
    in_specs = (
        P(("surf", "pair"), None, None, None),
        P(("surf", "pair"), None, None, None),
        P(("surf", "pair"), None, None),
        P(("surf", "pair"), None, None),
        P(("surf", "pair"), None, None),
        P("surf", None, "pair"),
    )
    out_specs = (P(("surf", "pair"), None, None), P("surf", "pair"))
    return jax.shard_map(body, mesh=mesh, in_specs=in_specs, out_specs=out_specs, check_vma=False)
```

profile of v0, /device:TPU:0, one launch (start us, length us, event | category | flops | bytes accessed | tf_op | source)
XLA Modules:
  0.0 124.8 jit_solution(15489694525526723392)
XLA Ops:
  7.2 0.0 copy-start
  7.2 0.0 all-gather.2.cloned.1.call-start
  7.2 0.7 tile.24
  8.0 0.1 ne.104
  8.0 0.7 tile.20
  8.7 0.1 tile.21
  8.8 0.7 tile.22
  9.4 0.1 tile.23
  9.5 0.8 copy.27
  10.3 0.8 gather_fusion
  11.1 0.1 copy.28
  11.2 0.1 reshape.202
  11.3 3.9 %convert_bitcast_fusion = bf16[2,4,4,192,192]{3,4,1,2,0:T(8,128)(2,1)} fusion(bf16[2,4,128,192]{2,3,1,0:T(8,128)(2,1)} %param.11, bf16[2,4,128,192]{2,3,1,0:T(8,128)(2,1)} %param.10, bf16[2,128,128]{2,1,0:T(8,128)(2,1)} %param.12), kind=kOutput, calls=%fused_computation.4 | convolution fusion | flops 353697792 | bytes 3211264 | tf_op jit(solution)/shard_map/bkri,blrj->bklij/dot_general | solution.py:43
  15.2 4.8 %copy.29 = bf16[2,4,4,192,192]{4,3,2,1,0:T(8,128)(2,1)} copy(bf16[2,4,4,192,192]{3,4,1,2,0:T(8,128)(2,1)} %convert_bitcast_fusion) | data formatting | bytes 4718592 | tf_op jit(solution)/shard_map/convert_element_type | solution.py:44
  20.0 4.0 %gather_fusion.2 = bf16[20,192,192]{2,1,0:T(8,128)(2,1)} fusion(bf16[32,192,192]{2,1,0:T(8,128)(2,1)} %bitcast.41, s32[1024]{0:T(1024)S(1)} %get-tuple-element.16), kind=kCustom, calls=%fused_computation.2 | custom fusion | bytes 2949200 | tf_op jit(solution)/shard_map/gather | solution.py:51
  24.0 2.6 %gather_fusion.1 = bf16[20,192,192]{2,1,0:T(8,128)(2,1)S(1)} fusion(bf16[32,192,192]{2,1,0:T(8,128)(2,1)} %bitcast.42, s32[1024]{0:T(1024)S(1)} %get-tuple-element.17), kind=kCustom, calls=%fused_computation.1 | custom fusion | bytes 2949200 | tf_op jit(solution)/shard_map/gather | solution.py:50
  26.6 4.7 %copy.31 = bf16[20,192,192]{1,0,2:T(8,128)(2,1)} copy(bf16[20,192,192]{2,1,0:T(8,128)(2,1)} %gather_fusion.2) | data formatting | bytes 2949120 | tf_op jit(solution)/shard_map/gather | solution.py:51
  31.3 2.4 %fusion.15 = f32[192,192,20]{0,2,1:T(8,128)S(1)} fusion(bf16[20,192,192]{1,0,2:T(8,128)(2,1)} %copy.31, s32[20]{0:T(128)S(1)} %fusion.20, pred[20]{0:T(512)(128)(4,1)S(1)} %ne.104), kind=kOutput, calls=%fused_computation.20 | convolution fusion | flops 29492000 | bytes 4423780 | tf_op jit(solution)/shard_map/ps,sji->pij/dot_general | solution.py:59
  33.7 1.9 %bitcast_add_fusion = f32[20,192,192]{2,0,1:T(8,128)S(1)} fusion(f32[192,192,20]{0,2,1:T(8,128)S(1)} %fusion.15, bf16[20,192,192]{2,1,0:T(8,128)(2,1)S(1)} %gather_fusion.1, s32[20]{0:T(128)S(1)} %fusion.20), kind=kOutput, calls=%fused_computation.3 | convolution fusion | flops 30228880 | bytes 7372880 | tf_op jit(solution)/shard_map/ps,sij->pij/dot_general | solution.py:56
  35.6 0.5 fusion.29
  36.2 6.1 %collective-permute-start.1 = (f32[4,192,192]{2,0,1:T(4,128)S(1)}, f32[4,192,192]{2,0,1:T(4,128)S(1)}, u32[]{:S(2)}, u32[]{:S(2)}) collective-permute-start(f32[4,192,192]{2,0,1:T(4,128)S(1)} %get-tuple-element.10), channel_id=1, source_target_pairs={{0,28},{4,0},{8,4},{12,8},{16,12},{20,16},{24,20},{28,24},{1,29},{... | collective-permute-start | bytes 1769480 | tf_op jit(solution)/shard_map/ppermute | solution.py:12
  42.2 3.8 %collective-permute-start = (f32[4,192,192]{2,0,1:T(4,128)S(1)}, f32[4,192,192]{2,0,1:T(4,128)S(1)}, u32[]{:S(2)}, u32[]{:S(2)}) collective-permute-start(f32[4,192,192]{2,0,1:T(4,128)S(1)} %get-tuple-element.13), channel_id=1, source_target_pairs={{0,24},{4,28},{8,0},{12,4},{16,8},{20,12},{24,16},{28,20},{1,25},{... | collective-permute-start | bytes 1769480 | tf_op jit(solution)/shard_map/ppermute | solution.py:12
  46.1 14.1 %collective-permute-done.1 = f32[4,192,192]{2,0,1:T(4,128)S(1)} collective-permute-done((f32[4,192,192]{2,0,1:T(4,128)S(1)}, f32[4,192,192]{2,0,1:T(4,128)S(1)}, u32[]{:S(2)}, u32[]{:S(2)}) %collective-permute-start.1) | collective-permute-done | bytes 589856 | tf_op jit(solution)/shard_map/ppermute | solution.py:12
  60.2 17.9 %collective-permute-done.3 = f32[4,192,192]{2,0,1:T(4,128)S(1)} collective-permute-done((f32[4,192,192]{2,0,1:T(4,128)S(1)}, f32[4,192,192]{2,0,1:T(4,128)S(1)}, u32[]{:S(2)}, u32[]{:S(2)}) %collective-permute-start.3) | collective-permute-done | bytes 589856 | tf_op jit(solution)/shard_map/ppermute | solution.py:12
  78.0 0.1 collective-permute-done.2
  78.1 14.7 %collective-permute-done = f32[4,192,192]{2,0,1:T(4,128)S(1)} collective-permute-done((f32[4,192,192]{2,0,1:T(4,128)S(1)}, f32[4,192,192]{2,0,1:T(4,128)S(1)}, u32[]{:S(2)}, u32[]{:S(2)}) %collective-permute-start) | collective-permute-done | bytes 589856 | tf_op jit(solution)/shard_map/ppermute | solution.py:12
  92.8 1.1 fusion.27
  93.9 0.8 copy.33
  94.6 0.0 all-gather.2.cloned.1.call-update
  94.7 1.0 copy.34
  95.7 19.7 %all-gather.2.cloned.1.call-done = bf16[16,192,192]{2,1,0:T(8,128)(2,1)} async-done(((bf16[4,192,192]{2,1,0:T(8,128)(2,1)}), bf16[16,192,192]{2,1,0:T(8,128)(2,1)}) %all-gather.2.cloned.1.call-update) | async-done | bytes 1179664 | tf_op jit(solution)/shard_map/all_gather | solution.py:73
  115.4 2.6 %convolution_bitcast_fusion = f32[192,128]{1,0:T(8,128)} fusion(bf16[16,192,192]{2,1,0:T(8,128)(2,1)} %all-gather.2.cloned.1.call-done, bf16[16,192,128]{2,1,0:T(8,128)(2,1)S(1)} %copy-done), kind=kOutput, calls=%fused_computation.9 | convolution fusion | flops 150994944 | bytes 2064384 | tf_op jit(solution)/shard_map/pij,pjc->ic/dot_general | solution.py:71
  (8 shorter events, 0.1 us)
Async XLA Ops:
  7.2 108.3 %copy-start = (bf16[16,192,128]{2,1,0:T(8,128)(2,1)S(1)}, bf16[16,192,128]{2,1,0:T(8,128)(2,1)}, u32[]{:S(2)}) copy-start(bf16[16,192,128]{2,1,0:T(8,128)(2,1)} %param.15) | copy-start | bytes 2359300
  7.2 108.2 %all-gather.2.cloned.1.call-start = ((), (), s32[]{:S(2)}) async-start(), calls=%async_computation | async-start | bytes 1966080 | tf_op jit(solution)/shard_map/all_gather | solution.py:73
  35.6 57.2 %copy-start.1 = (f32[4,192,192]{2,1,0:T(8,128)S(1)}, f32[4,192,192]{2,1,0:T(8,128)}, u32[]{:S(2)}) copy-start(f32[4,192,192]{2,1,0:T(8,128)} %param.14) | copy-start | bytes 1769476
  36.2 24.0 %collective-permute-start.1 = (f32[4,192,192]{2,0,1:T(4,128)S(1)}, f32[4,192,192]{2,0,1:T(4,128)S(1)}, u32[]{:S(2)}, u32[]{:S(2)}) collective-permute-start(f32[4,192,192]{2,0,1:T(4,128)S(1)} %get-tuple-element.10), channel_id=1, source_target_pairs={{0,28},{4,0},{8,4},{12,8},{16,12},{20,16},{24,20},{28,24},{1,29},{... | collective-permute-start | bytes 1769480 | tf_op jit(solution)/shard_map/ppermute | solution.py:12
  42.2 35.8 %collective-permute-start.3 = (f32[4,192,192]{2,0,1:T(4,128)S(1)}, f32[4,192,192]{2,0,1:T(4,128)S(1)}, u32[]{:S(2)}, u32[]{:S(2)}) collective-permute-start(f32[4,192,192]{2,0,1:T(4,128)S(1)} %get-tuple-element.11), channel_id=1, source_target_pairs={{0,8},{4,12},{8,16},{12,20},{16,24},{20,28},{24,0},{28,4},{1,9},{5... | collective-permute-start | bytes 1769480 | tf_op jit(solution)/shard_map/ppermute | solution.py:12
  42.2 35.8 %collective-permute-start.2 = (f32[4,192,192]{2,0,1:T(4,128)S(1)}, f32[4,192,192]{2,0,1:T(4,128)S(1)}, u32[]{:S(2)}, u32[]{:S(2)}) collective-permute-start(f32[4,192,192]{2,0,1:T(4,128)S(1)} %get-tuple-element.12), channel_id=1, source_target_pairs={{0,4},{4,8},{8,12},{12,16},{16,20},{20,24},{24,28},{28,0},{1,5},{5... | collective-permute-start | bytes 1769480 | tf_op jit(solution)/shard_map/ppermute | solution.py:12
  42.2 50.5 %collective-permute-start = (f32[4,192,192]{2,0,1:T(4,128)S(1)}, f32[4,192,192]{2,0,1:T(4,128)S(1)}, u32[]{:S(2)}, u32[]{:S(2)}) collective-permute-start(f32[4,192,192]{2,0,1:T(4,128)S(1)} %get-tuple-element.13), channel_id=1, source_target_pairs={{0,24},{4,28},{8,0},{12,4},{16,8},{20,12},{24,16},{28,20},{1,25},{... | collective-permute-start | bytes 1769480 | tf_op jit(solution)/shard_map/ppermute | solution.py:12
Sparse Core Ops, SparseCore 0:
  94.8 20.5 all-gather.1
where the time goes:
time: 125 us
  waiting for transfers between devices  66.5 us (53%)
  local copies, waits for them, and re-layouts  22.4 us (18%)
  between operations  14.1 us (11%)
  matrix products  10.8 us (9%)
  starting transfers between devices  9.95 us (8%)
    ppermute x4, waiting for transfers between devices, from_behind(): lax.ppermute(shard, axis, [(i, (i + by) % count) for i in range(count)])  46.7 us
    all_gather x1, waiting for transfers between devices, body(): lax.all_gather(rounded, 'pair', axis=0, tiled=True)  19.7 us
    ppermute x4, starting transfers between devices, from_behind(): lax.ppermute(shard, axis, [(i, (i + by) % count) for i in range(count)])  9.91 us
    gather x2, local copies, waits for them, and re-layouts, body(): products[(item_box * neighbours + item_second) * neighbours + item_first]  8.7 us
    convert_element_type x1, local copies, waits for them, and re-layouts, body(): products = jnp.einsum('bkri,blrj->bklij', left_panel, solved, preferred_e...  4.78 us
    dot_general x1, matrix products, body(): jnp.einsum('bkri,blrj->bklij', left_panel, solved, preferred_element_type...  3.94 us
    dot_general x1, matrix products, body(): jnp.einsum('pij,pjc->ic', lax.all_gather(rounded, 'pair', axis=0, tiled=T...  2.57 us
    gather x1, local copies, waits for them, and re-layouts, body(): products[(item_box * neighbours + item_first) * neighbours + item_second]  2.56 us
  transfers between devices with their start and end apart: 5, of which 5 were waited for; matrix products, arithmetic and copies ran while one was open for 1% of the time, Pallas kernels for 0%

commit v1 on v0

v1 whole, which is shorter than its diff:
```python
import jax
import jax.numpy as jnp
from jax import lax
from jax.experimental import pallas as pl
from jax.experimental.pallas import tpu as pltpu
from jax.sharding import PartitionSpec as P

REACH = 2
ROLES = 2 * REACH + 1
DIRECT, FAR, OWN, NEAR, COMB = range(ROLES)
LANES = 128


def dot_nt(a, b):
    return lax.dot_general(a, b, (((1,), (1,)), ((), ())), preferred_element_type=jnp.float32)


def terms_kernel(surf_count, pair_count, lt_ref, rt_ref, inv_ref, target_ref, direct_ref, far_ref, near_ref, comb_ref, own_ref, terms, acc):
    box_count, neighbours, skeleton, _ = lt_ref.shape
    slots = own_ref.shape[0]
    tail = skeleton - LANES
    me = lax.axis_index("surf")
    even = lax.rem(me, 2) == 0
    acc[...] = jnp.zeros_like(acc)
    cells = []
    for box in range(box_count):
        inverse = inv_ref[box]
        left = [lt_ref[box, k] for k in range(neighbours)]
        solved = [dot_nt(rt_ref[box, k], inverse).astype(jnp.bfloat16) for k in range(neighbours)]
        for second in range(neighbours):
            both = jnp.concatenate([solved[second], left[second]], axis=1)
            both = jnp.concatenate([both, both[LANES:]], axis=0)
            for first in range(second + 1):
                if first == second:
                    term = dot_nt(left[first], both[:, :LANES])
                else:
                    term = dot_nt(jnp.concatenate([left[first], solved[first]], axis=1), both)
                terms[len(cells)] = term
                block = target_ref[box, first, second]
                tile = block // (slots * pair_count)
                slot = lax.rem(block, slots)
                ahead = lax.rem(tile - me + surf_count, surf_count)
                ahead = jnp.where(ahead <= REACH, ahead, ahead - surf_count)
                role = jnp.where(even, ahead, -ahead) + REACH
                cells.append(role * slots + slot)
    for unit, cell in enumerate(cells):
        acc[cell] += terms[unit]
    lane = lax.broadcasted_iota(jnp.int32, (skeleton, LANES), 1)
    for role, ref in ((FAR, far_ref), (DIRECT, direct_ref), (NEAR, near_ref), (COMB, comb_ref)):
        for slot in range(slots):
            ref[slot] = acc[role * slots + slot, :, :LANES].astype(jnp.bfloat16)
        for pair in range(slots // 2):
            low = acc[role * slots + 2 * pair, :, LANES:]
            high = acc[role * slots + 2 * pair + 1, :, LANES:]
            ref[slots + pair] = jnp.where(lane < tail, low, high).astype(jnp.bfloat16)
    own_ref[...] = acc[OWN * slots : (OWN + 1) * slots, :, :skeleton]


def update_kernel(blocks_ref, own_ref, near_ref, direct_ref, comb_ref, *refs):
    slots, skeleton, _ = blocks_ref.shape
    shifts = (len(refs) - 1) // 2
    weights = refs[:shifts]
    updated_ref = refs[shifts]
    parts = refs[shifts + 1 :]
    tail = skeleton - LANES

    def received(row):
        return near_ref[row].astype(jnp.float32) + direct_ref[row].astype(jnp.float32) + comb_ref[row].astype(jnp.float32)

    total = [None] * shifts
    for pair in range(slots // 2):
        tails = received(slots + pair)
        for half in range(2):
            slot = 2 * pair + half
            gone = jnp.concatenate([received(slot), tails[:, half * tail : (half + 1) * tail]], axis=1)
            updated = blocks_ref[slot] - own_ref[slot] - gone
            updated_ref[slot] = updated
            rounded = updated.astype(jnp.bfloat16)
            for shift in range(shifts):
                part = jnp.dot(rounded, weights[shift][slot], preferred_element_type=jnp.float32)
                total[shift] = part if total[shift] is None else total[shift] + part
    for shift in range(shifts):
        parts[shift][...] = total[shift].astype(parts[shift].dtype)


def body(left_panel, right_panel, inverse, target, blocks, weights):
    box_count, neighbours, redundant, skeleton = left_panel.shape
    surf_count = lax.axis_size("surf")
    pair_count = lax.axis_size("pair")
    slots = blocks.shape[0]
    columns = weights.shape[2]
    packed = jax.ShapeDtypeStruct((slots + slots // 2, skeleton, LANES), jnp.bfloat16)
    units = box_count * neighbours * (neighbours + 1) // 2
    vmem = pl.BlockSpec(memory_space=pltpu.VMEM)
    smem = pl.BlockSpec(memory_space=pltpu.SMEM)

    def terms_call(*refs):
        terms_kernel(surf_count, pair_count, *refs)

    direct, far, near, comb, own = pl.pallas_call(
        terms_call,
        out_shape=[packed, packed, packed, packed, jax.ShapeDtypeStruct(blocks.shape, jnp.float32)],
        in_specs=[vmem, vmem, vmem, smem],
        out_specs=[vmem] * 5,
        scratch_shapes=[
            pltpu.VMEM((units, skeleton, 2 * LANES), jnp.float32),
            pltpu.VMEM((ROLES * slots, skeleton, 2 * LANES), jnp.float32),
        ],
        name="terms",
    )(jnp.swapaxes(left_panel, 2, 3), jnp.swapaxes(right_panel, 2, 3), inverse, target)

    def send(piece, even_by, odd_by):
        moves = [(i, (i + (odd_by if i % 2 else even_by)) % surf_count) for i in range(surf_count)]
        return lax.ppermute(piece, "surf", moves)

    me = lax.axis_index("pair")
    far = send(far, 1, -1)
    direct = send(direct, -2, 2)
    near = send(near, 1, -1)
    comb = (comb.astype(jnp.float32) + far.astype(jnp.float32)).astype(jnp.bfloat16)
    comb = send(comb, 2, -2)

    panels = []
    for shift in range(pair_count):
        dest = lax.rem(me + shift, pair_count)
        mine = lax.dynamic_slice_in_dim(weights, dest * slots, slots, axis=0)
        if shift:
            mine = lax.ppermute(mine, "pair", [(i, (i + shift) % pair_count) for i in range(pair_count)])
        panels.append(mine)

    part = jax.ShapeDtypeStruct((skeleton, columns), jnp.bfloat16)
    updated, kept, *parts = pl.pallas_call(
        update_kernel,
        out_shape=[jax.ShapeDtypeStruct(blocks.shape, jnp.float32), jax.ShapeDtypeStruct((skeleton, columns), jnp.float32)] + [part] * (pair_count - 1),
        in_specs=[vmem] * (5 + pair_count),
        out_specs=[vmem] * (1 + pair_count),
        name="update",
    )(blocks, own, near, direct, comb, *panels)
    for shift, piece in enumerate(parts, 1):
        back = lax.ppermute(piece, "pair", [(i, (i - shift) % pair_count) for i in range(pair_count)])
        kept = kept + back.astype(jnp.float32)
    return (updated, kept)


def solution(mesh):
    if mesh.shape["surf"] % 2 or mesh.shape["surf"] < 2 * REACH + 1:
        raise ValueError("surf size")
    in_specs = (
        P(("surf", "pair"), None, None, None),
        P(("surf", "pair"), None, None, None),
        P(("surf", "pair"), None, None),
        P(("surf", "pair"), None, None),
        P(("surf", "pair"), None, None),
        P("surf", None, "pair"),
    )
    out_specs = (P(("surf", "pair"), None, None), P("surf", "pair"))
    return jax.shard_map(body, mesh=mesh, in_specs=in_specs, out_specs=out_specs, check_vma=False)
```

time: 125 us -> 39.4 us (0.32)
  waiting for transfers between devices: 66.5 us -> 13.7 us
  local copies, waits for them, and re-layouts: 22.4 us -> 1.51 us
  between operations: 14.1 us -> 0.68 us
  matrix products: 10.8 us -> 0 us
  Pallas kernels: 0 us -> 7.08 us
  starting transfers between devices: 9.95 us -> 14 us
    ppermute x4 -> x10, waiting for transfers between devices: 46.7 us -> 13.7 us  [the longest x3 6.27 us: body(): lax.ppermute(mine, 'pair', [(i, (i + shift) % pair_count) for i in range(...]
    all_gather x1 -> x0, waiting for transfers between devices: 19.7 us -> none  [body(): lax.all_gather(rounded, 'pair', axis=0, tiled=True)]
    gather x5 -> x0, local copies, waits for them, and re-layouts: 12.1 us -> none  [the longest x2 8.7 us: body(): products[(item_box * neighbours + item_second) * neighbours + item_first]]
    dot_general x4 -> x0, matrix products: 10.8 us -> none  [the longest x1 3.94 us: body(): jnp.einsum('bkri,blrj->bklij', left_panel, solved, preferred_element_type...]
    pallas_call x0 -> x2, Pallas kernels: none -> 7.08 us  [the longest x1 3.92 us: body(): pl.pallas_call(terms_call, out_shape=[packed, packed, packed, packed, jax...]
    convert_element_type x2 -> x0, local copies, waits for them, and re-layouts: 5.56 us -> none  [the longest x1 4.78 us: body(): products = jnp.einsum('bkri,blrj->bklij', left_panel, solved, preferred_e...]
    ppermute x4 -> x10, starting transfers between devices: 9.91 us -> 14 us  [the longest x4 9.23 us: send(): return lax.ppermute(piece, 'surf', moves)]
    another operation x5 -> x0, local copies, waits for them, and re-layouts: 2.2 us -> none  [the longest x3 1.47 us: body(): item_first = jnp.tile(jnp.asarray(firsts), box_count)]
  transfers between devices with their start and end apart: 5 -> 10, of which waited for: 5 -> 6; matrix products, arithmetic and copies ran while one was open for 1% -> 2% of each run, Pallas kernels for 0% -> 0%
where the time goes in v1:
time: 39.4 us; the launch traced here: 38.6 us
  starting transfers between devices  14 us (36%)
  waiting for transfers between devices  13.7 us (35%)
  Pallas kernels  7.08 us (18%)
  other arithmetic  1.64 us (4%)
  local copies, waits for them, and re-layouts  1.51 us (4%)
  between operations  0.68 us (2%)
    ppermute x4, starting transfers between devices, send(): return lax.ppermute(piece, 'surf', moves)  9.23 us
    ppermute x3, waiting for transfers between devices, body(): lax.ppermute(mine, 'pair', [(i, (i + shift) % pair_count) for i in range(...  6.27 us
    ppermute x3, waiting for transfers between devices, body(): lax.ppermute(piece, 'pair', [(i, (i - shift) % pair_count) for i in range...  4.25 us
    pallas_call x1, Pallas kernels, body(): pl.pallas_call(terms_call, out_shape=[packed, packed, packed, packed, jax...  3.92 us
    ppermute x4, waiting for transfers between devices, send(): return lax.ppermute(piece, 'surf', moves)  3.16 us
    pallas_call x1, Pallas kernels, body(): pl.pallas_call(update_kernel, out_shape=[jax.ShapeDtypeStruct(blocks.shap...  3.15 us
    ppermute x3, starting transfers between devices, body(): lax.ppermute(piece, 'pair', [(i, (i - shift) % pair_count) for i in range...  2.6 us
    ppermute x3, starting transfers between devices, body(): lax.ppermute(mine, 'pair', [(i, (i + shift) % pair_count) for i in range(...  2.22 us
  transfers between devices with their start and end apart: 10, of which 6 were waited for; matrix products, arithmetic and copies ran while one was open for 2% of the time, Pallas kernels for 0%

profile of v1, /device:TPU:0, one launch (start us, length us, event | category | flops | bytes accessed | tf_op | source)
XLA Modules:
  0.0 38.6 jit_solution(9865342442181300797)
XLA Ops:
  0.6 0.0 copy-start
  0.6 3.9 %terms.1 = (bf16[6,192,128]{2,1,0:T(8,128)(2,1)}, bf16[6,192,128]{2,1,0:T(8,128)(2,1)}, bf16[6,192,128]{2,1,0:T(8,128)(2,1)}, bf16[6,192,128]{2,1,0:T(8,128)(2,1)}, f32[4,192,192]{2,1,0:T(8,128)}) custom-call(bf16[2,4,192,128]{3,2,1,0:T(8,128)(2,1)} %bitcast.2, bf16[2,4,192,128]{3,2,1,0:T(8,128)(2,1)} %bitcast.3, bf16[2,128,128]{2,1,0:T(8,128)(2,1)} %refs_2_.1, ...), custom_call_target="tpu_custom_call" | custom-call | tf_op jit(solution)/shard_map/terms/pallas_call | solution.py:100
  4.6 3.0 %collective-permute-start.2 = (bf16[6,192,128]{2,1,0:T(8,128)(2,1)}, bf16[6,192,128]{2,1,0:T(8,128)(2,1)S(1)}, u32[]{:S(2)}, u32[]{:S(2)}) collective-permute-start(bf16[6,192,128]{2,1,0:T(8,128)(2,1)} %get-tuple-element.16), channel_id=1, source_target_pairs={{0,4},{4,0},{8,12},{12,8},{16,20},{20,16},{24,28},{28,24},{1,5},{5... | collective-permute-start | bytes 884744 | tf_op jit(solution)/shard_map/ppermute | solution.py:114
  7.6 0.0 copy-done
  7.6 0.8 %constant_dynamic-slice_fusion = (bf16[4,192,128]{2,1,0:T(8,128)(2,1)S(1)}, bf16[4,192,128]{2,1,0:T(8,128)(2,1)S(1)}, bf16[4,192,128]{2,1,0:T(8,128)(2,1)}, bf16[4,192,128]{2,1,0:T(8,128)(2,1)S(1)}) fusion(bf16[16,192,128]{2,1,0:T(8,128)(2,1)S(1)} %copy-done, s32[]{:T(128)S(6)} %select_n.15, s32[]{:T(128)S(6)} %select_n.13, s32[]{:T(128)S(6)} %select_n.12, ...), kind=kLoop, calls=%fused_computation.2 | loop fusion | bytes 1572880 | tf_op jit(solution)/shard_map/dynamic_slice | solution.py:126
  8.3 0.7 %collective-permute-start.6 = (bf16[4,192,128]{2,1,0:T(8,128)(2,1)S(1)}, bf16[4,192,128]{2,1,0:T(8,128)(2,1)S(1)}, u32[]{:S(2)}, u32[]{:S(2)}) collective-permute-start(bf16[4,192,128]{2,1,0:T(8,128)(2,1)S(1)} %get-tuple-element.22), channel_id=1, source_target_pairs={{0,3},{1,0},{2,1},{3,2},{4,7},{5,4},{6,5},{7,6},{8,11},{9,8},{10,9... | collective-permute-start | bytes 589832 | tf_op jit(solution)/shard_map/ppermute | solution.py:128
  9.0 0.5 %collective-permute-start = (bf16[6,192,128]{2,1,0:T(8,128)(2,1)S(1)}, bf16[6,192,128]{2,1,0:T(8,128)(2,1)S(1)}, u32[]{:S(2)}, u32[]{:S(2)}) collective-permute-start(bf16[6,192,128]{2,1,0:T(8,128)(2,1)S(1)} %copy-done.9), channel_id=1, source_target_pairs={{0,4},{4,0},{8,12},{12,8},{16,20},{20,16},{24,28},{28,24},{1,5},{5... | collective-permute-start | bytes 884744 | tf_op jit(solution)/shard_map/ppermute | solution.py:114
  9.5 3.6 %collective-permute-start.1 = (bf16[6,192,128]{2,1,0:T(8,128)(2,1)S(1)}, bf16[6,192,128]{2,1,0:T(8,128)(2,1)S(1)}, u32[]{:S(2)}, u32[]{:S(2)}) collective-permute-start(bf16[6,192,128]{2,1,0:T(8,128)(2,1)S(1)} %copy-done.8), channel_id=1, source_target_pairs={{0,24},{4,12},{8,0},{12,20},{16,8},{20,28},{24,16},{28,4},{1,25},{... | collective-permute-start | bytes 884744 | tf_op jit(solution)/shard_map/ppermute | solution.py:114
  13.1 2.5 %collective-permute-done.2 = bf16[6,192,128]{2,1,0:T(8,128)(2,1)S(1)} collective-permute-done((bf16[6,192,128]{2,1,0:T(8,128)(2,1)}, bf16[6,192,128]{2,1,0:T(8,128)(2,1)S(1)}, u32[]{:S(2)}, u32[]{:S(2)}) %collective-permute-start.2) | collective-permute-done | bytes 294944 | tf_op jit(solution)/shard_map/ppermute | solution.py:114
  15.6 0.1 add_convert_fusion
  15.7 2.1 %collective-permute-start.3 = (bf16[6,192,128]{2,1,0:T(8,128)(2,1)S(1)}, bf16[6,192,128]{2,1,0:T(8,128)(2,1)S(1)}, u32[]{:S(2)}, u32[]{:S(2)}) collective-permute-start(bf16[6,192,128]{2,1,0:T(8,128)(2,1)S(1)} %add_convert_fusion), channel_id=1, source_target_pairs={{0,8},{4,28},{8,16},{12,4},{16,24},{20,12},{24,0},{28,20},{1,9},{5... | collective-permute-start | bytes 884744 | tf_op jit(solution)/shard_map/ppermute | solution.py:114
  17.8 0.0 collective-permute-start.4
  17.8 0.0 collective-permute-done.6.refs_3_
  17.9 1.6 %collective-permute-start.5 = (bf16[4,192,128]{2,1,0:T(8,128)(2,1)S(1)}, bf16[4,192,128]{2,1,0:T(8,128)(2,1)S(1)}, u32[]{:S(2)}, u32[]{:S(2)}) collective-permute-start(bf16[4,192,128]{2,1,0:T(8,128)(2,1)S(1)} %get-tuple-element.25), channel_id=1, source_target_pairs={{0,2},{1,3},{2,0},{3,1},{4,6},{5,7},{6,4},{7,5},{8,10},{9,11},{10,... | collective-permute-start | bytes 589832 | tf_op jit(solution)/shard_map/ppermute | solution.py:128
  19.4 5.0 %collective-permute-done.4.refs_1_ = bf16[4,192,128]{2,1,0:T(8,128)(2,1)S(1)} collective-permute-done((bf16[4,192,128]{2,1,0:T(8,128)(2,1)S(1)}, bf16[4,192,128]{2,1,0:T(8,128)(2,1)S(1)}, u32[]{:S(2)}, u32[]{:S(2)}) %collective-permute-start.4) | collective-permute-done | bytes 196640 | tf_op jit(solution)/shard_map/ppermute | solution.py:128
  24.4 1.3 %collective-permute-done.5.refs_2_ = bf16[4,192,128]{2,1,0:T(8,128)(2,1)S(1)} collective-permute-done((bf16[4,192,128]{2,1,0:T(8,128)(2,1)S(1)}, bf16[4,192,128]{2,1,0:T(8,128)(2,1)S(1)}, u32[]{:S(2)}, u32[]{:S(2)}) %collective-permute-start.5) | collective-permute-done | bytes 196640 | tf_op jit(solution)/shard_map/ppermute | solution.py:128
  25.7 0.0 collective-permute-done.near_ref
  25.7 0.0 collective-permute-done.1.direct_ref
  25.7 0.6 %collective-permute-done.3.comb_ref = bf16[6,192,128]{2,1,0:T(8,128)(2,1)S(1)} collective-permute-done((bf16[6,192,128]{2,1,0:T(8,128)(2,1)S(1)}, bf16[6,192,128]{2,1,0:T(8,128)(2,1)S(1)}, u32[]{:S(2)}, u32[]{:S(2)}) %collective-permute-start.3) | collective-permute-done | bytes 294944 | tf_op jit(solution)/shard_map/ppermute | solution.py:114
  26.3 0.0 copy-done.5
  26.3 0.0 copy-done.7
  26.4 0.1 copy-done.1
  26.5 0.1 copy-done.2
  26.6 0.4 %copy-done.3 = bf16[6,192,128]{2,1,0:T(8,128)(2,1)} copy-done((bf16[6,192,128]{2,1,0:T(8,128)(2,1)}, bf16[6,192,128]{2,1,0:T(8,128)(2,1)S(1)}, u32[]{:S(2)}) %copy-start.3) | copy-done | bytes 294936
  27.1 3.2 %update.1 = (f32[4,192,192]{2,1,0:T(8,128)}, f32[192,128]{1,0:T(8,128)}, bf16[192,128]{1,0:T(8,128)(2,1)}, bf16[192,128]{1,0:T(8,128)(2,1)}, bf16[192,128]{1,0:T(8,128)(2,1)}) custom-call(f32[4,192,192]{2,1,0:T(8,128)} %blocks_ref.1, f32[4,192,192]{2,1,0:T(8,128)} %get-tuple-element.12.own_ref, bf16[6,192,128]{2,1,0:T(8,128)(2,1)} %copy-done.1, ...), custom_call_target="tpu_custom_call" | custom-call | tf_op jit(solution)/shard_map/update/pallas_call | solution.py:132
  30.2 2.1 %collective-permute-start.7 = (bf16[192,128]{1,0:T(8,128)(2,1)}, bf16[192,128]{1,0:T(8,128)(2,1)S(1)}, u32[]{:S(2)}, u32[]{:S(2)}) collective-permute-start(bf16[192,128]{1,0:T(8,128)(2,1)} %get-tuple-element.19), channel_id=1, source_target_pairs={{0,3},{1,0},{2,1},{3,2},{4,7},{5,4},{6,5},{7,6},{8,11},{9,8},{10,9... | collective-permute-start | bytes 147464 | tf_op jit(solution)/shard_map/ppermute | solution.py:140
  32.3 0.5 %collective-permute-start.8 = (bf16[192,128]{1,0:T(8,128)(2,1)}, bf16[192,128]{1,0:T(8,128)(2,1)S(1)}, u32[]{:S(2)}, u32[]{:S(2)}) collective-permute-start(bf16[192,128]{1,0:T(8,128)(2,1)} %get-tuple-element.20), channel_id=1, source_target_pairs={{0,2},{1,3},{2,0},{3,1},{4,6},{5,7},{6,4},{7,5},{8,10},{9,11},{10,... | collective-permute-start | bytes 147464 | tf_op jit(solution)/shard_map/ppermute | solution.py:140
  32.8 0.0 collective-permute-start.9
  32.8 1.5 %collective-permute-done.7 = bf16[192,128]{1,0:T(8,128)(2,1)S(1)} collective-permute-done((bf16[192,128]{1,0:T(8,128)(2,1)}, bf16[192,128]{1,0:T(8,128)(2,1)S(1)}, u32[]{:S(2)}, u32[]{:S(2)}) %collective-permute-start.7) | collective-permute-done | bytes 49184 | tf_op jit(solution)/shard_map/ppermute | solution.py:140
  34.4 2.7 %collective-permute-done.8 = bf16[192,128]{1,0:T(8,128)(2,1)S(1)} collective-permute-done((bf16[192,128]{1,0:T(8,128)(2,1)}, bf16[192,128]{1,0:T(8,128)(2,1)S(1)}, u32[]{:S(2)}, u32[]{:S(2)}) %collective-permute-start.8) | collective-permute-done | bytes 49184 | tf_op jit(solution)/shard_map/ppermute | solution.py:140
  37.1 0.0 collective-permute-done.9
  37.1 1.6 %convert_add_fusion = f32[192,128]{1,0:T(8,128)} fusion(bf16[192,128]{1,0:T(8,128)(2,1)S(1)} %collective-permute-done.9, bf16[192,128]{1,0:T(8,128)(2,1)S(1)} %collective-permute-done.8, f32[192,128]{1,0:T(8,128)} %get-tuple-element.18, bf16[192,128]{1,0:T(8,128)(2,1)S(1)} %collective-permute-done.7), kind=kLoop, calls=%fused_computation.1 | loop fusion | flops 147456 | bytes 344064 | tf_op jit(solution)/shard_map/add | solution.py:141
  (13 shorter events, 0.0 us)
Async XLA Ops:
  0.6 6.9 %copy-start = (bf16[16,192,128]{2,1,0:T(8,128)(2,1)S(1)}, bf16[16,192,128]{2,1,0:T(8,128)(2,1)}, u32[]{:S(2)}) copy-start(bf16[16,192,128]{2,1,0:T(8,128)(2,1)} %param.11) | copy-start | bytes 2359300
  4.6 11.1 %collective-permute-start.2 = (bf16[6,192,128]{2,1,0:T(8,128)(2,1)}, bf16[6,192,128]{2,1,0:T(8,128)(2,1)S(1)}, u32[]{:S(2)}, u32[]{:S(2)}) collective-permute-start(bf16[6,192,128]{2,1,0:T(8,128)(2,1)} %get-tuple-element.16), channel_id=1, source_target_pairs={{0,4},{4,0},{8,12},{12,8},{16,20},{20,16},{24,28},{28,24},{1,5},{5... | collective-permute-start | bytes 884744 | tf_op jit(solution)/shard_map/ppermute | solution.py:114
  7.6 1.4 %copy-start.9 = (bf16[6,192,128]{2,1,0:T(8,128)(2,1)S(1)}, bf16[6,192,128]{2,1,0:T(8,128)(2,1)}, u32[]{:S(2)}) copy-start(bf16[6,192,128]{2,1,0:T(8,128)(2,1)} %get-tuple-element.13) | copy-start | bytes 884740
  7.6 1.9 %copy-start.8 = (bf16[6,192,128]{2,1,0:T(8,128)(2,1)S(1)}, bf16[6,192,128]{2,1,0:T(8,128)(2,1)}, u32[]{:S(2)}) copy-start(bf16[6,192,128]{2,1,0:T(8,128)(2,1)} %get-tuple-element.14) | copy-start | bytes 884740
  7.6 8.1 %copy-start.4 = (bf16[6,192,128]{2,1,0:T(8,128)(2,1)S(1)}, bf16[6,192,128]{2,1,0:T(8,128)(2,1)}, u32[]{:S(2)}) copy-start(bf16[6,192,128]{2,1,0:T(8,128)(2,1)} %get-tuple-element.15) | copy-start | bytes 884740
  8.3 9.5 %collective-permute-start.6 = (bf16[4,192,128]{2,1,0:T(8,128)(2,1)S(1)}, bf16[4,192,128]{2,1,0:T(8,128)(2,1)S(1)}, u32[]{:S(2)}, u32[]{:S(2)}) collective-permute-start(bf16[4,192,128]{2,1,0:T(8,128)(2,1)S(1)} %get-tuple-element.22), channel_id=1, source_target_pairs={{0,3},{1,0},{2,1},{3,2},{4,7},{5,4},{6,5},{7,6},{8,11},{9,8},{10,9... | collective-permute-start | bytes 589832 | tf_op jit(solution)/shard_map/ppermute | solution.py:128
  9.0 16.7 %collective-permute-start = (bf16[6,192,128]{2,1,0:T(8,128)(2,1)S(1)}, bf16[6,192,128]{2,1,0:T(8,128)(2,1)S(1)}, u32[]{:S(2)}, u32[]{:S(2)}) collective-permute-start(bf16[6,192,128]{2,1,0:T(8,128)(2,1)S(1)} %copy-done.9), channel_id=1, source_target_pairs={{0,4},{4,0},{8,12},{12,8},{16,20},{20,16},{24,28},{28,24},{1,5},{5... | collective-permute-start | bytes 884744 | tf_op jit(solution)/shard_map/ppermute | solution.py:114
  9.5 16.2 %collective-permute-start.1 = (bf16[6,192,128]{2,1,0:T(8,128)(2,1)S(1)}, bf16[6,192,128]{2,1,0:T(8,128)(2,1)S(1)}, u32[]{:S(2)}, u32[]{:S(2)}) collective-permute-start(bf16[6,192,128]{2,1,0:T(8,128)(2,1)S(1)} %copy-done.8), channel_id=1, source_target_pairs={{0,24},{4,12},{8,0},{12,20},{16,8},{20,28},{24,16},{28,4},{1,25},{... | collective-permute-start | bytes 884744 | tf_op jit(solution)/shard_map/ppermute | solution.py:114
  15.7 10.6 %collective-permute-start.3 = (bf16[6,192,128]{2,1,0:T(8,128)(2,1)S(1)}, bf16[6,192,128]{2,1,0:T(8,128)(2,1)S(1)}, u32[]{:S(2)}, u32[]{:S(2)}) collective-permute-start(bf16[6,192,128]{2,1,0:T(8,128)(2,1)S(1)} %add_convert_fusion), channel_id=1, source_target_pairs={{0,8},{4,28},{8,16},{12,4},{16,24},{20,12},{24,0},{28,20},{1,9},{5... | collective-permute-start | bytes 884744 | tf_op jit(solution)/shard_map/ppermute | solution.py:114
  17.8 6.5 %collective-permute-start.4 = (bf16[4,192,128]{2,1,0:T(8,128)(2,1)S(1)}, bf16[4,192,128]{2,1,0:T(8,128)(2,1)S(1)}, u32[]{:S(2)}, u32[]{:S(2)}) collective-permute-start(bf16[4,192,128]{2,1,0:T(8,128)(2,1)S(1)} %get-tuple-element.23), channel_id=1, source_target_pairs={{0,1},{1,2},{2,3},{3,0},{4,5},{5,6},{6,7},{7,4},{8,9},{9,10},{10,1... | collective-permute-start | bytes 589832 | tf_op jit(solution)/shard_map/ppermute | solution.py:128
  17.9 8.5 %copy-start.5 = (bf16[4,192,128]{2,1,0:T(8,128)(2,1)}, bf16[4,192,128]{2,1,0:T(8,128)(2,1)S(1)}, u32[]{:S(2)}) copy-start(bf16[4,192,128]{2,1,0:T(8,128)(2,1)S(1)} %collective-permute-done.6.refs_3_) | copy-start | bytes 589828
  17.9 7.8 %collective-permute-start.5 = (bf16[4,192,128]{2,1,0:T(8,128)(2,1)S(1)}, bf16[4,192,128]{2,1,0:T(8,128)(2,1)S(1)}, u32[]{:S(2)}, u32[]{:S(2)}) collective-permute-start(bf16[4,192,128]{2,1,0:T(8,128)(2,1)S(1)} %get-tuple-element.25), channel_id=1, source_target_pairs={{0,2},{1,3},{2,0},{3,1},{4,6},{5,7},{6,4},{7,5},{8,10},{9,11},{10,... | collective-permute-start | bytes 589832 | tf_op jit(solution)/shard_map/ppermute | solution.py:128
  24.4 1.9 %copy-start.6 = (bf16[4,192,128]{2,1,0:T(8,128)(2,1)}, bf16[4,192,128]{2,1,0:T(8,128)(2,1)S(1)}, u32[]{:S(2)}) copy-start(bf16[4,192,128]{2,1,0:T(8,128)(2,1)S(1)} %collective-permute-done.4.refs_1_) | copy-start | bytes 589828
  25.7 0.7 %copy-start.7 = (bf16[4,192,128]{2,1,0:T(8,128)(2,1)}, bf16[4,192,128]{2,1,0:T(8,128)(2,1)S(1)}, u32[]{:S(2)}) copy-start(bf16[4,192,128]{2,1,0:T(8,128)(2,1)S(1)} %collective-permute-done.5.refs_2_) | copy-start | bytes 589828
  25.7 0.8 %copy-start.1 = (bf16[6,192,128]{2,1,0:T(8,128)(2,1)}, bf16[6,192,128]{2,1,0:T(8,128)(2,1)S(1)}, u32[]{:S(2)}) copy-start(bf16[6,192,128]{2,1,0:T(8,128)(2,1)S(1)} %collective-permute-done.near_ref) | copy-start | bytes 884740
  25.7 0.9 %copy-start.2 = (bf16[6,192,128]{2,1,0:T(8,128)(2,1)}, bf16[6,192,128]{2,1,0:T(8,128)(2,1)S(1)}, u32[]{:S(2)}) copy-start(bf16[6,192,128]{2,1,0:T(8,128)(2,1)S(1)} %collective-permute-done.1.direct_ref) | copy-start | bytes 884740
  26.3 0.7 %copy-start.3 = (bf16[6,192,128]{2,1,0:T(8,128)(2,1)}, bf16[6,192,128]{2,1,0:T(8,128)(2,1)S(1)}, u32[]{:S(2)}) copy-start(bf16[6,192,128]{2,1,0:T(8,128)(2,1)S(1)} %collective-permute-done.3.comb_ref) | copy-start | bytes 884740
  30.2 4.1 %collective-permute-start.7 = (bf16[192,128]{1,0:T(8,128)(2,1)}, bf16[192,128]{1,0:T(8,128)(2,1)S(1)}, u32[]{:S(2)}, u32[]{:S(2)}) collective-permute-start(bf16[192,128]{1,0:T(8,128)(2,1)} %get-tuple-element.19), channel_id=1, source_target_pairs={{0,3},{1,0},{2,1},{3,2},{4,7},{5,4},{6,5},{7,6},{8,11},{9,8},{10,9... | collective-permute-start | bytes 147464 | tf_op jit(solution)/shard_map/ppermute | solution.py:140
  32.3 4.8 %collective-permute-start.8 = (bf16[192,128]{1,0:T(8,128)(2,1)}, bf16[192,128]{1,0:T(8,128)(2,1)S(1)}, u32[]{:S(2)}, u32[]{:S(2)}) collective-permute-start(bf16[192,128]{1,0:T(8,128)(2,1)} %get-tuple-element.20), channel_id=1, source_target_pairs={{0,2},{1,3},{2,0},{3,1},{4,6},{5,7},{6,4},{7,5},{8,10},{9,11},{10,... | collective-permute-start | bytes 147464 | tf_op jit(solution)/shard_map/ppermute | solution.py:140
  32.8 4.3 %collective-permute-start.9 = (bf16[192,128]{1,0:T(8,128)(2,1)}, bf16[192,128]{1,0:T(8,128)(2,1)S(1)}, u32[]{:S(2)}, u32[]{:S(2)}) collective-permute-start(bf16[192,128]{1,0:T(8,128)(2,1)} %get-tuple-element.21), channel_id=1, source_target_pairs={{0,1},{1,2},{2,3},{3,0},{4,5},{5,6},{6,7},{7,4},{8,9},{9,10},{10,1... | collective-permute-start | bytes 147464 | tf_op jit(solution)/shard_map/ppermute | solution.py:140

commit v2 on v1

v2 whole, which is shorter than its diff:
```python
import functools

import jax
import jax.numpy as jnp
from jax import lax
from jax.experimental import pallas as pl
from jax.experimental.pallas import tpu as pltpu
from jax.sharding import PartitionSpec as P

REACH = 2
ROLES = 2 * REACH + 1
DIRECT, FAR, OWN, NEAR, COMB = range(ROLES)
LANES = 128
CHUNKS = 2


def dot_nt(a, b):
    return lax.dot_general(a, b, (((1,), (1,)), ((), ())), preferred_element_type=jnp.float32)


def terms_kernel(chunk, surf_count, pair_count, lt_ref, target_ref, read_target, out_refs, terms, acc, ready):
    direct_ref, far_ref, near_ref, comb_ref, own_ref = out_refs
    box_count, neighbours, skeleton, _ = lt_ref.shape
    slots, rows, _ = own_ref.shape
    span = slice(chunk * rows, (chunk + 1) * rows)
    tail = skeleton - LANES
    me = lax.axis_index("surf")
    even = lax.rem(me, 2) == 0
    acc[...] = jnp.zeros_like(acc)
    units = []
    for box in range(box_count):
        left, solved = ready(box)
        for second in range(neighbours):
            both = jnp.concatenate([solved[second], left[second]], axis=1)
            both = jnp.concatenate([both, both[LANES:]], axis=0)
            for first in range(second + 1):
                if first == second:
                    term = dot_nt(left[first][span], both[:, :LANES])
                else:
                    term = dot_nt(jnp.concatenate([left[first][span], solved[first][span]], axis=1), both)
                terms[len(units)] = term
                units.append((box, first, second))
    read_target.wait()
    for unit, at in enumerate(units):
        block = target_ref[at]
        tile = block // (slots * pair_count)
        slot = lax.rem(block, slots)
        ahead = lax.rem(tile - me + surf_count, surf_count)
        ahead = jnp.where(ahead <= REACH, ahead, ahead - surf_count)
        role = jnp.where(even, ahead, -ahead) + REACH
        acc[role * slots + slot] += terms[unit]
    lane = lax.broadcasted_iota(jnp.int32, (rows, LANES), 1)
    for role, ref in ((DIRECT, direct_ref), (FAR, far_ref), (NEAR, near_ref), (COMB, comb_ref)):
        for slot in range(slots):
            ref[slot] = acc[role * slots + slot, :, :LANES].astype(jnp.bfloat16)
        for pair in range(slots // 2):
            low = acc[role * slots + 2 * pair, :, LANES:]
            high = acc[role * slots + 2 * pair + 1, :, LANES:]
            ref[slots + pair] = jnp.where(lane < tail, low, high).astype(jnp.bfloat16)
    own_ref[...] = acc[OWN * slots : (OWN + 1) * slots, :, :skeleton]


def first_terms(surf_count, pair_count, lt_hbm, rt_hbm, inv_hbm, weights_hbm, target_hbm, *refs):
    *refs, rt_ref, inv_ref, terms, acc, sem, weights_sem, target_ref, target_sem = refs
    out_refs, (lt_ref, solved_ref), weight_refs = refs[:ROLES], refs[ROLES : ROLES + 2], refs[ROLES + 2 :]
    box_count, neighbours = lt_ref.shape[:2]
    outer_count = pair_count // 2
    slots = weight_refs[0].shape[0]
    read_target = pltpu.make_async_copy(target_hbm, target_ref, target_sem)
    read_target.start()
    copies = []
    for box in range(box_count):
        group = []
        for hbm, ref in ((inv_hbm, inv_ref), (rt_hbm, rt_ref), (lt_hbm, lt_ref)):
            group.append(pltpu.make_async_copy(hbm.at[box], ref.at[box], sem.at[3 * box + len(group)]))
            group[-1].start()
        copies.append(group)
    me = lax.axis_index("pair")
    outer, inner = me // 2, lax.rem(me, 2)
    cuts = []
    for shift in range(outer_count):
        for half in range(2):
            dest = lax.rem(outer + shift, outer_count) * 2 + (inner if half == 0 else 1 - inner)
            if shift:
                cut = weight_refs[shift].at[pl.ds(half * slots, slots)]
            else:
                cut = weight_refs[-1 if half else 0]
            cuts.append(pltpu.make_async_copy(weights_hbm.at[pl.ds(dest * slots, slots)], cut, weights_sem.at[len(cuts)]))
            cuts[-1].start()

    def ready(box):
        for copy in copies[box]:
            copy.wait()
        inverse = inv_ref[box]
        solved = []
        for k in range(neighbours):
            solved.append(dot_nt(rt_ref[box, k], inverse).astype(jnp.bfloat16))
            solved_ref[box, k] = solved[k]
        return [lt_ref[box, k] for k in range(neighbours)], solved

    terms_kernel(0, surf_count, pair_count, lt_ref, target_ref, read_target, out_refs, terms, acc, ready)
    for copy in cuts:
        copy.wait()


def later_terms(chunk, surf_count, pair_count, lt_ref, solved_ref, target_hbm, *refs):
    *out_refs, terms, acc, target_ref, target_sem = refs
    read_target = pltpu.make_async_copy(target_hbm, target_ref, target_sem)
    read_target.start()
    neighbours = lt_ref.shape[1]

    def ready(box):
        return [lt_ref[box, k] for k in range(neighbours)], [solved_ref[box, k] for k in range(neighbours)]

    terms_kernel(chunk, surf_count, pair_count, lt_ref, target_ref, read_target, out_refs, terms, acc, ready)


def update_kernel(chunk, outer_count, *refs):
    blocks_ref, own_ref, direct_ref, near_ref, comb_ref, kept_w, peer_w = refs[:7]
    outer_w = refs[7 : 6 + outer_count]
    updated_ref, kept_ref, peer_ref, *outer_refs = refs[6 + outer_count :]
    slots, rows, skeleton = own_ref.shape
    span = slice(chunk * rows, (chunk + 1) * rows)
    tail = skeleton - LANES

    def received(row):
        return near_ref[row].astype(jnp.float32) + direct_ref[row].astype(jnp.float32) + comb_ref[row].astype(jnp.float32)

    panels = [(kept_w, 0), (peer_w, 0)]
    for shift in range(1, outer_count):
        panels += [(outer_w[shift - 1], 0), (peer_w, shift * slots)]
    total = [None] * len(panels)
    for pair in range(slots // 2):
        tails = received(slots + pair)
        for half in range(2):
            slot = 2 * pair + half
            gone = jnp.concatenate([received(slot), tails[:, half * tail : (half + 1) * tail]], axis=1)
            updated = blocks_ref[slot, span] - own_ref[slot] - gone
            updated_ref[slot] = updated
            rounded = updated.astype(jnp.bfloat16)
            for at, (panel, base) in enumerate(panels):
                part = jnp.dot(rounded, panel[base + slot], preferred_element_type=jnp.float32)
                total[at] = part if total[at] is None else total[at] + part
    kept_ref[...] = total[0]
    peer_ref[0] = total[1].astype(peer_ref.dtype)
    for shift in range(outer_count - 1):
        outer_refs[shift][...] = total[2 + 2 * shift]
        peer_ref[1 + shift] = total[3 + 2 * shift].astype(peer_ref.dtype)


def body(left_panel, right_panel, inverse, target, blocks, weights):
    box_count, neighbours, redundant, skeleton = left_panel.shape
    surf_count = lax.axis_size("surf")
    pair_count = lax.axis_size("pair")
    outer_count = pair_count // 2
    slots = blocks.shape[0]
    columns = weights.shape[2]
    rows = skeleton // CHUNKS
    units = box_count * neighbours * (neighbours + 1) // 2
    vmem = pl.BlockSpec(memory_space=pltpu.VMEM)
    hbm = pl.BlockSpec(memory_space=pltpu.HBM)

    def shape(*dims, dtype=jnp.bfloat16):
        return jax.ShapeDtypeStruct(dims, dtype)

    def to_tile(piece, even_by, odd_by):
        moves = [(i, (i + (odd_by if i % 2 else even_by)) % surf_count) for i in range(surf_count)]
        return lax.ppermute(piece, "surf", moves)

    def to_outer(piece, shift):
        moves = [(i, ((i // 2 + shift) % outer_count) * 2 + i % 2) for i in range(pair_count)]
        return lax.ppermute(piece, "pair", moves)

    def to_peer(piece):
        return lax.ppermute(piece, "pair", [(i, i ^ 1) for i in range(pair_count)])

    panels_shape = shape(box_count, neighbours, skeleton, redundant)
    packed = shape(slots + slots // 2, rows, LANES)
    pieces = [packed] * (ROLES - 1) + [shape(slots, rows, skeleton, dtype=jnp.float32)]
    cuts = [shape(slots, skeleton, columns)] + [shape(2 * slots, skeleton, columns)] * (outer_count - 1) + [shape(slots, skeleton, columns)]
    sums = [pltpu.VMEM((units, rows, 2 * LANES), jnp.float32), pltpu.VMEM((ROLES * slots, rows, 2 * LANES), jnp.float32)]
    read = [pltpu.SMEM(target.shape, target.dtype), pltpu.SemaphoreType.DMA]
    target = pltpu.with_memory_space_constraint(target, pltpu.HBM)
    direct, far, near, comb, own = ([] for _ in range(ROLES))
    lt, solved = None, None
    for chunk in range(CHUNKS):
        if chunk == 0:
            out = pl.pallas_call(
                functools.partial(first_terms, surf_count, pair_count),
                out_shape=pieces + [panels_shape, panels_shape] + cuts,
                in_specs=[hbm] * 5,
                out_specs=[vmem] * (ROLES + 2 + len(cuts)),
                scratch_shapes=[
                    pltpu.VMEM(panels_shape.shape, jnp.bfloat16),
                    pltpu.VMEM((box_count, redundant, redundant), jnp.bfloat16),
                    *sums,
                    pltpu.SemaphoreType.DMA((3 * box_count,)),
                    pltpu.SemaphoreType.DMA((pair_count,)),
                    *read,
                ],
                compiler_params=pltpu.CompilerParams(vmem_limit_bytes=16 << 20),
                name="first_terms",
            )(*(pltpu.with_memory_space_constraint(array, pltpu.HBM) for array in (jnp.swapaxes(left_panel, 2, 3), jnp.swapaxes(right_panel, 2, 3), inverse, weights)), target)
            lt, solved = out[ROLES : ROLES + 2]
            kept_w, *outer_w, peer_w = out[ROLES + 2 :]
        else:
            out = pl.pallas_call(
                functools.partial(later_terms, chunk, surf_count, pair_count),
                out_shape=pieces,
                in_specs=[vmem, vmem, hbm],
                out_specs=[vmem] * ROLES,
                scratch_shapes=sums + read,
                compiler_params=pltpu.CompilerParams(vmem_limit_bytes=16 << 20),
                name="later_terms",
            )(lt, solved, target)
        direct.append(to_tile(out[0], -2, 2))
        far.append(to_tile(out[1], 1, -1))
        near.append(to_tile(out[2], 1, -1))
        comb.append(out[3])
        own.append(out[4])

    outer_w = [to_outer(piece, shift) for shift, piece in enumerate(outer_w, 1)]
    peer_w = to_peer(jnp.concatenate([peer_w] + [piece[slots:] for piece in outer_w], axis=0))
    rest_w = [piece[:slots] for piece in outer_w]
    for chunk in range(CHUNKS):
        merged = (comb[chunk].astype(jnp.float32) + far[chunk].astype(jnp.float32)).astype(jnp.bfloat16)
        comb[chunk] = to_tile(merged, 2, -2)

    updated, panel = [], []
    for chunk in range(CHUNKS):
        fresh, kept, peer, *outer = pl.pallas_call(
            functools.partial(update_kernel, chunk, outer_count),
            out_shape=[shape(slots, rows, skeleton, dtype=jnp.float32), shape(rows, columns, dtype=jnp.float32), shape(outer_count, rows, columns)]
            + [shape(rows, columns, dtype=jnp.float32)] * (outer_count - 1),
            in_specs=[vmem] * (7 + len(rest_w)),
            out_specs=[vmem] * (2 + outer_count),
            compiler_params=pltpu.CompilerParams(vmem_limit_bytes=8 << 20),
            name="update",
        )(blocks, own[chunk], direct[chunk], near[chunk], comb[chunk], kept_w, peer_w, *rest_w)
        peer = to_peer(peer).astype(jnp.float32)
        kept = kept + peer[0]
        for shift in range(1, outer_count):
            piece = (outer[shift - 1] + peer[shift]).astype(jnp.bfloat16)
            kept = kept + to_outer(piece, -shift).astype(jnp.float32)
        updated.append(fresh)
        panel.append(kept)
    updated = jnp.concatenate(updated, axis=1)
    return (updated, jnp.concatenate(panel, axis=0))


def solution(mesh):
    if mesh.shape["surf"] % 2 or mesh.shape["surf"] < 2 * REACH + 1 or mesh.shape["pair"] % 2:
        raise ValueError("mesh sizes")
    in_specs = (
        P(("surf", "pair"), None, None, None),
        P(("surf", "pair"), None, None, None),
        P(("surf", "pair"), None, None),
        P(("surf", "pair"), None, None),
        P(("surf", "pair"), None, None),
        P("surf", None, "pair"),
    )
    out_specs = (P(("surf", "pair"), None, None), P("surf", "pair"))

    return jax.shard_map(body, mesh=mesh, in_specs=in_specs, out_specs=out_specs, check_vma=False)
```

time: 39.4 us -> 40.9 us (1.038); the launches traced: 38.6 us -> 40.7 us
  starting transfers between devices: 14 us -> 18 us
  Pallas kernels: 7.08 us -> 5.28 us
  local copies, waits for them, and re-layouts: 1.51 us -> 0.03 us
  waiting for transfers between devices: 13.7 us -> 14.9 us
    ppermute x10 -> x14, starting transfers between devices: 14 us -> 18 us  [the longest x8 12.7 us: to_tile(): return lax.ppermute(piece, 'surf', moves)]
    pallas_call x2 -> x4, Pallas kernels: 7.08 us -> 5.28 us  [the longest x1 2.76 us: body(): pl.pallas_call(functools.partial(first_terms, surf_count, pair_count), ou...]
    concatenate x0 -> x3, other arithmetic: none -> 1.62 us  [the longest x1 0.93 us: body(): updated = jnp.concatenate(updated, axis=1)]
    add x1 -> x2, other arithmetic: 1.56 us -> 0.02 us  [body(): kept = kept + to_outer(piece, -shift).astype(jnp.float32)]
    ppermute x10 -> x14, waiting for transfers between devices: 13.7 us -> 14.9 us  [the longest x8 10.3 us: to_tile(): return lax.ppermute(piece, 'surf', moves)]
    dynamic_slice x1 -> x0, local copies, waits for them, and re-layouts: 0.77 us -> none  [body(): mine = lax.dynamic_slice_in_dim(weights, dest * slots, slots, axis=0)]
    unnamed x20 -> x2, local copies, waits for them, and re-layouts: 0.74 us -> 0.01 us
  transfers between devices with their start and end apart: 10 -> 14, of which waited for: 6 -> 7; matrix products, arithmetic and copies ran while one was open for 2% -> 3% of each run, Pallas kernels for 0% -> 6%
where the time goes in v2:
time: 40.9 us; the launch traced here: 40.7 us
  starting transfers between devices  18 us (44%)
  waiting for transfers between devices  14.9 us (36%)
  Pallas kernels  5.28 us (13%)
  other arithmetic  1.75 us (4%)
  between operations  0.77 us (2%)
    ppermute x8, starting transfers between devices, to_tile(): return lax.ppermute(piece, 'surf', moves)  12.7 us
    ppermute x8, waiting for transfers between devices, to_tile(): return lax.ppermute(piece, 'surf', moves)  10.3 us
    ppermute x3, starting transfers between devices, to_outer(): return lax.ppermute(piece, 'pair', moves)  5.18 us
    ppermute x3, waiting for transfers between devices, to_outer(): return lax.ppermute(piece, 'pair', moves)  4.57 us
    pallas_call x1, Pallas kernels, body(): pl.pallas_call(functools.partial(first_terms, surf_count, pair_count), ou...  2.76 us
    pallas_call x1, Pallas kernels, body(): pl.pallas_call(functools.partial(later_terms, chunk, surf_count, pair_cou...  1.68 us
    concatenate x1, other arithmetic, body(): updated = jnp.concatenate(updated, axis=1)  0.93 us
    pallas_call x2, Pallas kernels, body(): pl.pallas_call(functools.partial(update_kernel, chunk, outer_count), out_...  0.84 us
  transfers between devices with their start and end apart: 14, of which 7 were waited for; matrix products, arithmetic and copies ran while one was open for 3% of the time, Pallas kernels for 6%

profile of v2, /device:TPU:0, one launch (start us, length us, event | category | flops | bytes accessed | tf_op | source)
XLA Modules:
  0.0 40.7 jit_solution(8173769077180206200)
XLA Ops:
  0.6 2.8 %first_terms.1 = (bf16[6,96,128]{2,1,0:T(8,128)(2,1)S(1)}, bf16[6,96,128]{2,1,0:T(8,128)(2,1)S(1)}, bf16[6,96,128]{2,1,0:T(8,128)(2,1)S(1)}, bf16[6,96,128]{2,1,...) custom-call(bf16[2,4,192,128]{3,2,1,0:T(8,128)(2,1)} %bitcast.26, ...), custom_call_target="tpu_custom_call" | custom-call | tf_op jit(solution)/shard_map/first_terms/pallas_call | solution.py:188
  3.4 3.0 %collective-permute-start.4 = (bf16[8,192,128]{2,1,0:T(8,128)(2,1)S(1)}, bf16[8,192,128]{2,1,0:T(8,128)(2,1)S(1)}, u32[]{:S(2)}, u32[]{:S(2)}) collective-permute-start(bf16[8,192,128]{2,1,0:T(8,128)(2,1)S(1)} %get-tuple-element.32), channel_id=1, source_target_pairs={{0,2},{1,3},{2,0},{3,1},{4,6},{5,7},{6,4},{7,5},{8,10},{9,11},{10,... | collective-permute-start | bytes 1179656 | tf_op jit(solution)/shard_map/ppermute | solution.py:172
  6.4 3.6 %collective-permute-start = (bf16[6,96,128]{2,1,0:T(8,128)(2,1)S(1)}, bf16[6,96,128]{2,1,0:T(8,128)(2,1)S(1)}, u32[]{:S(2)}, u32[]{:S(2)}) collective-permute-start(bf16[6,96,128]{2,1,0:T(8,128)(2,1)S(1)} %get-tuple-element.26), channel_id=1, source_target_pairs={{0,24},{4,12},{8,0},{12,20},{16,8},{20,28},{24,16},{28,4},{1,25},{... | collective-permute-start | bytes 442376 | tf_op jit(solution)/shard_map/ppermute | solution.py:168
  10.0 0.0 collective-permute-start.1
  10.0 2.0 %collective-permute-start.2 = (bf16[6,96,128]{2,1,0:T(8,128)(2,1)S(1)}, bf16[6,96,128]{2,1,0:T(8,128)(2,1)S(1)}, u32[]{:S(2)}, u32[]{:S(2)}) collective-permute-start(bf16[6,96,128]{2,1,0:T(8,128)(2,1)S(1)} %get-tuple-element.29), channel_id=1, source_target_pairs={{0,4},{4,0},{8,12},{12,8},{16,20},{20,16},{24,28},{28,24},{1,5},{5... | collective-permute-start | bytes 442376 | tf_op jit(solution)/shard_map/ppermute | solution.py:168
  12.1 1.7 %later_terms.1 = (bf16[6,96,128]{2,1,0:T(8,128)(2,1)S(1)}, bf16[6,96,128]{2,1,0:T(8,128)(2,1)S(1)}, bf16[6,96,128]{2,1,0:T(8,128)(2,1)S(1)}, bf16[6,96,128]{2,1,0:T(8,128)(2,1)S(1)}, f32[4,96,192]{2,1,0:T(8,128)S(1)}) custom-call(bf16[2,4,192,128]{3,2,1,0:T(8,128)(2,1)S(1)} %get-tuple-element.34.lt_ref, ...), custom_call_target="tpu_custom_call" | custom-call | tf_op jit(solution)/shard_map/later_terms/pallas_call | solution.py:207
  13.7 0.5 %collective-permute-start.6 = (bf16[6,96,128]{2,1,0:T(8,128)(2,1)S(1)}, bf16[6,96,128]{2,1,0:T(8,128)(2,1)S(1)}, u32[]{:S(2)}, u32[]{:S(2)}) collective-permute-start(bf16[6,96,128]{2,1,0:T(8,128)(2,1)S(1)} %get-tuple-element.37), channel_id=1, source_target_pairs={{0,24},{4,12},{8,0},{12,20},{16,8},{20,28},{24,16},{28,4},{1,25},{... | collective-permute-start | bytes 442376 | tf_op jit(solution)/shard_map/ppermute | solution.py:168
  14.3 1.3 %collective-permute-done.4 = bf16[8,192,128]{2,1,0:T(8,128)(2,1)S(1)} collective-permute-done((bf16[8,192,128]{2,1,0:T(8,128)(2,1)S(1)}, bf16[8,192,128]{2,1,0:T(8,128)(2,1)S(1)}, u32[]{:S(2)}, u32[]{:S(2)}) %collective-permute-start.4) | collective-permute-done | bytes 393248 | tf_op jit(solution)/shard_map/ppermute | solution.py:172
  15.5 1.8 %collective-permute-start.8 = (bf16[6,96,128]{2,1,0:T(8,128)(2,1)S(1)}, bf16[6,96,128]{2,1,0:T(8,128)(2,1)S(1)}, u32[]{:S(2)}, u32[]{:S(2)}) collective-permute-start(bf16[6,96,128]{2,1,0:T(8,128)(2,1)S(1)} %get-tuple-element.40), channel_id=1, source_target_pairs={{0,4},{4,0},{8,12},{12,8},{16,20},{20,16},{24,28},{28,24},{1,5},{5... | collective-permute-start | bytes 442376 | tf_op jit(solution)/shard_map/ppermute | solution.py:168
  17.3 0.0 copy-start
  17.4 1.6 %collective-permute-done.2 = bf16[6,96,128]{2,1,0:T(8,128)(2,1)S(1)} collective-permute-done((bf16[6,96,128]{2,1,0:T(8,128)(2,1)S(1)}, bf16[6,96,128]{2,1,0:T(8,128)(2,1)S(1)}, u32[]{:S(2)}, u32[]{:S(2)}) %collective-permute-start.2) | collective-permute-done | bytes 147488 | tf_op jit(solution)/shard_map/ppermute | solution.py:168
  19.0 0.0 collective-permute-start.5
  19.1 2.3 %collective-permute-done.8 = bf16[6,96,128]{2,1,0:T(8,128)(2,1)S(1)} collective-permute-done((bf16[6,96,128]{2,1,0:T(8,128)(2,1)S(1)}, bf16[6,96,128]{2,1,0:T(8,128)(2,1)S(1)}, u32[]{:S(2)}, u32[]{:S(2)}) %collective-permute-start.8) | collective-permute-done | bytes 147488 | tf_op jit(solution)/shard_map/ppermute | solution.py:168
  21.4 1.1 %collective-permute-start.3 = (bf16[6,96,128]{2,1,0:T(8,128)(2,1)S(1)}, bf16[6,96,128]{2,1,0:T(8,128)(2,1)S(1)}, u32[]{:S(2)}, u32[]{:S(2)}) collective-permute-start(bf16[6,96,128]{2,1,0:T(8,128)(2,1)S(1)} %add_convert_fusion.1), channel_id=1, source_target_pairs={{0,8},{4,28},{8,16},{12,4},{16,24},{20,12},{24,0},{28,20},{1,9},{5... | collective-permute-start | bytes 442376 | tf_op jit(solution)/shard_map/ppermute | solution.py:168
  22.5 0.0 collective-permute-done.refs_2_
  22.6 3.6 %collective-permute-start.7 = (bf16[6,96,128]{2,1,0:T(8,128)(2,1)S(1)}, bf16[6,96,128]{2,1,0:T(8,128)(2,1)S(1)}, u32[]{:S(2)}, u32[]{:S(2)}) collective-permute-start(bf16[6,96,128]{2,1,0:T(8,128)(2,1)S(1)} %get-tuple-element.38), channel_id=1, source_target_pairs={{0,4},{4,0},{8,12},{12,8},{16,20},{20,16},{24,28},{28,24},{1,5},{5... | collective-permute-start | bytes 442376 | tf_op jit(solution)/shard_map/ppermute | solution.py:168
  26.2 0.0 collective-permute-done.1.refs_3_
  26.2 0.0 collective-permute-start.9
  26.2 2.6 %collective-permute-done.3.refs_4_ = bf16[6,96,128]{2,1,0:T(8,128)(2,1)S(1)} collective-permute-done((bf16[6,96,128]{2,1,0:T(8,128)(2,1)S(1)}, bf16[6,96,128]{2,1,0:T(8,128)(2,1)S(1)}, u32[]{:S(2)}, u32[]{:S(2)}) %collective-permute-start.3) | collective-permute-done | bytes 147488 | tf_op jit(solution)/shard_map/ppermute | solution.py:168
  28.8 0.0 collective-permute-done.5.refs_6_
  28.8 0.4 %update.2 = (f32[4,96,192]{2,1,0:T(8,128)S(1)}, f32[96,128]{1,0:T(8,128)S(1)}, bf16[2,96,128]{2,1,0:T(8,128)(2,1)S(1)}, f32[96,128]{1,0:T(8,128)S(1)}) custom-call(f32[4,192,192]{2,1,0:T(8,128)S(1)} %copy-done, f32[4,96,192]{2,1,0:T(8,128)S(1)} %get-tuple-element.25.refs_1_, bf16[6,96,128]{2,1,0:T(8,128)(2,1)S(1)} %collective-permute-done.refs_2_, ...), custom_call_target="tpu_custom_call" | custom-call | tf_op jit(solution)/shard_map/update/pallas_call | solution.py:231
  29.2 0.1 collective-permute-start.10
  29.3 0.0 collective-permute-done.6.refs_2_
  29.3 3.8 %collective-permute-done.9.refs_4_ = bf16[6,96,128]{2,1,0:T(8,128)(2,1)S(1)} collective-permute-done((bf16[6,96,128]{2,1,0:T(8,128)(2,1)S(1)}, bf16[6,96,128]{2,1,0:T(8,128)(2,1)S(1)}, u32[]{:S(2)}, u32[]{:S(2)}) %collective-permute-start.9) | collective-permute-done | bytes 147488 | tf_op jit(solution)/shard_map/ppermute | solution.py:168
  33.1 0.4 %update.3 = (f32[4,96,192]{2,1,0:T(8,128)S(1)}, f32[96,128]{1,0:T(8,128)S(1)}, bf16[2,96,128]{2,1,0:T(8,128)(2,1)S(1)}, f32[96,128]{1,0:T(8,128)S(1)}) custom-call(f32[4,192,192]{2,1,0:T(8,128)S(1)} %copy-done, f32[4,96,192]{2,1,0:T(8,128)S(1)} %get-tuple-element.36.refs_1_, bf16[6,96,128]{2,1,0:T(8,128)(2,1)S(1)} %collective-permute-done.6.refs_2_, ...), custom_call_target="tpu_custom_call" | custom-call | tf_op jit(solution)/shard_map/update/pallas_call | solution.py:231
  33.5 0.1 collective-permute-start.12
  33.6 0.9 %pad_maximum_fusion = f32[4,192,192]{2,1,0:T(8,128)} fusion(f32[4,96,192]{2,1,0:T(8,128)S(1)} %get-tuple-element.41, f32[4,96,192]{2,1,0:T(8,128)S(1)} %get-tuple-element.33), kind=kLoop, calls=%fused_computation | loop fusion | flops 147456 | bytes 1179648 | tf_op jit(solution)/shard_map/concatenate | solution.py:247
  34.6 1.6 %collective-permute-start.11 = (bf16[96,128]{1,0:T(8,128)(2,1)S(1)}, bf16[96,128]{1,0:T(8,128)(2,1)S(1)}, u32[]{:S(2)}, u32[]{:S(2)}) collective-permute-start(bf16[96,128]{1,0:T(8,128)(2,1)S(1)} %fusion.5), channel_id=1, source_target_pairs={{0,2},{1,3},{2,0},{3,1},{4,6},{5,7},{6,4},{7,5},{8,10},{9,11},{10,... | collective-permute-start | bytes 73736 | tf_op jit(solution)/shard_map/ppermute | solution.py:172
  36.2 0.6 %collective-permute-start.13 = (bf16[96,128]{1,0:T(8,128)(2,1)S(1)}, bf16[96,128]{1,0:T(8,128)(2,1)S(1)}, u32[]{:S(2)}, u32[]{:S(2)}) collective-permute-start(bf16[96,128]{1,0:T(8,128)(2,1)S(1)} %fusion.1), channel_id=1, source_target_pairs={{0,2},{1,3},{2,0},{3,1},{4,6},{5,7},{6,4},{7,5},{8,10},{9,11},{10,... | collective-permute-start | bytes 73736 | tf_op jit(solution)/shard_map/ppermute | solution.py:172
  36.8 1.7 %collective-permute-done.11 = bf16[96,128]{1,0:T(8,128)(2,1)S(1)} collective-permute-done((bf16[96,128]{1,0:T(8,128)(2,1)S(1)}, bf16[96,128]{1,0:T(8,128)(2,1)S(1)}, u32[]{:S(2)}, u32[]{:S(2)}) %collective-permute-start.11) | collective-permute-done | bytes 24608 | tf_op jit(solution)/shard_map/ppermute | solution.py:172
  38.5 1.6 %collective-permute-done.13 = bf16[96,128]{1,0:T(8,128)(2,1)S(1)} collective-permute-done((bf16[96,128]{1,0:T(8,128)(2,1)S(1)}, bf16[96,128]{1,0:T(8,128)(2,1)S(1)}, u32[]{:S(2)}, u32[]{:S(2)}) %collective-permute-start.13) | collective-permute-done | bytes 24608 | tf_op jit(solution)/shard_map/ppermute | solution.py:172
  40.1 0.6 %pad_maximum_fusion.2 = f32[192,128]{1,0:T(8,128)} fusion(f32[96,128]{1,0:T(8,128)S(1)} %fusion.3, f32[96,128]{1,0:T(8,128)S(1)} %fusion.7), kind=kLoop, calls=%fused_computation.4 | loop fusion | flops 24576 | bytes 196608 | tf_op jit(solution)/shard_map/concatenate | solution.py:248
  (14 shorter events, 0.2 us)
Async XLA Ops:
  3.4 12.1 %collective-permute-start.4 = (bf16[8,192,128]{2,1,0:T(8,128)(2,1)S(1)}, bf16[8,192,128]{2,1,0:T(8,128)(2,1)S(1)}, u32[]{:S(2)}, u32[]{:S(2)}) collective-permute-start(bf16[8,192,128]{2,1,0:T(8,128)(2,1)S(1)} %get-tuple-element.32), channel_id=1, source_target_pairs={{0,2},{1,3},{2,0},{3,1},{4,6},{5,7},{6,4},{7,5},{8,10},{9,11},{10,... | collective-permute-start | bytes 1179656 | tf_op jit(solution)/shard_map/ppermute | solution.py:172
  6.4 16.1 %collective-permute-start = (bf16[6,96,128]{2,1,0:T(8,128)(2,1)S(1)}, bf16[6,96,128]{2,1,0:T(8,128)(2,1)S(1)}, u32[]{:S(2)}, u32[]{:S(2)}) collective-permute-start(bf16[6,96,128]{2,1,0:T(8,128)(2,1)S(1)} %get-tuple-element.26), channel_id=1, source_target_pairs={{0,24},{4,12},{8,0},{12,20},{16,8},{20,28},{24,16},{28,4},{1,25},{... | collective-permute-start | bytes 442376 | tf_op jit(solution)/shard_map/ppermute | solution.py:168
  10.0 16.1 %collective-permute-start.1 = (bf16[6,96,128]{2,1,0:T(8,128)(2,1)S(1)}, bf16[6,96,128]{2,1,0:T(8,128)(2,1)S(1)}, u32[]{:S(2)}, u32[]{:S(2)}) collective-permute-start(bf16[6,96,128]{2,1,0:T(8,128)(2,1)S(1)} %get-tuple-element.27), channel_id=1, source_target_pairs={{0,4},{4,0},{8,12},{12,8},{16,20},{20,16},{24,28},{28,24},{1,5},{5... | collective-permute-start | bytes 442376 | tf_op jit(solution)/shard_map/ppermute | solution.py:168
  10.0 9.0 %collective-permute-start.2 = (bf16[6,96,128]{2,1,0:T(8,128)(2,1)S(1)}, bf16[6,96,128]{2,1,0:T(8,128)(2,1)S(1)}, u32[]{:S(2)}, u32[]{:S(2)}) collective-permute-start(bf16[6,96,128]{2,1,0:T(8,128)(2,1)S(1)} %get-tuple-element.29), channel_id=1, source_target_pairs={{0,4},{4,0},{8,12},{12,8},{16,20},{20,16},{24,28},{28,24},{1,5},{5... | collective-permute-start | bytes 442376 | tf_op jit(solution)/shard_map/ppermute | solution.py:168
  13.7 15.6 %collective-permute-start.6 = (bf16[6,96,128]{2,1,0:T(8,128)(2,1)S(1)}, bf16[6,96,128]{2,1,0:T(8,128)(2,1)S(1)}, u32[]{:S(2)}, u32[]{:S(2)}) collective-permute-start(bf16[6,96,128]{2,1,0:T(8,128)(2,1)S(1)} %get-tuple-element.37), channel_id=1, source_target_pairs={{0,24},{4,12},{8,0},{12,20},{16,8},{20,28},{24,16},{28,4},{1,25},{... | collective-permute-start | bytes 442376 | tf_op jit(solution)/shard_map/ppermute | solution.py:168
  15.5 5.8 %collective-permute-start.8 = (bf16[6,96,128]{2,1,0:T(8,128)(2,1)S(1)}, bf16[6,96,128]{2,1,0:T(8,128)(2,1)S(1)}, u32[]{:S(2)}, u32[]{:S(2)}) collective-permute-start(bf16[6,96,128]{2,1,0:T(8,128)(2,1)S(1)} %get-tuple-element.40), channel_id=1, source_target_pairs={{0,4},{4,0},{8,12},{12,8},{16,20},{20,16},{24,28},{28,24},{1,5},{5... | collective-permute-start | bytes 442376 | tf_op jit(solution)/shard_map/ppermute | solution.py:168
  17.3 11.5 %copy-start = (f32[4,192,192]{2,1,0:T(8,128)S(1)}, f32[4,192,192]{2,1,0:T(8,128)}, u32[]{:S(2)}) copy-start(f32[4,192,192]{2,1,0:T(8,128)} %refs_0_.3) | copy-start | bytes 1769476
  19.0 9.8 %collective-permute-start.5 = (bf16[8,192,128]{2,1,0:T(8,128)(2,1)S(1)}, bf16[8,192,128]{2,1,0:T(8,128)(2,1)S(1)}, u32[]{:S(2)}, u32[]{:S(2)}) collective-permute-start(bf16[8,192,128]{2,1,0:T(8,128)(2,1)S(1)} %pad_maximum_fusion.1), channel_id=1, source_target_pairs={{0,1},{1,0},{2,3},{3,2},{4,5},{5,4},{6,7},{7,6},{8,9},{9,8},{10,11... | collective-permute-start | bytes 1179656 | tf_op jit(solution)/shard_map/ppermute | solution.py:175
  21.4 7.4 %collective-permute-start.3 = (bf16[6,96,128]{2,1,0:T(8,128)(2,1)S(1)}, bf16[6,96,128]{2,1,0:T(8,128)(2,1)S(1)}, u32[]{:S(2)}, u32[]{:S(2)}) collective-permute-start(bf16[6,96,128]{2,1,0:T(8,128)(2,1)S(1)} %add_convert_fusion.1), channel_id=1, source_target_pairs={{0,8},{4,28},{8,16},{12,4},{16,24},{20,12},{24,0},{28,20},{1,9},{5... | collective-permute-start | bytes 442376 | tf_op jit(solution)/shard_map/ppermute | solution.py:168
  22.6 6.8 %collective-permute-start.7 = (bf16[6,96,128]{2,1,0:T(8,128)(2,1)S(1)}, bf16[6,96,128]{2,1,0:T(8,128)(2,1)S(1)}, u32[]{:S(2)}, u32[]{:S(2)}) collective-permute-start(bf16[6,96,128]{2,1,0:T(8,128)(2,1)S(1)} %get-tuple-element.38), channel_id=1, source_target_pairs={{0,4},{4,0},{8,12},{12,8},{16,20},{20,16},{24,28},{28,24},{1,5},{5... | collective-permute-start | bytes 442376 | tf_op jit(solution)/shard_map/ppermute | solution.py:168
  26.2 6.9 %collective-permute-start.9 = (bf16[6,96,128]{2,1,0:T(8,128)(2,1)S(1)}, bf16[6,96,128]{2,1,0:T(8,128)(2,1)S(1)}, u32[]{:S(2)}, u32[]{:S(2)}) collective-permute-start(bf16[6,96,128]{2,1,0:T(8,128)(2,1)S(1)} %add_convert_fusion), channel_id=1, source_target_pairs={{0,8},{4,28},{8,16},{12,4},{16,24},{20,12},{24,0},{28,20},{1,9},{5... | collective-permute-start | bytes 442376 | tf_op jit(solution)/shard_map/ppermute | solution.py:168
  29.2 5.3 %collective-permute-start.10 = (bf16[2,96,128]{2,1,0:T(8,128)(2,1)S(1)}, bf16[2,96,128]{2,1,0:T(8,128)(2,1)S(1)}, u32[]{:S(2)}, u32[]{:S(2)}) collective-permute-start(bf16[2,96,128]{2,1,0:T(8,128)(2,1)S(1)} %get-tuple-element.43), channel_id=1, source_target_pairs={{0,1},{1,0},{2,3},{3,2},{4,5},{5,4},{6,7},{7,6},{8,9},{9,8},{10,11... | collective-permute-start | bytes 147464 | tf_op jit(solution)/shard_map/ppermute | solution.py:175
  33.5 2.6 %collective-permute-start.12 = (bf16[2,96,128]{2,1,0:T(8,128)(2,1)S(1)}, bf16[2,96,128]{2,1,0:T(8,128)(2,1)S(1)}, u32[]{:S(2)}, u32[]{:S(2)}) collective-permute-start(bf16[2,96,128]{2,1,0:T(8,128)(2,1)S(1)} %get-tuple-element.46), channel_id=1, source_target_pairs={{0,1},{1,0},{2,3},{3,2},{4,5},{5,4},{6,7},{7,6},{8,9},{9,8},{10,11... | collective-permute-start | bytes 147464 | tf_op jit(solution)/shard_map/ppermute | solution.py:175
  34.6 3.9 %collective-permute-start.11 = (bf16[96,128]{1,0:T(8,128)(2,1)S(1)}, bf16[96,128]{1,0:T(8,128)(2,1)S(1)}, u32[]{:S(2)}, u32[]{:S(2)}) collective-permute-start(bf16[96,128]{1,0:T(8,128)(2,1)S(1)} %fusion.5), channel_id=1, source_target_pairs={{0,2},{1,3},{2,0},{3,1},{4,6},{5,7},{6,4},{7,5},{8,10},{9,11},{10,... | collective-permute-start | bytes 73736 | tf_op jit(solution)/shard_map/ppermute | solution.py:172
  36.2 3.9 %collective-permute-start.13 = (bf16[96,128]{1,0:T(8,128)(2,1)S(1)}, bf16[96,128]{1,0:T(8,128)(2,1)S(1)}, u32[]{:S(2)}, u32[]{:S(2)}) collective-permute-start(bf16[96,128]{1,0:T(8,128)(2,1)S(1)} %fusion.1), channel_id=1, source_target_pairs={{0,2},{1,3},{2,0},{3,1},{4,6},{5,7},{6,4},{7,5},{8,10},{9,11},{10,... | collective-permute-start | bytes 73736 | tf_op jit(solution)/shard_map/ppermute | solution.py:172

commit v3 on v1

v3 whole, which is shorter than its diff:
```python
import functools

import jax
import jax.numpy as jnp
from jax import lax
from jax.experimental import pallas as pl
from jax.experimental.pallas import tpu as pltpu
from jax.sharding import PartitionSpec as P

REACH = 2
ROLES = 2 * REACH + 1
DIRECT, FAR, OWN, NEAR, COMB = range(ROLES)
LANES = 128
CHUNKS = 2


def dot_nt(a, b):
    return lax.dot_general(a, b, (((1,), (1,)), ((), ())), preferred_element_type=jnp.float32)


def terms_kernel(surf_count, pair_count, lt_hbm, rt_hbm, inv_hbm, weights_hbm, target_hbm, *refs):
    out_refs, weight_refs, refs = refs[: ROLES + 2 * (CHUNKS - 1)], refs[ROLES + 2 * (CHUNKS - 1) : -8], refs[-8:]
    lt_ref, rt_ref, inv_ref, target_ref, acc, sem, weights_sem, target_sem = refs
    direct_ref, near_ref, own_ref = out_refs[:3]
    far_refs, comb_refs = out_refs[3 : 3 + CHUNKS], out_refs[3 + CHUNKS :]
    box_count, neighbours, skeleton, _ = lt_ref.shape
    slots = own_ref.shape[0]
    outer_count = pair_count // 2
    tail = skeleton - LANES
    read_target = pltpu.make_async_copy(target_hbm, target_ref, target_sem)
    read_target.start()
    copies = []
    for box in range(box_count):
        group = []
        for hbm, ref in ((inv_hbm, inv_ref), (rt_hbm, rt_ref), (lt_hbm, lt_ref)):
            group.append(pltpu.make_async_copy(hbm.at[box], ref.at[box], sem.at[3 * box + len(group)]))
            group[-1].start()
        copies.append(group)
    pair = lax.axis_index("pair")
    outer, inner = pair // 2, lax.rem(pair, 2)
    cuts = []
    for shift in range(outer_count):
        for half in range(2):
            dest = lax.rem(outer + shift, outer_count) * 2 + (inner if half == 0 else 1 - inner)
            if shift:
                cut = weight_refs[shift].at[pl.ds(half * slots, slots)]
            else:
                cut = weight_refs[-1 if half else 0]
            cuts.append(pltpu.make_async_copy(weights_hbm.at[pl.ds(dest * slots, slots)], cut, weights_sem.at[len(cuts)]))
            cuts[-1].start()
    acc[...] = jnp.zeros_like(acc)
    me = lax.axis_index("surf")
    even = lax.rem(me, 2) == 0

    def cell(*at):
        block = target_ref[at]
        tile = block // (slots * pair_count)
        ahead = lax.rem(tile - me + surf_count, surf_count)
        ahead = jnp.where(ahead <= REACH, ahead, ahead - surf_count)
        return (jnp.where(even, ahead, -ahead) + REACH) * slots + lax.rem(block, slots)

    read_target.wait()
    for box in range(box_count):
        for copy in copies[box]:
            copy.wait()
        inverse = inv_ref[box]
        left = [lt_ref[box, k] for k in range(neighbours)]
        solved = [dot_nt(rt_ref[box, k], inverse).astype(jnp.bfloat16) for k in range(neighbours)]
        for second in range(neighbours):
            both = jnp.concatenate([solved[second], left[second]], axis=1)
            both = jnp.concatenate([both, both[LANES:]], axis=0)
            for first in range(second + 1):
                if first == second:
                    term = dot_nt(left[first], both[:, :LANES])
                else:
                    term = dot_nt(jnp.concatenate([left[first], solved[first]], axis=1), both)
                acc[cell(box, first, second)] += term
    lane = lax.broadcasted_iota(jnp.int32, (skeleton, LANES), 1)
    for role, refs in ((FAR, far_refs), (DIRECT, [direct_ref]), (COMB, comb_refs), (NEAR, [near_ref])):
        rows = skeleton // len(refs)
        for chunk, ref in enumerate(refs):
            span = slice(chunk * rows, (chunk + 1) * rows)
            for slot in range(slots):
                ref[slot] = acc[role * slots + slot, span, :LANES].astype(jnp.bfloat16)
            for two in range(slots // 2):
                low = acc[role * slots + 2 * two, span, LANES:]
                high = acc[role * slots + 2 * two + 1, span, LANES:]
                ref[slots + two] = jnp.where(lane[:rows] < tail, low, high).astype(jnp.bfloat16)
    own_ref[...] = acc[OWN * slots : (OWN + 1) * slots, :, :skeleton]
    for copy in cuts:
        copy.wait()


def update_kernel(chunk, outer_count, *refs):
    blocks_ref, own_ref, direct_ref, near_ref, comb_ref, kept_w, peer_w = refs[:7]
    outer_w = refs[7 : 6 + outer_count]
    updated_ref, kept_ref, peer_ref, *outer_refs = refs[-2 - outer_count :]
    slots, skeleton, _ = own_ref.shape
    rows = comb_ref.shape[1]
    span = slice(chunk * rows, (chunk + 1) * rows)
    tail = skeleton - LANES

    def received(row):
        return near_ref[row, span].astype(jnp.float32) + direct_ref[row, span].astype(jnp.float32) + comb_ref[row].astype(jnp.float32)

    panels = [(kept_w, 0), (peer_w, 0)]
    for shift in range(1, outer_count):
        panels += [(outer_w[shift - 1], 0), (peer_w, shift * slots)]
    total = [None] * len(panels)
    for two in range(slots // 2):
        tails = received(slots + two)
        for half in range(2):
            slot = 2 * two + half
            gone = jnp.concatenate([received(slot), tails[:, half * tail : (half + 1) * tail]], axis=1)
            updated = blocks_ref[slot, span] - own_ref[slot, span] - gone
            updated_ref[slot] = updated
            rounded = updated.astype(jnp.bfloat16)
            for at, (panel, base) in enumerate(panels):
                part = jnp.dot(rounded, panel[base + slot], preferred_element_type=jnp.float32)
                total[at] = part if total[at] is None else total[at] + part
    kept_ref[span] = total[0]
    peer_ref[0, span] = total[1].astype(peer_ref.dtype)
    for shift in range(outer_count - 1):
        outer_refs[shift][span] = total[2 + 2 * shift]
        peer_ref[1 + shift, span] = total[3 + 2 * shift].astype(peer_ref.dtype)


def body(left_panel, right_panel, inverse, target, blocks, weights):
    box_count, neighbours, redundant, skeleton = left_panel.shape
    surf_count = lax.axis_size("surf")
    pair_count = lax.axis_size("pair")
    outer_count = pair_count // 2
    slots = blocks.shape[0]
    columns = weights.shape[2]
    rows = skeleton // CHUNKS
    vmem = pl.BlockSpec(memory_space=pltpu.VMEM)
    hbm = pl.BlockSpec(memory_space=pltpu.HBM)

    def shape(*dims, dtype=jnp.bfloat16):
        return jax.ShapeDtypeStruct(dims, dtype)

    def to_tile(piece, even_by, odd_by):
        moves = [(i, (i + (odd_by if i % 2 else even_by)) % surf_count) for i in range(surf_count)]
        return lax.ppermute(piece, "surf", moves)

    def to_outer(piece, shift):
        moves = [(i, ((i // 2 + shift) % outer_count) * 2 + i % 2) for i in range(pair_count)]
        return lax.ppermute(piece, "pair", moves)

    def to_peer(piece):
        return lax.ppermute(piece, "pair", [(i, i ^ 1) for i in range(pair_count)])

    panels_shape = (box_count, neighbours, skeleton, redundant)
    full = shape(slots + slots // 2, skeleton, LANES)
    part = shape(slots + slots // 2, rows, LANES)
    cuts = [shape(slots, skeleton, columns)] + [shape(2 * slots, skeleton, columns)] * (outer_count - 1) + [shape(slots, skeleton, columns)]
    out_shape = [full, full, shape(*blocks.shape, dtype=jnp.float32)] + [part] * (2 * CHUNKS) + cuts
    args = (jnp.swapaxes(left_panel, 2, 3), jnp.swapaxes(right_panel, 2, 3), inverse, weights, target)
    direct, near, own, *out = pl.pallas_call(
        functools.partial(terms_kernel, surf_count, pair_count),
        out_shape=out_shape,
        in_specs=[hbm] * len(args),
        out_specs=[vmem] * len(out_shape),
        scratch_shapes=[
            pltpu.VMEM(panels_shape, jnp.bfloat16),
            pltpu.VMEM(panels_shape, jnp.bfloat16),
            pltpu.VMEM((box_count, redundant, redundant), jnp.bfloat16),
            pltpu.SMEM(target.shape, target.dtype),
            pltpu.VMEM((ROLES * slots, skeleton, 2 * LANES), jnp.float32),
            pltpu.SemaphoreType.DMA((3 * box_count,)),
            pltpu.SemaphoreType.DMA((pair_count,)),
            pltpu.SemaphoreType.DMA,
        ],
        compiler_params=pltpu.CompilerParams(vmem_limit_bytes=20 << 20),
        name="terms",
    )(*(pltpu.with_memory_space_constraint(array, pltpu.HBM) for array in args))
    far, comb, (kept_w, *outer_w, peer_w) = out[:CHUNKS], out[CHUNKS : 2 * CHUNKS], out[2 * CHUNKS :]

    far = [to_tile(piece, 1, -1) for piece in far]
    direct = to_tile(direct, -2, 2)
    near = to_tile(near, 1, -1)
    outer_w = [to_outer(piece, shift) for shift, piece in enumerate(outer_w, 1)]
    peer_w = to_peer(jnp.concatenate([peer_w] + [piece[slots:] for piece in outer_w], axis=0))
    outer_w = [piece[:slots] for piece in outer_w]
    for chunk in range(CHUNKS):
        merged = (comb[chunk].astype(jnp.float32) + far[chunk].astype(jnp.float32)).astype(jnp.bfloat16)
        comb[chunk] = to_tile(merged, 2, -2)

    updated, sums = [], []
    for chunk in range(CHUNKS):
        inputs = [blocks, own, direct, near, comb[chunk], kept_w, peer_w, *outer_w]
        fresh, *sums = pl.pallas_call(
            functools.partial(update_kernel, chunk, outer_count),
            out_shape=[shape(slots, rows, skeleton, dtype=jnp.float32), shape(skeleton, columns, dtype=jnp.float32), shape(outer_count, skeleton, columns)]
            + [shape(skeleton, columns, dtype=jnp.float32)] * (outer_count - 1),
            in_specs=[vmem] * (len(inputs) + len(sums)),
            out_specs=[vmem] * (2 + outer_count),
            input_output_aliases={len(inputs) + at: 1 + at for at in range(len(sums))},
            compiler_params=pltpu.CompilerParams(vmem_limit_bytes=8 << 20),
            name="update",
        )(*inputs, *sums)
        updated.append(fresh)
    kept, peer, *outer = sums
    peer = to_peer(peer).astype(jnp.float32)
    kept = kept + peer[0]
    for shift in range(1, outer_count):
        piece = (outer[shift - 1] + peer[shift]).astype(jnp.bfloat16)
        kept = kept + to_outer(piece, -shift).astype(jnp.float32)
    return (jnp.concatenate(updated, axis=1), kept)


def solution(mesh):
    if mesh.shape["surf"] % 2 or mesh.shape["surf"] < 2 * REACH + 1 or mesh.shape["pair"] % 2:
        raise ValueError("mesh sizes")
    in_specs = (
        P(("surf", "pair"), None, None, None),
        P(("surf", "pair"), None, None, None),
        P(("surf", "pair"), None, None),
        P(("surf", "pair"), None, None),
        P(("surf", "pair"), None, None),
        P("surf", None, "pair"),
    )
    out_specs = (P(("surf", "pair"), None, None), P("surf", "pair"))

    return jax.shard_map(body, mesh=mesh, in_specs=in_specs, out_specs=out_specs, check_vma=False)
```

time: 39.4 us -> 34.1 us (0.87); the launches traced: 38.6 us -> 34 us
  Pallas kernels: 7.08 us -> 3.57 us
  local copies, waits for them, and re-layouts: 1.51 us -> 0.03 us
    pallas_call x2 -> x3, Pallas kernels: 7.08 us -> 3.57 us  [the longest x1 2.72 us: body(): pl.pallas_call(functools.partial(terms_kernel, surf_count, pair_count), o...]
    concatenate x0 -> x2, other arithmetic: none -> 0.97 us  [the longest x1 0.93 us: body(): return (jnp.concatenate(updated, axis=1), kept)]
    add x1, other arithmetic: 1.56 us -> 0.65 us  [body(): kept = kept + to_outer(piece, -shift).astype(jnp.float32)]
    dynamic_slice x1 -> x0, local copies, waits for them, and re-layouts: 0.77 us -> none  [body(): mine = lax.dynamic_slice_in_dim(weights, dest * slots, slots, axis=0)]
    unnamed x20 -> x2, local copies, waits for them, and re-layouts: 0.74 us -> 0.01 us
  transfers between devices with their start and end apart: 10 -> 10, of which waited for: 6 -> 5; matrix products, arithmetic and copies ran while one was open for 2% -> 3% of each run, Pallas kernels for 0% -> 1%
where the time goes in v3:
time: 34.1 us; the launch traced here: 34 us
  waiting for transfers between devices  14 us (41%)
  starting transfers between devices  13.9 us (41%)
  Pallas kernels  3.57 us (10%)
  other arithmetic  1.74 us (5%)
  between operations  0.74 us (2%)
    ppermute x6, starting transfers between devices, to_tile(): return lax.ppermute(piece, 'surf', moves)  9.14 us
    ppermute x6, waiting for transfers between devices, to_tile(): return lax.ppermute(piece, 'surf', moves)  7.56 us
    ppermute x2, waiting for transfers between devices, to_outer(): return lax.ppermute(piece, 'pair', moves)  5.15 us
    ppermute x2, starting transfers between devices, to_outer(): return lax.ppermute(piece, 'pair', moves)  4.6 us
    pallas_call x1, Pallas kernels, body(): pl.pallas_call(functools.partial(terms_kernel, surf_count, pair_count), o...  2.72 us
    ppermute x2, waiting for transfers between devices, to_peer(): return lax.ppermute(piece, 'pair', [(i, i ^ 1) for i in range(pair_count)])  1.29 us
    concatenate x1, other arithmetic, body(): return (jnp.concatenate(updated, axis=1), kept)  0.93 us
    pallas_call x2, Pallas kernels, body(): pl.pallas_call(functools.partial(update_kernel, chunk, outer_count), out_...  0.85 us
  transfers between devices with their start and end apart: 10, of which 5 were waited for; matrix products, arithmetic and copies ran while one was open for 3% of the time, Pallas kernels for 1%

profile of v3, /device:TPU:0, one launch (start us, length us, event | category | flops | bytes accessed | tf_op | source)
XLA Modules:
  0.0 34.0 jit_solution(12291663121482069931)
XLA Ops:
  0.6 2.7 %terms.1 = (bf16[6,192,128]{2,1,0:T(8,128)(2,1)S(1)}, bf16[6,192,128]{2,1,0:T(8,128)(2,1)S(1)}, f32[4,192,192]{2,1,0:T(8,128)S(1)}, bf16[6,96,128]{2,1,0:T(8,128...) custom-call(bf16[2,4,192,128]{3,2,1,0:T(8,128)(2,1)} %bitcast.14, ...), custom_call_target="tpu_custom_call" | custom-call | tf_op jit(solution)/shard_map/terms/pallas_call | solution.py:159
  3.4 3.0 %collective-permute-start.4 = (bf16[8,192,128]{2,1,0:T(8,128)(2,1)S(1)}, bf16[8,192,128]{2,1,0:T(8,128)(2,1)S(1)}, u32[]{:S(2)}, u32[]{:S(2)}) collective-permute-start(bf16[8,192,128]{2,1,0:T(8,128)(2,1)S(1)} %get-tuple-element.27), channel_id=1, source_target_pairs={{0,2},{1,3},{2,0},{3,1},{4,6},{5,7},{6,4},{7,5},{8,10},{9,11},{10,... | collective-permute-start | bytes 1179656 | tf_op jit(solution)/shard_map/ppermute | solution.py:148
  6.4 1.5 %collective-permute-start.2 = (bf16[6,96,128]{2,1,0:T(8,128)(2,1)S(1)}, bf16[6,96,128]{2,1,0:T(8,128)(2,1)S(1)}, u32[]{:S(2)}, u32[]{:S(2)}) collective-permute-start(bf16[6,96,128]{2,1,0:T(8,128)(2,1)S(1)} %get-tuple-element.24), channel_id=1, source_target_pairs={{0,4},{4,0},{8,12},{12,8},{16,20},{20,16},{24,28},{28,24},{1,5},{5... | collective-permute-start | bytes 442376 | tf_op jit(solution)/shard_map/ppermute | solution.py:144
  7.9 0.5 %collective-permute-start.6 = (bf16[6,96,128]{2,1,0:T(8,128)(2,1)S(1)}, bf16[6,96,128]{2,1,0:T(8,128)(2,1)S(1)}, u32[]{:S(2)}, u32[]{:S(2)}) collective-permute-start(bf16[6,96,128]{2,1,0:T(8,128)(2,1)S(1)} %get-tuple-element.30), channel_id=1, source_target_pairs={{0,4},{4,0},{8,12},{12,8},{16,20},{20,16},{24,28},{28,24},{1,5},{5... | collective-permute-start | bytes 442376 | tf_op jit(solution)/shard_map/ppermute | solution.py:144
  8.4 3.6 %collective-permute-start = (bf16[6,192,128]{2,1,0:T(8,128)(2,1)S(1)}, bf16[6,192,128]{2,1,0:T(8,128)(2,1)S(1)}, u32[]{:S(2)}, u32[]{:S(2)}) collective-permute-start(bf16[6,192,128]{2,1,0:T(8,128)(2,1)S(1)} %get-tuple-element.21), channel_id=1, source_target_pairs={{0,24},{4,12},{8,0},{12,20},{16,8},{20,28},{24,16},{28,4},{1,25},{... | collective-permute-start | bytes 884744 | tf_op jit(solution)/shard_map/ppermute | solution.py:144
  12.0 0.0 collective-permute-start.1
  12.0 3.5 %collective-permute-done.4 = bf16[8,192,128]{2,1,0:T(8,128)(2,1)S(1)} collective-permute-done((bf16[8,192,128]{2,1,0:T(8,128)(2,1)S(1)}, bf16[8,192,128]{2,1,0:T(8,128)(2,1)S(1)}, u32[]{:S(2)}, u32[]{:S(2)}) %collective-permute-start.4) | collective-permute-done | bytes 393248 | tf_op jit(solution)/shard_map/ppermute | solution.py:148
  15.6 0.0 copy-start
  15.6 0.1 collective-permute-start.5
  15.7 0.0 collective-permute-done.2
  15.8 1.9 %collective-permute-start.3 = (bf16[6,96,128]{2,1,0:T(8,128)(2,1)S(1)}, bf16[6,96,128]{2,1,0:T(8,128)(2,1)S(1)}, u32[]{:S(2)}, u32[]{:S(2)}) collective-permute-start(bf16[6,96,128]{2,1,0:T(8,128)(2,1)S(1)} %add_convert_fusion.1), channel_id=1, source_target_pairs={{0,8},{4,28},{8,16},{12,4},{16,24},{20,12},{24,0},{28,20},{1,9},{5... | collective-permute-start | bytes 442376 | tf_op jit(solution)/shard_map/ppermute | solution.py:144
  17.6 0.0 collective-permute-done.6
  17.7 1.6 %collective-permute-start.7 = (bf16[6,96,128]{2,1,0:T(8,128)(2,1)S(1)}, bf16[6,96,128]{2,1,0:T(8,128)(2,1)S(1)}, u32[]{:S(2)}, u32[]{:S(2)}) collective-permute-start(bf16[6,96,128]{2,1,0:T(8,128)(2,1)S(1)} %add_convert_fusion), channel_id=1, source_target_pairs={{0,8},{4,28},{8,16},{12,4},{16,24},{20,12},{24,0},{28,20},{1,9},{5... | collective-permute-start | bytes 442376 | tf_op jit(solution)/shard_map/ppermute | solution.py:144
  19.3 5.0 %collective-permute-done.3.refs_4_ = bf16[6,96,128]{2,1,0:T(8,128)(2,1)S(1)} collective-permute-done((bf16[6,96,128]{2,1,0:T(8,128)(2,1)S(1)}, bf16[6,96,128]{2,1,0:T(8,128)(2,1)S(1)}, u32[]{:S(2)}, u32[]{:S(2)}) %collective-permute-start.3) | collective-permute-done | bytes 147488 | tf_op jit(solution)/shard_map/ppermute | solution.py:144
  24.4 0.0 collective-permute-done.refs_2_
  24.4 0.0 collective-permute-done.1.refs_3_
  24.4 0.0 collective-permute-done.5.refs_6_
  24.4 0.0 copy-done
  24.4 0.4 %update.2 = (f32[4,96,192]{2,1,0:T(8,128)S(1)}, f32[192,128]{1,0:T(8,128)S(1)}, bf16[2,192,128]{2,1,0:T(8,128)(2,1)S(1)}, f32[192,128]{1,0:T(8,128)S(1)}) custom-call(f32[4,192,192]{2,1,0:T(8,128)S(1)} %copy-done, f32[4,192,192]{2,1,0:T(8,128)S(1)} %get-tuple-element.20.refs_1_, bf16[6,192,128]{2,1,0:T(8,128)(2,1)S(1)} %collective-permute-done.refs_2_, ...), custom_call_target="tpu_custom_call" | custom-call | tf_op jit(solution)/shard_map/update/pallas_call | solution.py:192
  24.8 2.5 %collective-permute-done.7.refs_4_ = bf16[6,96,128]{2,1,0:T(8,128)(2,1)S(1)} collective-permute-done((bf16[6,96,128]{2,1,0:T(8,128)(2,1)S(1)}, bf16[6,96,128]{2,1,0:T(8,128)(2,1)S(1)}, u32[]{:S(2)}, u32[]{:S(2)}) %collective-permute-start.7) | collective-permute-done | bytes 147488 | tf_op jit(solution)/shard_map/ppermute | solution.py:144
  27.3 0.4 %update.3 = (f32[4,96,192]{2,1,0:T(8,128)S(1)}, f32[192,128]{1,0:T(8,128)S(1)}, bf16[2,192,128]{2,1,0:T(8,128)(2,1)S(1)}, f32[192,128]{1,0:T(8,128)S(1)}) custom-call(f32[4,192,192]{2,1,0:T(8,128)S(1)} %copy-done, f32[4,192,192]{2,1,0:T(8,128)S(1)} %get-tuple-element.20.refs_1_, ...), custom_call_target="tpu_custom_call", output_to_operand_aliasing={{1}: (8, {}), {2}: (9, {}), {3}: (10, {})} | custom-call | tf_op jit(solution)/shard_map/update/pallas_call | solution.py:192
  27.7 0.1 collective-permute-start.8
  27.8 1.3 %collective-permute-done.8 = bf16[2,192,128]{2,1,0:T(8,128)(2,1)S(1)} collective-permute-done((bf16[2,192,128]{2,1,0:T(8,128)(2,1)S(1)}, bf16[2,192,128]{2,1,0:T(8,128)(2,1)S(1)}, u32[]{:S(2)}, u32[]{:S(2)}) %collective-permute-start.8) | collective-permute-done | bytes 98336 | tf_op jit(solution)/shard_map/ppermute | solution.py:151
  29.1 1.6 %collective-permute-start.9 = (bf16[192,128]{1,0:T(8,128)(2,1)S(1)}, bf16[192,128]{1,0:T(8,128)(2,1)S(1)}, u32[]{:S(2)}, u32[]{:S(2)}) collective-permute-start(bf16[192,128]{1,0:T(8,128)(2,1)S(1)} %fusion.1), channel_id=1, source_target_pairs={{0,2},{1,3},{2,0},{3,1},{4,6},{5,7},{6,4},{7,5},{8,10},{9,11},{10,... | collective-permute-start | bytes 147464 | tf_op jit(solution)/shard_map/ppermute | solution.py:148
  30.7 0.9 %pad_maximum_fusion = f32[4,192,192]{2,1,0:T(8,128)} fusion(f32[4,96,192]{2,1,0:T(8,128)S(1)} %get-tuple-element.34, f32[4,96,192]{2,1,0:T(8,128)S(1)} %get-tuple-element.28), kind=kLoop, calls=%fused_computation | loop fusion | flops 147456 | bytes 1179648 | tf_op jit(solution)/shard_map/concatenate | solution.py:209
  31.6 1.7 %collective-permute-done.9 = bf16[192,128]{1,0:T(8,128)(2,1)S(1)} collective-permute-done((bf16[192,128]{1,0:T(8,128)(2,1)S(1)}, bf16[192,128]{1,0:T(8,128)(2,1)S(1)}, u32[]{:S(2)}, u32[]{:S(2)}) %collective-permute-start.9) | collective-permute-done | bytes 49184 | tf_op jit(solution)/shard_map/ppermute | solution.py:148
  33.3 0.7 %fusion.3 = f32[192,128]{1,0:T(8,128)} fusion(f32[192,128]{1,0:T(8,128)S(1)} %get-tuple-element.35, f32[2,192,128]{2,1,0:T(8,128)S(1)} %convert_element_type.33, bf16[192,128]{1,0:T(8,128)(2,1)S(1)} %collective-permute-done.9), kind=kLoop, calls=%fused_computation.9 | loop fusion | flops 73728 | bytes 344064 | tf_op jit(solution)/shard_map/add | solution.py:208
  (6 shorter events, 0.2 us)
Async XLA Ops:
  3.4 12.2 %collective-permute-start.4 = (bf16[8,192,128]{2,1,0:T(8,128)(2,1)S(1)}, bf16[8,192,128]{2,1,0:T(8,128)(2,1)S(1)}, u32[]{:S(2)}, u32[]{:S(2)}) collective-permute-start(bf16[8,192,128]{2,1,0:T(8,128)(2,1)S(1)} %get-tuple-element.27), channel_id=1, source_target_pairs={{0,2},{1,3},{2,0},{3,1},{4,6},{5,7},{6,4},{7,5},{8,10},{9,11},{10,... | collective-permute-start | bytes 1179656 | tf_op jit(solution)/shard_map/ppermute | solution.py:148
  6.4 9.3 %collective-permute-start.2 = (bf16[6,96,128]{2,1,0:T(8,128)(2,1)S(1)}, bf16[6,96,128]{2,1,0:T(8,128)(2,1)S(1)}, u32[]{:S(2)}, u32[]{:S(2)}) collective-permute-start(bf16[6,96,128]{2,1,0:T(8,128)(2,1)S(1)} %get-tuple-element.24), channel_id=1, source_target_pairs={{0,4},{4,0},{8,12},{12,8},{16,20},{20,16},{24,28},{28,24},{1,5},{5... | collective-permute-start | bytes 442376 | tf_op jit(solution)/shard_map/ppermute | solution.py:144
  7.9 9.7 %collective-permute-start.6 = (bf16[6,96,128]{2,1,0:T(8,128)(2,1)S(1)}, bf16[6,96,128]{2,1,0:T(8,128)(2,1)S(1)}, u32[]{:S(2)}, u32[]{:S(2)}) collective-permute-start(bf16[6,96,128]{2,1,0:T(8,128)(2,1)S(1)} %get-tuple-element.30), channel_id=1, source_target_pairs={{0,4},{4,0},{8,12},{12,8},{16,20},{20,16},{24,28},{28,24},{1,5},{5... | collective-permute-start | bytes 442376 | tf_op jit(solution)/shard_map/ppermute | solution.py:144
  8.4 15.9 %collective-permute-start = (bf16[6,192,128]{2,1,0:T(8,128)(2,1)S(1)}, bf16[6,192,128]{2,1,0:T(8,128)(2,1)S(1)}, u32[]{:S(2)}, u32[]{:S(2)}) collective-permute-start(bf16[6,192,128]{2,1,0:T(8,128)(2,1)S(1)} %get-tuple-element.21), channel_id=1, source_target_pairs={{0,24},{4,12},{8,0},{12,20},{16,8},{20,28},{24,16},{28,4},{1,25},{... | collective-permute-start | bytes 884744 | tf_op jit(solution)/shard_map/ppermute | solution.py:144
  12.0 12.3 %collective-permute-start.1 = (bf16[6,192,128]{2,1,0:T(8,128)(2,1)S(1)}, bf16[6,192,128]{2,1,0:T(8,128)(2,1)S(1)}, u32[]{:S(2)}, u32[]{:S(2)}) collective-permute-start(bf16[6,192,128]{2,1,0:T(8,128)(2,1)S(1)} %get-tuple-element.22), channel_id=1, source_target_pairs={{0,4},{4,0},{8,12},{12,8},{16,20},{20,16},{24,28},{28,24},{1,5},{5... | collective-permute-start | bytes 884744 | tf_op jit(solution)/shard_map/ppermute | solution.py:144
  15.6 8.8 %copy-start = (f32[4,192,192]{2,1,0:T(8,128)S(1)}, f32[4,192,192]{2,1,0:T(8,128)}, u32[]{:S(2)}) copy-start(f32[4,192,192]{2,1,0:T(8,128)} %refs_0_.3) | copy-start | bytes 1769476
  15.6 8.8 %collective-permute-start.5 = (bf16[8,192,128]{2,1,0:T(8,128)(2,1)S(1)}, bf16[8,192,128]{2,1,0:T(8,128)(2,1)S(1)}, u32[]{:S(2)}, u32[]{:S(2)}) collective-permute-start(bf16[8,192,128]{2,1,0:T(8,128)(2,1)S(1)} %pad_maximum_fusion.1), channel_id=1, source_target_pairs={{0,1},{1,0},{2,3},{3,2},{4,5},{5,4},{6,7},{7,6},{8,9},{9,8},{10,11... | collective-permute-start | bytes 1179656 | tf_op jit(solution)/shard_map/ppermute | solution.py:151
  15.8 8.6 %collective-permute-start.3 = (bf16[6,96,128]{2,1,0:T(8,128)(2,1)S(1)}, bf16[6,96,128]{2,1,0:T(8,128)(2,1)S(1)}, u32[]{:S(2)}, u32[]{:S(2)}) collective-permute-start(bf16[6,96,128]{2,1,0:T(8,128)(2,1)S(1)} %add_convert_fusion.1), channel_id=1, source_target_pairs={{0,8},{4,28},{8,16},{12,4},{16,24},{20,12},{24,0},{28,20},{1,9},{5... | collective-permute-start | bytes 442376 | tf_op jit(solution)/shard_map/ppermute | solution.py:144
  17.7 9.6 %collective-permute-start.7 = (bf16[6,96,128]{2,1,0:T(8,128)(2,1)S(1)}, bf16[6,96,128]{2,1,0:T(8,128)(2,1)S(1)}, u32[]{:S(2)}, u32[]{:S(2)}) collective-permute-start(bf16[6,96,128]{2,1,0:T(8,128)(2,1)S(1)} %add_convert_fusion), channel_id=1, source_target_pairs={{0,8},{4,28},{8,16},{12,4},{16,24},{20,12},{24,0},{28,20},{1,9},{5... | collective-permute-start | bytes 442376 | tf_op jit(solution)/shard_map/ppermute | solution.py:144
  27.7 1.4 %collective-permute-start.8 = (bf16[2,192,128]{2,1,0:T(8,128)(2,1)S(1)}, bf16[2,192,128]{2,1,0:T(8,128)(2,1)S(1)}, u32[]{:S(2)}, u32[]{:S(2)}) collective-permute-start(bf16[2,192,128]{2,1,0:T(8,128)(2,1)S(1)} %get-tuple-element.36), channel_id=1, source_target_pairs={{0,1},{1,0},{2,3},{3,2},{4,5},{5,4},{6,7},{7,6},{8,9},{9,8},{10,11... | collective-permute-start | bytes 294920 | tf_op jit(solution)/shard_map/ppermute | solution.py:151
  29.1 4.2 %collective-permute-start.9 = (bf16[192,128]{1,0:T(8,128)(2,1)S(1)}, bf16[192,128]{1,0:T(8,128)(2,1)S(1)}, u32[]{:S(2)}, u32[]{:S(2)}) collective-permute-start(bf16[192,128]{1,0:T(8,128)(2,1)S(1)} %fusion.1), channel_id=1, source_target_pairs={{0,2},{1,3},{2,0},{3,1},{4,6},{5,7},{6,4},{7,5},{8,10},{9,11},{10,... | collective-permute-start | bytes 147464 | tf_op jit(solution)/shard_map/ppermute | solution.py:148

commit v4 on v3

--- a/solution.py
+++ b/solution.py
@@ -12,6 +12,11 @@
 DIRECT, FAR, OWN, NEAR, COMB = range(ROLES)
 LANES = 128
 CHUNKS = 2
+
+
+def chunk_rows(skeleton):
+    cuts = [skeleton * at // CHUNKS // 16 * 16 for at in range(CHUNKS)] + [skeleton]
+    return list(zip(cuts, cuts[1:]))
 
 
 def dot_nt(a, b):
@@ -29,13 +34,11 @@
     tail = skeleton - LANES
     read_target = pltpu.make_async_copy(target_hbm, target_ref, target_sem)
     read_target.start()
-    copies = []
-    for box in range(box_count):
-        group = []
-        for hbm, ref in ((inv_hbm, inv_ref), (rt_hbm, rt_ref), (lt_hbm, lt_ref)):
-            group.append(pltpu.make_async_copy(hbm.at[box], ref.at[box], sem.at[3 * box + len(group)]))
-            group[-1].start()
-        copies.append(group)
+    copies = [
+        pltpu.make_async_copy(hbm, ref, sem.at[at]) for at, (hbm, ref) in enumerate(((inv_hbm, inv_ref), (rt_hbm, rt_ref), (lt_hbm, lt_ref)))
+    ]
+    for copy in copies:
+        copy.start()
     pair = lax.axis_index("pair")
     outer, inner = pair // 2, lax.rem(pair, 2)
     cuts = []
@@ -59,13 +62,13 @@
         ahead = jnp.where(ahead <= REACH, ahead, ahead - surf_count)
         return (jnp.where(even, ahead, -ahead) + REACH) * slots + lax.rem(block, slots)
 
+    copies[0].wait()
+    copies[1].wait()
+    solves = [[dot_nt(rt_ref[box, k], inv_ref[box]).astype(jnp.bfloat16) for k in range(neighbours)] for box in range(box_count)]
+    copies[2].wait()
     read_target.wait()
     for box in range(box_count):
-        for copy in copies[box]:
-            copy.wait()
-        inverse = inv_ref[box]
-        left = [lt_ref[box, k] for k in range(neighbours)]
-        solved = [dot_nt(rt_ref[box, k], inverse).astype(jnp.bfloat16) for k in range(neighbours)]
+        left, solved = [lt_ref[box, k] for k in range(neighbours)], solves[box]
         for second in range(neighbours):
             both = jnp.concatenate([solved[second], left[second]], axis=1)
             both = jnp.concatenate([both, both[LANES:]], axis=0)
@@ -77,9 +80,9 @@
                 acc[cell(box, first, second)] += term
     lane = lax.broadcasted_iota(jnp.int32, (skeleton, LANES), 1)
     for role, refs in ((FAR, far_refs), (DIRECT, [direct_ref]), (COMB, comb_refs), (NEAR, [near_ref])):
-        rows = skeleton // len(refs)
-        for chunk, ref in enumerate(refs):
-            span = slice(chunk * rows, (chunk + 1) * rows)
+        spans = chunk_rows(skeleton) if len(refs) == CHUNKS else [(0, skeleton)]
+        for (start, stop), ref in zip(spans, refs):
+            span, rows = slice(start, stop), stop - start
             for slot in range(slots):
                 ref[slot] = acc[role * slots + slot, span, :LANES].astype(jnp.bfloat16)
             for two in range(slots // 2):
@@ -94,10 +97,9 @@
 def update_kernel(chunk, outer_count, *refs):
     blocks_ref, own_ref, direct_ref, near_ref, comb_ref, kept_w, peer_w = refs[:7]
     outer_w = refs[7 : 6 + outer_count]
-    updated_ref, kept_ref, peer_ref, *outer_refs = refs[-2 - outer_count :]
+    updated_ref, kept_ref, *part_refs = refs[-1 - 2 * outer_count :]
     slots, skeleton, _ = own_ref.shape
-    rows = comb_ref.shape[1]
-    span = slice(chunk * rows, (chunk + 1) * rows)
+    span = slice(*chunk_rows(skeleton)[chunk])
     tail = skeleton - LANES
 
     def received(row):
@@ -119,10 +121,8 @@
                 part = jnp.dot(rounded, panel[base + slot], preferred_element_type=jnp.float32)
                 total[at] = part if total[at] is None else total[at] + part
     kept_ref[span] = total[0]
-    peer_ref[0, span] = total[1].astype(peer_ref.dtype)
-    for shift in range(outer_count - 1):
-        outer_refs[shift][span] = total[2 + 2 * shift]
-        peer_ref[1 + shift, span] = total[3 + 2 * shift].astype(peer_ref.dtype)
+    for at, ref in enumerate(part_refs, 1):
+        ref[span] = total[at].astype(ref.dtype)
 
 
 def body(left_panel, right_panel, inverse, target, blocks, weights):
@@ -132,7 +132,7 @@
     outer_count = pair_count // 2
     slots = blocks.shape[0]
     columns = weights.shape[2]
-    rows = skeleton // CHUNKS
+    rows = [stop - start for start, stop in chunk_rows(skeleton)]
     vmem = pl.BlockSpec(memory_space=pltpu.VMEM)
     hbm = pl.BlockSpec(memory_space=pltpu.HBM)
 
@@ -152,9 +152,9 @@
 
     panels_shape = (box_count, neighbours, skeleton, redundant)
     full = shape(slots + slots // 2, skeleton, LANES)
-    part = shape(slots + slots // 2, rows, LANES)
+    parts = [shape(slots + slots // 2, count, LANES) for count in rows]
     cuts = [shape(slots, skeleton, columns)] + [shape(2 * slots, skeleton, columns)] * (outer_count - 1) + [shape(slots, skeleton, columns)]
-    out_shape = [full, full, shape(*blocks.shape, dtype=jnp.float32)] + [part] * (2 * CHUNKS) + cuts
+    out_shape = [full, full, shape(*blocks.shape, dtype=jnp.float32)] + 2 * parts + cuts
     args = (jnp.swapaxes(left_panel, 2, 3), jnp.swapaxes(right_panel, 2, 3), inverse, weights, target)
     direct, near, own, *out = pl.pallas_call(
         functools.partial(terms_kernel, surf_count, pair_count),
@@ -167,7 +167,7 @@
             pltpu.VMEM((box_count, redundant, redundant), jnp.bfloat16),
             pltpu.SMEM(target.shape, target.dtype),
             pltpu.VMEM((ROLES * slots, skeleton, 2 * LANES), jnp.float32),
-            pltpu.SemaphoreType.DMA((3 * box_count,)),
+            pltpu.SemaphoreType.DMA((3,)),
             pltpu.SemaphoreType.DMA((pair_count,)),
             pltpu.SemaphoreType.DMA,
         ],
@@ -191,21 +191,20 @@
         inputs = [blocks, own, direct, near, comb[chunk], kept_w, peer_w, *outer_w]
         fresh, *sums = pl.pallas_call(
             functools.partial(update_kernel, chunk, outer_count),
-            out_shape=[shape(slots, rows, skeleton, dtype=jnp.float32), shape(skeleton, columns, dtype=jnp.float32), shape(outer_count, skeleton, columns)]
-            + [shape(skeleton, columns, dtype=jnp.float32)] * (outer_count - 1),
+            out_shape=[shape(slots, rows[chunk], skeleton, dtype=jnp.float32), shape(skeleton, columns, dtype=jnp.float32)]
+            + [shape(skeleton, columns)] * (pair_count - 1),
             in_specs=[vmem] * (len(inputs) + len(sums)),
-            out_specs=[vmem] * (2 + outer_count),
+            out_specs=[vmem] * (1 + pair_count),
             input_output_aliases={len(inputs) + at: 1 + at for at in range(len(sums))},
             compiler_params=pltpu.CompilerParams(vmem_limit_bytes=8 << 20),
             name="update",
         )(*inputs, *sums)
         updated.append(fresh)
-    kept, peer, *outer = sums
-    peer = to_peer(peer).astype(jnp.float32)
-    kept = kept + peer[0]
-    for shift in range(1, outer_count):
-        piece = (outer[shift - 1] + peer[shift]).astype(jnp.bfloat16)
-        kept = kept + to_outer(piece, -shift).astype(jnp.float32)
+    kept, *parts = sums
+    for at, piece in enumerate(parts, 1):
+        shift, cross = divmod(at, 2)
+        moves = [(i, ((i // 2 - shift) % outer_count) * 2 + (i % 2 ^ cross)) for i in range(pair_count)]
+        kept = kept + lax.ppermute(piece, "pair", moves).astype(jnp.float32)
     return (jnp.concatenate(updated, axis=1), kept)
 
 

time: 34.1 us -> 33.8 us (level)
  waiting for transfers between devices: 14 us -> 13.5 us
    ppermute x0 -> x3, waiting for transfers between devices: none -> 2.48 us  [body(): kept = kept + lax.ppermute(piece, 'pair', moves).astype(jnp.float32)]
    ppermute x0 -> x3, starting transfers between devices: none -> 1.92 us  [body(): kept = kept + lax.ppermute(piece, 'pair', moves).astype(jnp.float32)]
    ppermute x2 -> x1, waiting for transfers between devices: 5.15 us -> 3.48 us  [to_outer(): return lax.ppermute(piece, 'pair', moves)]
    ppermute x2 -> x1, starting transfers between devices: 4.6 us -> 3.03 us  [to_outer(): return lax.ppermute(piece, 'pair', moves)]
    ppermute x2 -> x1, waiting for transfers between devices: 1.29 us -> 0.01 us  [to_peer(): return lax.ppermute(piece, 'pair', [(i, i ^ 1) for i in range(pair_count)])]
  transfers between devices with their start and end apart: 10 -> 11, of which waited for: 5 -> 5; matrix products, arithmetic and copies ran while one was open for 3% -> 3% of each run, Pallas kernels for 1% -> 1%
where the time goes in v4:
time: 33.8 us; the launch traced here: 33.7 us
  starting transfers between devices  14.2 us (42%)
  waiting for transfers between devices  13.5 us (40%)
  Pallas kernels  3.53 us (10%)
  other arithmetic  1.72 us (5%)
  between operations  0.73 us (2%)
    ppermute x6, starting transfers between devices, to_tile(): return lax.ppermute(piece, 'surf', moves)  9.14 us
    ppermute x6, waiting for transfers between devices, to_tile(): return lax.ppermute(piece, 'surf', moves)  7.56 us
    ppermute x1, waiting for transfers between devices, to_outer(): return lax.ppermute(piece, 'pair', moves)  3.48 us
    ppermute x1, starting transfers between devices, to_outer(): return lax.ppermute(piece, 'pair', moves)  3.03 us
    pallas_call x1, Pallas kernels, body(): pl.pallas_call(functools.partial(terms_kernel, surf_count, pair_count), o...  2.67 us
    ppermute x3, waiting for transfers between devices, body(): kept = kept + lax.ppermute(piece, 'pair', moves).astype(jnp.float32)  2.48 us
    ppermute x3, starting transfers between devices, body(): kept = kept + lax.ppermute(piece, 'pair', moves).astype(jnp.float32)  1.92 us
    concatenate x1, other arithmetic, body(): return (jnp.concatenate(updated, axis=1), kept)  0.93 us
  transfers between devices with their start and end apart: 11, of which 5 were waited for; matrix products, arithmetic and copies ran while one was open for 3% of the time, Pallas kernels for 1%

profile of v4, /device:TPU:0, one launch (start us, length us, event | category | flops | bytes accessed | tf_op | source)
XLA Modules:
  0.0 33.7 jit_solution(16070996114275861153)
XLA Ops:
  0.6 2.7 %terms.1 = (bf16[6,192,128]{2,1,0:T(8,128)(2,1)S(1)}, bf16[6,192,128]{2,1,0:T(8,128)(2,1)S(1)}, f32[4,192,192]{2,1,0:T(8,128)S(1)}, bf16[6,96,128]{2,1,0:T(8,128...) custom-call(bf16[2,4,192,128]{3,2,1,0:T(8,128)(2,1)} %bitcast.2, ...), custom_call_target="tpu_custom_call" | custom-call | tf_op jit(solution)/shard_map/terms/pallas_call | solution.py:159
  3.3 3.0 %collective-permute-start.4 = (bf16[8,192,128]{2,1,0:T(8,128)(2,1)S(1)}, bf16[8,192,128]{2,1,0:T(8,128)(2,1)S(1)}, u32[]{:S(2)}, u32[]{:S(2)}) collective-permute-start(bf16[8,192,128]{2,1,0:T(8,128)(2,1)S(1)} %get-tuple-element.29), channel_id=1, source_target_pairs={{0,2},{1,3},{2,0},{3,1},{4,6},{5,7},{6,4},{7,5},{8,10},{9,11},{10,... | collective-permute-start | bytes 1179656 | tf_op jit(solution)/shard_map/ppermute | solution.py:148
  6.3 1.5 %collective-permute-start.2 = (bf16[6,96,128]{2,1,0:T(8,128)(2,1)S(1)}, bf16[6,96,128]{2,1,0:T(8,128)(2,1)S(1)}, u32[]{:S(2)}, u32[]{:S(2)}) collective-permute-start(bf16[6,96,128]{2,1,0:T(8,128)(2,1)S(1)} %get-tuple-element.26), channel_id=1, source_target_pairs={{0,4},{4,0},{8,12},{12,8},{16,20},{20,16},{24,28},{28,24},{1,5},{5... | collective-permute-start | bytes 442376 | tf_op jit(solution)/shard_map/ppermute | solution.py:144
  7.9 0.5 %collective-permute-start.6 = (bf16[6,96,128]{2,1,0:T(8,128)(2,1)S(1)}, bf16[6,96,128]{2,1,0:T(8,128)(2,1)S(1)}, u32[]{:S(2)}, u32[]{:S(2)}) collective-permute-start(bf16[6,96,128]{2,1,0:T(8,128)(2,1)S(1)} %get-tuple-element.32), channel_id=1, source_target_pairs={{0,4},{4,0},{8,12},{12,8},{16,20},{20,16},{24,28},{28,24},{1,5},{5... | collective-permute-start | bytes 442376 | tf_op jit(solution)/shard_map/ppermute | solution.py:144
  8.4 3.6 %collective-permute-start = (bf16[6,192,128]{2,1,0:T(8,128)(2,1)S(1)}, bf16[6,192,128]{2,1,0:T(8,128)(2,1)S(1)}, u32[]{:S(2)}, u32[]{:S(2)}) collective-permute-start(bf16[6,192,128]{2,1,0:T(8,128)(2,1)S(1)} %get-tuple-element.23), channel_id=1, source_target_pairs={{0,24},{4,12},{8,0},{12,20},{16,8},{20,28},{24,16},{28,4},{1,25},{... | collective-permute-start | bytes 884744 | tf_op jit(solution)/shard_map/ppermute | solution.py:144
  12.0 0.0 collective-permute-start.1
  12.0 3.5 %collective-permute-done.4 = bf16[8,192,128]{2,1,0:T(8,128)(2,1)S(1)} collective-permute-done((bf16[8,192,128]{2,1,0:T(8,128)(2,1)S(1)}, bf16[8,192,128]{2,1,0:T(8,128)(2,1)S(1)}, u32[]{:S(2)}, u32[]{:S(2)}) %collective-permute-start.4) | collective-permute-done | bytes 393248 | tf_op jit(solution)/shard_map/ppermute | solution.py:148
  15.5 0.0 copy-start
  15.6 0.1 collective-permute-start.5
  15.6 0.0 collective-permute-done.2
  15.7 1.9 %collective-permute-start.3 = (bf16[6,96,128]{2,1,0:T(8,128)(2,1)S(1)}, bf16[6,96,128]{2,1,0:T(8,128)(2,1)S(1)}, u32[]{:S(2)}, u32[]{:S(2)}) collective-permute-start(bf16[6,96,128]{2,1,0:T(8,128)(2,1)S(1)} %add_convert_fusion.1), channel_id=1, source_target_pairs={{0,8},{4,28},{8,16},{12,4},{16,24},{20,12},{24,0},{28,20},{1,9},{5... | collective-permute-start | bytes 442376 | tf_op jit(solution)/shard_map/ppermute | solution.py:144
  17.6 0.0 collective-permute-done.6
  17.6 1.6 %collective-permute-start.7 = (bf16[6,96,128]{2,1,0:T(8,128)(2,1)S(1)}, bf16[6,96,128]{2,1,0:T(8,128)(2,1)S(1)}, u32[]{:S(2)}, u32[]{:S(2)}) collective-permute-start(bf16[6,96,128]{2,1,0:T(8,128)(2,1)S(1)} %add_convert_fusion), channel_id=1, source_target_pairs={{0,8},{4,28},{8,16},{12,4},{16,24},{20,12},{24,0},{28,20},{1,9},{5... | collective-permute-start | bytes 442376 | tf_op jit(solution)/shard_map/ppermute | solution.py:144
  19.2 5.1 %collective-permute-done.3.refs_4_ = bf16[6,96,128]{2,1,0:T(8,128)(2,1)S(1)} collective-permute-done((bf16[6,96,128]{2,1,0:T(8,128)(2,1)S(1)}, bf16[6,96,128]{2,1,0:T(8,128)(2,1)S(1)}, u32[]{:S(2)}, u32[]{:S(2)}) %collective-permute-start.3) | collective-permute-done | bytes 147488 | tf_op jit(solution)/shard_map/ppermute | solution.py:144
  24.3 0.0 collective-permute-done.refs_2_
  24.3 0.0 collective-permute-done.1.refs_3_
  24.3 0.0 collective-permute-done.5.refs_6_
  24.3 0.0 copy-done
  24.3 0.4 %update.2 = (f32[4,96,192]{2,1,0:T(8,128)S(1)}, f32[192,128]{1,0:T(8,128)S(1)}, bf16[192,128]{1,0:T(8,128)(2,1)S(1)}, bf16[192,128]{1,0:T(8,128)(2,1)S(1)}, bf16[192,128]{1,0:T(8,128)(2,1)S(1)}) custom-call(f32[4,192,192]{2,1,0:T(8,128)S(1)} %copy-done, f32[4,192,192]{2,1,0:T(8,128)S(1)} %get-tuple-element.22.refs_1_, ...), custom_call_target="tpu_custom_call" | custom-call | tf_op jit(solution)/shard_map/update/pallas_call | solution.py:192
  24.8 2.5 %collective-permute-done.7.refs_4_ = bf16[6,96,128]{2,1,0:T(8,128)(2,1)S(1)} collective-permute-done((bf16[6,96,128]{2,1,0:T(8,128)(2,1)S(1)}, bf16[6,96,128]{2,1,0:T(8,128)(2,1)S(1)}, u32[]{:S(2)}, u32[]{:S(2)}) %collective-permute-start.7) | collective-permute-done | bytes 147488 | tf_op jit(solution)/shard_map/ppermute | solution.py:144
  27.3 0.4 %update.3 = (f32[4,96,192]{2,1,0:T(8,128)S(1)}, f32[192,128]{1,0:T(8,128)S(1)}, bf16[192,128]{1,0:T(8,128)(2,1)S(1)}, bf16[192,128]{1,0:T(8,128)(2,1)S(1)}, bf16[192,128]{1,0:T(8,128)(2,1)S(1)}) custom-call(f32[4,192,192]{2,1,0:T(8,128)S(1)} %copy-done, ...), custom_call_target="tpu_custom_call", output_to_operand_aliasing={{1}: (8, {}), {2}: (9, {}), {3}: (10, {}), {4}: (11, {})} | custom-call | tf_op jit(solution)/shard_map/update/pallas_call | solution.py:192
  27.7 0.1 collective-permute-start.8
  27.8 1.6 %collective-permute-start.9 = (bf16[192,128]{1,0:T(8,128)(2,1)S(1)}, bf16[192,128]{1,0:T(8,128)(2,1)S(1)}, u32[]{:S(2)}, u32[]{:S(2)}) collective-permute-start(bf16[192,128]{1,0:T(8,128)(2,1)S(1)} %get-tuple-element.40), channel_id=1, source_target_pairs={{0,2},{1,3},{2,0},{3,1},{4,6},{5,7},{6,4},{7,5},{8,10},{9,11},{10,... | collective-permute-start | bytes 147464 | tf_op jit(solution)/shard_map/ppermute | solution.py:207
  29.3 0.3 collective-permute-start.10
  29.6 0.9 %pad_maximum_fusion = f32[4,192,192]{2,1,0:T(8,128)} fusion(f32[4,96,192]{2,1,0:T(8,128)S(1)} %get-tuple-element.37, f32[4,96,192]{2,1,0:T(8,128)S(1)} %get-tuple-element.30), kind=kLoop, calls=%fused_computation | loop fusion | flops 147456 | bytes 1179648 | tf_op jit(solution)/shard_map/concatenate | solution.py:208
  30.5 0.0 collective-permute-done.8
  30.5 1.4 %collective-permute-done.9 = bf16[192,128]{1,0:T(8,128)(2,1)S(1)} collective-permute-done((bf16[192,128]{1,0:T(8,128)(2,1)S(1)}, bf16[192,128]{1,0:T(8,128)(2,1)S(1)}, u32[]{:S(2)}, u32[]{:S(2)}) %collective-permute-start.9) | collective-permute-done | bytes 49184 | tf_op jit(solution)/shard_map/ppermute | solution.py:207
  31.9 1.1 %collective-permute-done.10 = bf16[192,128]{1,0:T(8,128)(2,1)S(1)} collective-permute-done((bf16[192,128]{1,0:T(8,128)(2,1)S(1)}, bf16[192,128]{1,0:T(8,128)(2,1)S(1)}, u32[]{:S(2)}, u32[]{:S(2)}) %collective-permute-start.10) | collective-permute-done | bytes 49184 | tf_op jit(solution)/shard_map/ppermute | solution.py:207
  33.0 0.7 %convert_add_fusion = f32[192,128]{1,0:T(8,128)} fusion(bf16[192,128]{1,0:T(8,128)(2,1)S(1)} %collective-permute-done.10, bf16[192,128]{1,0:T(8,128)(2,1)S(1)} %collective-permute-done.9, f32[192,128]{1,0:T(8,128)S(1)} %get-tuple-element.38, bf16[192,128]{1,0:T(8,128)(2,1)S(1)} %collective-permute-done.8), kind=kLoop, calls=%fused_computation.4 | loop fusion | flops 147456 | bytes 344064 | tf_op jit(solution)/shard_map/add | solution.py:207
  (4 shorter events, 0.1 us)
Async XLA Ops:
  3.3 12.1 %collective-permute-start.4 = (bf16[8,192,128]{2,1,0:T(8,128)(2,1)S(1)}, bf16[8,192,128]{2,1,0:T(8,128)(2,1)S(1)}, u32[]{:S(2)}, u32[]{:S(2)}) collective-permute-start(bf16[8,192,128]{2,1,0:T(8,128)(2,1)S(1)} %get-tuple-element.29), channel_id=1, source_target_pairs={{0,2},{1,3},{2,0},{3,1},{4,6},{5,7},{6,4},{7,5},{8,10},{9,11},{10,... | collective-permute-start | bytes 1179656 | tf_op jit(solution)/shard_map/ppermute | solution.py:148
  6.3 9.3 %collective-permute-start.2 = (bf16[6,96,128]{2,1,0:T(8,128)(2,1)S(1)}, bf16[6,96,128]{2,1,0:T(8,128)(2,1)S(1)}, u32[]{:S(2)}, u32[]{:S(2)}) collective-permute-start(bf16[6,96,128]{2,1,0:T(8,128)(2,1)S(1)} %get-tuple-element.26), channel_id=1, source_target_pairs={{0,4},{4,0},{8,12},{12,8},{16,20},{20,16},{24,28},{28,24},{1,5},{5... | collective-permute-start | bytes 442376 | tf_op jit(solution)/shard_map/ppermute | solution.py:144
  7.9 9.7 %collective-permute-start.6 = (bf16[6,96,128]{2,1,0:T(8,128)(2,1)S(1)}, bf16[6,96,128]{2,1,0:T(8,128)(2,1)S(1)}, u32[]{:S(2)}, u32[]{:S(2)}) collective-permute-start(bf16[6,96,128]{2,1,0:T(8,128)(2,1)S(1)} %get-tuple-element.32), channel_id=1, source_target_pairs={{0,4},{4,0},{8,12},{12,8},{16,20},{20,16},{24,28},{28,24},{1,5},{5... | collective-permute-start | bytes 442376 | tf_op jit(solution)/shard_map/ppermute | solution.py:144
  8.4 15.9 %collective-permute-start = (bf16[6,192,128]{2,1,0:T(8,128)(2,1)S(1)}, bf16[6,192,128]{2,1,0:T(8,128)(2,1)S(1)}, u32[]{:S(2)}, u32[]{:S(2)}) collective-permute-start(bf16[6,192,128]{2,1,0:T(8,128)(2,1)S(1)} %get-tuple-element.23), channel_id=1, source_target_pairs={{0,24},{4,12},{8,0},{12,20},{16,8},{20,28},{24,16},{28,4},{1,25},{... | collective-permute-start | bytes 884744 | tf_op jit(solution)/shard_map/ppermute | solution.py:144
  12.0 12.3 %collective-permute-start.1 = (bf16[6,192,128]{2,1,0:T(8,128)(2,1)S(1)}, bf16[6,192,128]{2,1,0:T(8,128)(2,1)S(1)}, u32[]{:S(2)}, u32[]{:S(2)}) collective-permute-start(bf16[6,192,128]{2,1,0:T(8,128)(2,1)S(1)} %get-tuple-element.24), channel_id=1, source_target_pairs={{0,4},{4,0},{8,12},{12,8},{16,20},{20,16},{24,28},{28,24},{1,5},{5... | collective-permute-start | bytes 884744 | tf_op jit(solution)/shard_map/ppermute | solution.py:144
  15.5 8.8 %copy-start = (f32[4,192,192]{2,1,0:T(8,128)S(1)}, f32[4,192,192]{2,1,0:T(8,128)}, u32[]{:S(2)}) copy-start(f32[4,192,192]{2,1,0:T(8,128)} %refs_0_.3) | copy-start | bytes 1769476
  15.6 8.8 %collective-permute-start.5 = (bf16[8,192,128]{2,1,0:T(8,128)(2,1)S(1)}, bf16[8,192,128]{2,1,0:T(8,128)(2,1)S(1)}, u32[]{:S(2)}, u32[]{:S(2)}) collective-permute-start(bf16[8,192,128]{2,1,0:T(8,128)(2,1)S(1)} %pad_maximum_fusion.1), channel_id=1, source_target_pairs={{0,1},{1,0},{2,3},{3,2},{4,5},{5,4},{6,7},{7,6},{8,9},{9,8},{10,11... | collective-permute-start | bytes 1179656 | tf_op jit(solution)/shard_map/ppermute | solution.py:151
  15.7 8.6 %collective-permute-start.3 = (bf16[6,96,128]{2,1,0:T(8,128)(2,1)S(1)}, bf16[6,96,128]{2,1,0:T(8,128)(2,1)S(1)}, u32[]{:S(2)}, u32[]{:S(2)}) collective-permute-start(bf16[6,96,128]{2,1,0:T(8,128)(2,1)S(1)} %add_convert_fusion.1), channel_id=1, source_target_pairs={{0,8},{4,28},{8,16},{12,4},{16,24},{20,12},{24,0},{28,20},{1,9},{5... | collective-permute-start | bytes 442376 | tf_op jit(solution)/shard_map/ppermute | solution.py:144
  17.6 9.6 %collective-permute-start.7 = (bf16[6,96,128]{2,1,0:T(8,128)(2,1)S(1)}, bf16[6,96,128]{2,1,0:T(8,128)(2,1)S(1)}, u32[]{:S(2)}, u32[]{:S(2)}) collective-permute-start(bf16[6,96,128]{2,1,0:T(8,128)(2,1)S(1)} %add_convert_fusion), channel_id=1, source_target_pairs={{0,8},{4,28},{8,16},{12,4},{16,24},{20,12},{24,0},{28,20},{1,9},{5... | collective-permute-start | bytes 442376 | tf_op jit(solution)/shard_map/ppermute | solution.py:144
  27.7 2.9 %collective-permute-start.8 = (bf16[192,128]{1,0:T(8,128)(2,1)S(1)}, bf16[192,128]{1,0:T(8,128)(2,1)S(1)}, u32[]{:S(2)}, u32[]{:S(2)}) collective-permute-start(bf16[192,128]{1,0:T(8,128)(2,1)S(1)} %get-tuple-element.39), channel_id=1, source_target_pairs={{0,1},{1,0},{2,3},{3,2},{4,5},{5,4},{6,7},{7,6},{8,9},{9,8},{10,11... | collective-permute-start | bytes 147464 | tf_op jit(solution)/shard_map/ppermute | solution.py:207
  27.8 4.2 %collective-permute-start.9 = (bf16[192,128]{1,0:T(8,128)(2,1)S(1)}, bf16[192,128]{1,0:T(8,128)(2,1)S(1)}, u32[]{:S(2)}, u32[]{:S(2)}) collective-permute-start(bf16[192,128]{1,0:T(8,128)(2,1)S(1)} %get-tuple-element.40), channel_id=1, source_target_pairs={{0,2},{1,3},{2,0},{3,1},{4,6},{5,7},{6,4},{7,5},{8,10},{9,11},{10,... | collective-permute-start | bytes 147464 | tf_op jit(solution)/shard_map/ppermute | solution.py:207
  29.3 3.7 %collective-permute-start.10 = (bf16[192,128]{1,0:T(8,128)(2,1)S(1)}, bf16[192,128]{1,0:T(8,128)(2,1)S(1)}, u32[]{:S(2)}, u32[]{:S(2)}) collective-permute-start(bf16[192,128]{1,0:T(8,128)(2,1)S(1)} %get-tuple-element.41), channel_id=1, source_target_pairs={{0,3},{1,2},{2,1},{3,0},{4,7},{5,6},{6,5},{7,4},{8,11},{9,10},{10,... | collective-permute-start | bytes 147464 | tf_op jit(solution)/shard_map/ppermute | solution.py:207

commit v5 on v4

--- a/solution.py
+++ b/solution.py
@@ -105,9 +105,8 @@
     def received(row):
         return near_ref[row, span].astype(jnp.float32) + direct_ref[row, span].astype(jnp.float32) + comb_ref[row].astype(jnp.float32)
 
-    panels = [(kept_w, 0), (peer_w, 0)]
-    for shift in range(1, outer_count):
-        panels += [(outer_w[shift - 1], 0), (peer_w, shift * slots)]
+    panels = [((kept_w, 0), (peer_w, 0))]
+    panels += [((outer_w[shift - 1], 0), (peer_w, shift * slots)) for shift in range(1, outer_count)]
     total = [None] * len(panels)
     for two in range(slots // 2):
         tails = received(slots + two)
@@ -117,12 +116,13 @@
             updated = blocks_ref[slot, span] - own_ref[slot, span] - gone
             updated_ref[slot] = updated
             rounded = updated.astype(jnp.bfloat16)
-            for at, (panel, base) in enumerate(panels):
-                part = jnp.dot(rounded, panel[base + slot], preferred_element_type=jnp.float32)
+            for at, pair in enumerate(panels):
+                panel = jnp.concatenate([ref[base + slot] for ref, base in pair], axis=1)
+                part = jnp.dot(rounded, panel, preferred_element_type=jnp.float32)
                 total[at] = part if total[at] is None else total[at] + part
-    kept_ref[span] = total[0]
-    for at, ref in enumerate(part_refs, 1):
-        ref[span] = total[at].astype(ref.dtype)
+    columns = kept_ref.shape[-1]
+    for at, ref in enumerate((kept_ref, *part_refs)):
+        ref[span] = total[at // 2][:, at % 2 * columns : (at % 2 + 1) * columns].astype(ref.dtype)
 
 
 def body(left_panel, right_panel, inverse, target, blocks, weights):

time: 33.8 us -> 33.7 us (level)
  no operation moved by 1% of the time
where the time goes in v5:
time: 33.7 us; the launch traced here: 33.6 us
  starting transfers between devices  14.2 us (42%)
  waiting for transfers between devices  13.6 us (40%)
  Pallas kernels  3.35 us (10%)
  other arithmetic  1.72 us (5%)
  between operations  0.73 us (2%)
    ppermute x6, starting transfers between devices, to_tile(): return lax.ppermute(piece, 'surf', moves)  9.14 us
    ppermute x6, waiting for transfers between devices, to_tile(): return lax.ppermute(piece, 'surf', moves)  7.65 us
    ppermute x1, waiting for transfers between devices, to_outer(): return lax.ppermute(piece, 'pair', moves)  3.48 us
    ppermute x1, starting transfers between devices, to_outer(): return lax.ppermute(piece, 'pair', moves)  3.03 us
    pallas_call x1, Pallas kernels, body(): pl.pallas_call(functools.partial(terms_kernel, surf_count, pair_count), o...  2.67 us
    ppermute x3, waiting for transfers between devices, body(): kept = kept + lax.ppermute(piece, 'pair', moves).astype(jnp.float32)  2.48 us
    ppermute x3, starting transfers between devices, body(): kept = kept + lax.ppermute(piece, 'pair', moves).astype(jnp.float32)  1.92 us
    concatenate x1, other arithmetic, body(): return (jnp.concatenate(updated, axis=1), kept)  0.93 us
  transfers between devices with their start and end apart: 11, of which 5 were waited for; matrix products, arithmetic and copies ran while one was open for 3% of the time, Pallas kernels for 1%

profile of v5, /device:TPU:0, one launch (start us, length us, event | category | flops | bytes accessed | tf_op | source)
XLA Modules:
  0.0 33.6 jit_solution(4711394480024491134)
XLA Ops:
  0.6 2.7 %terms.1 = (bf16[6,192,128]{2,1,0:T(8,128)(2,1)S(1)}, bf16[6,192,128]{2,1,0:T(8,128)(2,1)S(1)}, f32[4,192,192]{2,1,0:T(8,128)S(1)}, bf16[6,96,128]{2,1,0:T(8,128...) custom-call(bf16[2,4,192,128]{3,2,1,0:T(8,128)(2,1)} %bitcast.2, ...), custom_call_target="tpu_custom_call" | custom-call | tf_op jit(solution)/shard_map/terms/pallas_call | solution.py:159
  3.3 3.0 %collective-permute-start.4 = (bf16[8,192,128]{2,1,0:T(8,128)(2,1)S(1)}, bf16[8,192,128]{2,1,0:T(8,128)(2,1)S(1)}, u32[]{:S(2)}, u32[]{:S(2)}) collective-permute-start(bf16[8,192,128]{2,1,0:T(8,128)(2,1)S(1)} %get-tuple-element.29), channel_id=1, source_target_pairs={{0,2},{1,3},{2,0},{3,1},{4,6},{5,7},{6,4},{7,5},{8,10},{9,11},{10,... | collective-permute-start | bytes 1179656 | tf_op jit(solution)/shard_map/ppermute | solution.py:148
  6.3 1.5 %collective-permute-start.2 = (bf16[6,96,128]{2,1,0:T(8,128)(2,1)S(1)}, bf16[6,96,128]{2,1,0:T(8,128)(2,1)S(1)}, u32[]{:S(2)}, u32[]{:S(2)}) collective-permute-start(bf16[6,96,128]{2,1,0:T(8,128)(2,1)S(1)} %get-tuple-element.26), channel_id=1, source_target_pairs={{0,4},{4,0},{8,12},{12,8},{16,20},{20,16},{24,28},{28,24},{1,5},{5... | collective-permute-start | bytes 442376 | tf_op jit(solution)/shard_map/ppermute | solution.py:144
  7.9 0.5 %collective-permute-start.6 = (bf16[6,96,128]{2,1,0:T(8,128)(2,1)S(1)}, bf16[6,96,128]{2,1,0:T(8,128)(2,1)S(1)}, u32[]{:S(2)}, u32[]{:S(2)}) collective-permute-start(bf16[6,96,128]{2,1,0:T(8,128)(2,1)S(1)} %get-tuple-element.32), channel_id=1, source_target_pairs={{0,4},{4,0},{8,12},{12,8},{16,20},{20,16},{24,28},{28,24},{1,5},{5... | collective-permute-start | bytes 442376 | tf_op jit(solution)/shard_map/ppermute | solution.py:144
  8.4 3.6 %collective-permute-start = (bf16[6,192,128]{2,1,0:T(8,128)(2,1)S(1)}, bf16[6,192,128]{2,1,0:T(8,128)(2,1)S(1)}, u32[]{:S(2)}, u32[]{:S(2)}) collective-permute-start(bf16[6,192,128]{2,1,0:T(8,128)(2,1)S(1)} %get-tuple-element.23), channel_id=1, source_target_pairs={{0,24},{4,12},{8,0},{12,20},{16,8},{20,28},{24,16},{28,4},{1,25},{... | collective-permute-start | bytes 884744 | tf_op jit(solution)/shard_map/ppermute | solution.py:144
  12.0 0.0 collective-permute-start.1
  12.0 3.5 %collective-permute-done.4 = bf16[8,192,128]{2,1,0:T(8,128)(2,1)S(1)} collective-permute-done((bf16[8,192,128]{2,1,0:T(8,128)(2,1)S(1)}, bf16[8,192,128]{2,1,0:T(8,128)(2,1)S(1)}, u32[]{:S(2)}, u32[]{:S(2)}) %collective-permute-start.4) | collective-permute-done | bytes 393248 | tf_op jit(solution)/shard_map/ppermute | solution.py:148
  15.5 0.0 copy-start
  15.6 0.1 collective-permute-start.5
  15.6 0.0 collective-permute-done.2
  15.7 1.9 %collective-permute-start.3 = (bf16[6,96,128]{2,1,0:T(8,128)(2,1)S(1)}, bf16[6,96,128]{2,1,0:T(8,128)(2,1)S(1)}, u32[]{:S(2)}, u32[]{:S(2)}) collective-permute-start(bf16[6,96,128]{2,1,0:T(8,128)(2,1)S(1)} %add_convert_fusion.1), channel_id=1, source_target_pairs={{0,8},{4,28},{8,16},{12,4},{16,24},{20,12},{24,0},{28,20},{1,9},{5... | collective-permute-start | bytes 442376 | tf_op jit(solution)/shard_map/ppermute | solution.py:144
  17.6 0.0 collective-permute-done.6
  17.6 1.6 %collective-permute-start.7 = (bf16[6,96,128]{2,1,0:T(8,128)(2,1)S(1)}, bf16[6,96,128]{2,1,0:T(8,128)(2,1)S(1)}, u32[]{:S(2)}, u32[]{:S(2)}) collective-permute-start(bf16[6,96,128]{2,1,0:T(8,128)(2,1)S(1)} %add_convert_fusion), channel_id=1, source_target_pairs={{0,8},{4,28},{8,16},{12,4},{16,24},{20,12},{24,0},{28,20},{1,9},{5... | collective-permute-start | bytes 442376 | tf_op jit(solution)/shard_map/ppermute | solution.py:144
  19.2 5.1 %collective-permute-done.3.refs_4_ = bf16[6,96,128]{2,1,0:T(8,128)(2,1)S(1)} collective-permute-done((bf16[6,96,128]{2,1,0:T(8,128)(2,1)S(1)}, bf16[6,96,128]{2,1,0:T(8,128)(2,1)S(1)}, u32[]{:S(2)}, u32[]{:S(2)}) %collective-permute-start.3) | collective-permute-done | bytes 147488 | tf_op jit(solution)/shard_map/ppermute | solution.py:144
  24.3 0.0 collective-permute-done.refs_2_
  24.3 0.0 collective-permute-done.1.refs_3_
  24.3 0.0 collective-permute-done.5.refs_6_
  24.3 0.0 copy-done
  24.3 0.3 %update.2 = (f32[4,96,192]{2,1,0:T(8,128)S(1)}, f32[192,128]{1,0:T(8,128)S(1)}, bf16[192,128]{1,0:T(8,128)(2,1)S(1)}, bf16[192,128]{1,0:T(8,128)(2,1)S(1)}, bf16[192,128]{1,0:T(8,128)(2,1)S(1)}) custom-call(f32[4,192,192]{2,1,0:T(8,128)S(1)} %copy-done, f32[4,192,192]{2,1,0:T(8,128)S(1)} %get-tuple-element.22.refs_1_, ...), custom_call_target="tpu_custom_call" | custom-call | tf_op jit(solution)/shard_map/update/pallas_call | solution.py:192
  24.7 2.6 %collective-permute-done.7.refs_4_ = bf16[6,96,128]{2,1,0:T(8,128)(2,1)S(1)} collective-permute-done((bf16[6,96,128]{2,1,0:T(8,128)(2,1)S(1)}, bf16[6,96,128]{2,1,0:T(8,128)(2,1)S(1)}, u32[]{:S(2)}, u32[]{:S(2)}) %collective-permute-start.7) | collective-permute-done | bytes 147488 | tf_op jit(solution)/shard_map/ppermute | solution.py:144
  27.3 0.3 update.3
  27.6 0.1 collective-permute-start.8
  27.7 1.6 %collective-permute-start.9 = (bf16[192,128]{1,0:T(8,128)(2,1)S(1)}, bf16[192,128]{1,0:T(8,128)(2,1)S(1)}, u32[]{:S(2)}, u32[]{:S(2)}) collective-permute-start(bf16[192,128]{1,0:T(8,128)(2,1)S(1)} %get-tuple-element.40), channel_id=1, source_target_pairs={{0,2},{1,3},{2,0},{3,1},{4,6},{5,7},{6,4},{7,5},{8,10},{9,11},{10,... | collective-permute-start | bytes 147464 | tf_op jit(solution)/shard_map/ppermute | solution.py:207
  29.2 0.3 collective-permute-start.10
  29.5 0.9 %pad_maximum_fusion = f32[4,192,192]{2,1,0:T(8,128)} fusion(f32[4,96,192]{2,1,0:T(8,128)S(1)} %get-tuple-element.37, f32[4,96,192]{2,1,0:T(8,128)S(1)} %get-tuple-element.30), kind=kLoop, calls=%fused_computation | loop fusion | flops 147456 | bytes 1179648 | tf_op jit(solution)/shard_map/concatenate | solution.py:208
  30.5 0.0 collective-permute-done.8
  30.5 1.4 %collective-permute-done.9 = bf16[192,128]{1,0:T(8,128)(2,1)S(1)} collective-permute-done((bf16[192,128]{1,0:T(8,128)(2,1)S(1)}, bf16[192,128]{1,0:T(8,128)(2,1)S(1)}, u32[]{:S(2)}, u32[]{:S(2)}) %collective-permute-start.9) | collective-permute-done | bytes 49184 | tf_op jit(solution)/shard_map/ppermute | solution.py:207
  31.8 1.1 %collective-permute-done.10 = bf16[192,128]{1,0:T(8,128)(2,1)S(1)} collective-permute-done((bf16[192,128]{1,0:T(8,128)(2,1)S(1)}, bf16[192,128]{1,0:T(8,128)(2,1)S(1)}, u32[]{:S(2)}, u32[]{:S(2)}) %collective-permute-start.10) | collective-permute-done | bytes 49184 | tf_op jit(solution)/shard_map/ppermute | solution.py:207
  32.9 0.7 %convert_add_fusion = f32[192,128]{1,0:T(8,128)} fusion(bf16[192,128]{1,0:T(8,128)(2,1)S(1)} %collective-permute-done.10, bf16[192,128]{1,0:T(8,128)(2,1)S(1)} %collective-permute-done.9, f32[192,128]{1,0:T(8,128)S(1)} %get-tuple-element.38, bf16[192,128]{1,0:T(8,128)(2,1)S(1)} %collective-permute-done.8), kind=kLoop, calls=%fused_computation.4 | loop fusion | flops 147456 | bytes 344064 | tf_op jit(solution)/shard_map/add | solution.py:207
  (4 shorter events, 0.1 us)
Async XLA Ops:
  3.3 12.1 %collective-permute-start.4 = (bf16[8,192,128]{2,1,0:T(8,128)(2,1)S(1)}, bf16[8,192,128]{2,1,0:T(8,128)(2,1)S(1)}, u32[]{:S(2)}, u32[]{:S(2)}) collective-permute-start(bf16[8,192,128]{2,1,0:T(8,128)(2,1)S(1)} %get-tuple-element.29), channel_id=1, source_target_pairs={{0,2},{1,3},{2,0},{3,1},{4,6},{5,7},{6,4},{7,5},{8,10},{9,11},{10,... | collective-permute-start | bytes 1179656 | tf_op jit(solution)/shard_map/ppermute | solution.py:148
  6.3 9.3 %collective-permute-start.2 = (bf16[6,96,128]{2,1,0:T(8,128)(2,1)S(1)}, bf16[6,96,128]{2,1,0:T(8,128)(2,1)S(1)}, u32[]{:S(2)}, u32[]{:S(2)}) collective-permute-start(bf16[6,96,128]{2,1,0:T(8,128)(2,1)S(1)} %get-tuple-element.26), channel_id=1, source_target_pairs={{0,4},{4,0},{8,12},{12,8},{16,20},{20,16},{24,28},{28,24},{1,5},{5... | collective-permute-start | bytes 442376 | tf_op jit(solution)/shard_map/ppermute | solution.py:144
  7.9 9.7 %collective-permute-start.6 = (bf16[6,96,128]{2,1,0:T(8,128)(2,1)S(1)}, bf16[6,96,128]{2,1,0:T(8,128)(2,1)S(1)}, u32[]{:S(2)}, u32[]{:S(2)}) collective-permute-start(bf16[6,96,128]{2,1,0:T(8,128)(2,1)S(1)} %get-tuple-element.32), channel_id=1, source_target_pairs={{0,4},{4,0},{8,12},{12,8},{16,20},{20,16},{24,28},{28,24},{1,5},{5... | collective-permute-start | bytes 442376 | tf_op jit(solution)/shard_map/ppermute | solution.py:144
  8.4 15.9 %collective-permute-start = (bf16[6,192,128]{2,1,0:T(8,128)(2,1)S(1)}, bf16[6,192,128]{2,1,0:T(8,128)(2,1)S(1)}, u32[]{:S(2)}, u32[]{:S(2)}) collective-permute-start(bf16[6,192,128]{2,1,0:T(8,128)(2,1)S(1)} %get-tuple-element.23), channel_id=1, source_target_pairs={{0,24},{4,12},{8,0},{12,20},{16,8},{20,28},{24,16},{28,4},{1,25},{... | collective-permute-start | bytes 884744 | tf_op jit(solution)/shard_map/ppermute | solution.py:144
  12.0 12.3 %collective-permute-start.1 = (bf16[6,192,128]{2,1,0:T(8,128)(2,1)S(1)}, bf16[6,192,128]{2,1,0:T(8,128)(2,1)S(1)}, u32[]{:S(2)}, u32[]{:S(2)}) collective-permute-start(bf16[6,192,128]{2,1,0:T(8,128)(2,1)S(1)} %get-tuple-element.24), channel_id=1, source_target_pairs={{0,4},{4,0},{8,12},{12,8},{16,20},{20,16},{24,28},{28,24},{1,5},{5... | collective-permute-start | bytes 884744 | tf_op jit(solution)/shard_map/ppermute | solution.py:144
  15.5 8.8 %copy-start = (f32[4,192,192]{2,1,0:T(8,128)S(1)}, f32[4,192,192]{2,1,0:T(8,128)}, u32[]{:S(2)}) copy-start(f32[4,192,192]{2,1,0:T(8,128)} %refs_0_.3) | copy-start | bytes 1769476
  15.6 8.8 %collective-permute-start.5 = (bf16[8,192,128]{2,1,0:T(8,128)(2,1)S(1)}, bf16[8,192,128]{2,1,0:T(8,128)(2,1)S(1)}, u32[]{:S(2)}, u32[]{:S(2)}) collective-permute-start(bf16[8,192,128]{2,1,0:T(8,128)(2,1)S(1)} %pad_maximum_fusion.1), channel_id=1, source_target_pairs={{0,1},{1,0},{2,3},{3,2},{4,5},{5,4},{6,7},{7,6},{8,9},{9,8},{10,11... | collective-permute-start | bytes 1179656 | tf_op jit(solution)/shard_map/ppermute | solution.py:151
  15.7 8.6 %collective-permute-start.3 = (bf16[6,96,128]{2,1,0:T(8,128)(2,1)S(1)}, bf16[6,96,128]{2,1,0:T(8,128)(2,1)S(1)}, u32[]{:S(2)}, u32[]{:S(2)}) collective-permute-start(bf16[6,96,128]{2,1,0:T(8,128)(2,1)S(1)} %add_convert_fusion.1), channel_id=1, source_target_pairs={{0,8},{4,28},{8,16},{12,4},{16,24},{20,12},{24,0},{28,20},{1,9},{5... | collective-permute-start | bytes 442376 | tf_op jit(solution)/shard_map/ppermute | solution.py:144
  17.6 9.6 %collective-permute-start.7 = (bf16[6,96,128]{2,1,0:T(8,128)(2,1)S(1)}, bf16[6,96,128]{2,1,0:T(8,128)(2,1)S(1)}, u32[]{:S(2)}, u32[]{:S(2)}) collective-permute-start(bf16[6,96,128]{2,1,0:T(8,128)(2,1)S(1)} %add_convert_fusion), channel_id=1, source_target_pairs={{0,8},{4,28},{8,16},{12,4},{16,24},{20,12},{24,0},{28,20},{1,9},{5... | collective-permute-start | bytes 442376 | tf_op jit(solution)/shard_map/ppermute | solution.py:144
  27.6 2.9 %collective-permute-start.8 = (bf16[192,128]{1,0:T(8,128)(2,1)S(1)}, bf16[192,128]{1,0:T(8,128)(2,1)S(1)}, u32[]{:S(2)}, u32[]{:S(2)}) collective-permute-start(bf16[192,128]{1,0:T(8,128)(2,1)S(1)} %get-tuple-element.39), channel_id=1, source_target_pairs={{0,1},{1,0},{2,3},{3,2},{4,5},{5,4},{6,7},{7,6},{8,9},{9,8},{10,11... | collective-permute-start | bytes 147464 | tf_op jit(solution)/shard_map/ppermute | solution.py:207
  27.7 4.2 %collective-permute-start.9 = (bf16[192,128]{1,0:T(8,128)(2,1)S(1)}, bf16[192,128]{1,0:T(8,128)(2,1)S(1)}, u32[]{:S(2)}, u32[]{:S(2)}) collective-permute-start(bf16[192,128]{1,0:T(8,128)(2,1)S(1)} %get-tuple-element.40), channel_id=1, source_target_pairs={{0,2},{1,3},{2,0},{3,1},{4,6},{5,7},{6,4},{7,5},{8,10},{9,11},{10,... | collective-permute-start | bytes 147464 | tf_op jit(solution)/shard_map/ppermute | solution.py:207
  29.2 3.7 %collective-permute-start.10 = (bf16[192,128]{1,0:T(8,128)(2,1)S(1)}, bf16[192,128]{1,0:T(8,128)(2,1)S(1)}, u32[]{:S(2)}, u32[]{:S(2)}) collective-permute-start(bf16[192,128]{1,0:T(8,128)(2,1)S(1)} %get-tuple-element.41), channel_id=1, source_target_pairs={{0,3},{1,2},{2,1},{3,0},{4,7},{5,6},{6,5},{7,4},{8,11},{9,10},{10,... | collective-permute-start | bytes 147464 | tf_op jit(solution)/shard_map/ppermute | solution.py:207

commit v6 on v5

--- a/solution.py
+++ b/solution.py
@@ -23,15 +23,27 @@
     return lax.dot_general(a, b, (((1,), (1,)), ((), ())), preferred_element_type=jnp.float32)
 
 
+def pack(acc, role, refs):
+    skeleton = acc.shape[1]
+    slots = acc.shape[0] // ROLES
+    spans = chunk_rows(skeleton) if len(refs) == CHUNKS else [(0, skeleton)]
+    for (start, stop), ref in zip(spans, refs):
+        for slot in range(slots):
+            ref[slot] = acc[role * slots + slot, start:stop, :LANES].astype(jnp.bfloat16)
+        lane = lax.broadcasted_iota(jnp.int32, (stop - start, LANES), 1)
+        for two in range(slots // 2):
+            low = acc[role * slots + 2 * two, start:stop, LANES:]
+            high = acc[role * slots + 2 * two + 1, start:stop, LANES:]
+            ref[slots + two] = jnp.where(lane < skeleton - LANES, low, high).astype(jnp.bfloat16)
+
+
 def terms_kernel(surf_count, pair_count, lt_hbm, rt_hbm, inv_hbm, weights_hbm, target_hbm, *refs):
-    out_refs, weight_refs, refs = refs[: ROLES + 2 * (CHUNKS - 1)], refs[ROLES + 2 * (CHUNKS - 1) : -8], refs[-8:]
-    lt_ref, rt_ref, inv_ref, target_ref, acc, sem, weights_sem, target_sem = refs
-    direct_ref, near_ref, own_ref = out_refs[:3]
-    far_refs, comb_refs = out_refs[3 : 3 + CHUNKS], out_refs[3 + CHUNKS :]
-    box_count, neighbours, skeleton, _ = lt_ref.shape
-    slots = own_ref.shape[0]
+    acc, direct_ref, *refs = refs
+    far_refs, weight_refs, refs = refs[:CHUNKS], refs[CHUNKS:-7], refs[-7:]
+    lt_ref, rt_ref, inv_ref, target_ref, sem, weights_sem, target_sem = refs
+    box_count, neighbours, skeleton = lt_ref.shape[:3]
+    slots = acc.shape[0] // ROLES
     outer_count = pair_count // 2
-    tail = skeleton - LANES
     read_target = pltpu.make_async_copy(target_hbm, target_ref, target_sem)
     read_target.start()
     copies = [
@@ -72,26 +84,24 @@
         for second in range(neighbours):
             both = jnp.concatenate([solved[second], left[second]], axis=1)
             both = jnp.concatenate([both, both[LANES:]], axis=0)
+            rows = [
+                jnp.concatenate([left[first], solved[first] if first != second else jnp.zeros_like(solved[first])], axis=1)
+                for first in range(second + 1)
+            ]
+            product = dot_nt(jnp.concatenate(rows, axis=0), both)
             for first in range(second + 1):
-                if first == second:
-                    term = dot_nt(left[first], both[:, :LANES])
-                else:
-                    term = dot_nt(jnp.concatenate([left[first], solved[first]], axis=1), both)
-                acc[cell(box, first, second)] += term
-    lane = lax.broadcasted_iota(jnp.int32, (skeleton, LANES), 1)
-    for role, refs in ((FAR, far_refs), (DIRECT, [direct_ref]), (COMB, comb_refs), (NEAR, [near_ref])):
-        spans = chunk_rows(skeleton) if len(refs) == CHUNKS else [(0, skeleton)]
-        for (start, stop), ref in zip(spans, refs):
-            span, rows = slice(start, stop), stop - start
-            for slot in range(slots):
-                ref[slot] = acc[role * slots + slot, span, :LANES].astype(jnp.bfloat16)
-            for two in range(slots // 2):
-                low = acc[role * slots + 2 * two, span, LANES:]
-                high = acc[role * slots + 2 * two + 1, span, LANES:]
-                ref[slots + two] = jnp.where(lane[:rows] < tail, low, high).astype(jnp.bfloat16)
-    own_ref[...] = acc[OWN * slots : (OWN + 1) * slots, :, :skeleton]
+                acc[cell(box, first, second)] += product[first * skeleton : (first + 1) * skeleton]
+    pack(acc, FAR, far_refs)
+    pack(acc, DIRECT, [direct_ref])
     for copy in cuts:
         copy.wait()
+
+
+def pack_kernel(acc, near_ref, own_ref, *comb_refs):
+    slots, skeleton, _ = own_ref.shape
+    pack(acc, NEAR, [near_ref])
+    pack(acc, COMB, comb_refs)
+    own_ref[...] = acc[OWN * slots : (OWN + 1) * slots, :, :skeleton]
 
 
 def update_kernel(chunk, outer_count, *refs):
@@ -154,9 +164,10 @@
     full = shape(slots + slots // 2, skeleton, LANES)
     parts = [shape(slots + slots // 2, count, LANES) for count in rows]
     cuts = [shape(slots, skeleton, columns)] + [shape(2 * slots, skeleton, columns)] * (outer_count - 1) + [shape(slots, skeleton, columns)]
-    out_shape = [full, full, shape(*blocks.shape, dtype=jnp.float32)] + 2 * parts + cuts
+    totals = shape(ROLES * slots, skeleton, 2 * LANES, dtype=jnp.float32)
+    out_shape = [totals, full, *parts, *cuts]
     args = (jnp.swapaxes(left_panel, 2, 3), jnp.swapaxes(right_panel, 2, 3), inverse, weights, target)
-    direct, near, own, *out = pl.pallas_call(
+    totals, direct, *out = pl.pallas_call(
         functools.partial(terms_kernel, surf_count, pair_count),
         out_shape=out_shape,
         in_specs=[hbm] * len(args),
@@ -166,7 +177,6 @@
             pltpu.VMEM(panels_shape, jnp.bfloat16),
             pltpu.VMEM((box_count, redundant, redundant), jnp.bfloat16),
             pltpu.SMEM(target.shape, target.dtype),
-            pltpu.VMEM((ROLES * slots, skeleton, 2 * LANES), jnp.float32),
             pltpu.SemaphoreType.DMA((3,)),
             pltpu.SemaphoreType.DMA((pair_count,)),
             pltpu.SemaphoreType.DMA,
@@ -174,7 +184,15 @@
         compiler_params=pltpu.CompilerParams(vmem_limit_bytes=20 << 20),
         name="terms",
     )(*(pltpu.with_memory_space_constraint(array, pltpu.HBM) for array in args))
-    far, comb, (kept_w, *outer_w, peer_w) = out[:CHUNKS], out[CHUNKS : 2 * CHUNKS], out[2 * CHUNKS :]
+    far, (kept_w, *outer_w, peer_w) = out[:CHUNKS], out[CHUNKS:]
+    near, own, *comb = pl.pallas_call(
+        pack_kernel,
+        out_shape=[full, shape(*blocks.shape, dtype=jnp.float32), *parts],
+        in_specs=[vmem],
+        out_specs=[vmem] * (2 + CHUNKS),
+        compiler_params=pltpu.CompilerParams(vmem_limit_bytes=4 << 20),
+        name="pack",
+    )(totals)
 
     far = [to_tile(piece, 1, -1) for piece in far]
     direct = to_tile(direct, -2, 2)

time: 33.7 us -> 33.7 us (level)
  waiting for transfers between devices: 13.6 us -> 11.9 us
  starting transfers between devices: 14.2 us -> 15.7 us
    ppermute x1, waiting for transfers between devices: 3.48 us -> 1.76 us  [to_outer(): return lax.ppermute(piece, 'pair', moves)]
    ppermute x6, starting transfers between devices: 9.14 us -> 10.7 us  [to_tile(): return lax.ppermute(piece, 'surf', moves)]
where the time goes in v6:
time: 33.7 us; the launch traced here: 33.6 us
  starting transfers between devices  15.7 us (47%)
  waiting for transfers between devices  11.9 us (35%)
  Pallas kernels  3.43 us (10%)
  other arithmetic  1.72 us (5%)
  between operations  0.73 us (2%)
    ppermute x6, starting transfers between devices, to_tile(): return lax.ppermute(piece, 'surf', moves)  10.7 us
    ppermute x6, waiting for transfers between devices, to_tile(): return lax.ppermute(piece, 'surf', moves)  7.66 us
    ppermute x1, starting transfers between devices, to_outer(): return lax.ppermute(piece, 'pair', moves)  3.03 us
    pallas_call x1, Pallas kernels, body(): pl.pallas_call(functools.partial(terms_kernel, surf_count, pair_count), o...  2.63 us
    ppermute x3, waiting for transfers between devices, body(): kept = kept + lax.ppermute(piece, 'pair', moves).astype(jnp.float32)  2.48 us
    ppermute x3, starting transfers between devices, body(): kept = kept + lax.ppermute(piece, 'pair', moves).astype(jnp.float32)  1.92 us
    ppermute x1, waiting for transfers between devices, to_outer(): return lax.ppermute(piece, 'pair', moves)  1.76 us
    concatenate x1, other arithmetic, body(): return (jnp.concatenate(updated, axis=1), kept)  0.93 us
  transfers between devices with their start and end apart: 11, of which 5 were waited for; matrix products, arithmetic and copies ran while one was open for 3% of the time, Pallas kernels for 1%

profile of v6, /device:TPU:0, one launch (start us, length us, event | category | flops | bytes accessed | tf_op | source)
XLA Modules:
  0.0 33.6 jit_solution(1670979496747634949)
XLA Ops:
  0.6 0.0 copy-start
  0.6 2.6 %terms.1 = (f32[20,192,256]{2,1,0:T(8,128)S(1)}, bf16[6,192,128]{2,1,0:T(8,128)(2,1)S(1)}, bf16[6,96,128]{2,1,0:T(8,128)(2,1)S(1)}, bf16[6,96,128]{2,1,0:T(8,128...) custom-call(bf16[2,4,192,128]{3,2,1,0:T(8,128)(2,1)} %bitcast.2, ...), custom_call_target="tpu_custom_call" | custom-call | tf_op jit(solution)/shard_map/terms/pallas_call | solution.py:170
  3.3 3.0 %collective-permute-start.4 = (bf16[8,192,128]{2,1,0:T(8,128)(2,1)S(1)}, bf16[8,192,128]{2,1,0:T(8,128)(2,1)S(1)}, u32[]{:S(2)}, u32[]{:S(2)}) collective-permute-start(bf16[8,192,128]{2,1,0:T(8,128)(2,1)S(1)} %get-tuple-element.31), channel_id=1, source_target_pairs={{0,2},{1,3},{2,0},{3,1},{4,6},{5,7},{6,4},{7,5},{8,10},{9,11},{10,... | collective-permute-start | bytes 1179656 | tf_op jit(solution)/shard_map/ppermute | solution.py:158
  6.3 1.5 %collective-permute-start.2 = (bf16[6,96,128]{2,1,0:T(8,128)(2,1)S(1)}, bf16[6,96,128]{2,1,0:T(8,128)(2,1)S(1)}, u32[]{:S(2)}, u32[]{:S(2)}) collective-permute-start(bf16[6,96,128]{2,1,0:T(8,128)(2,1)S(1)} %get-tuple-element.28), channel_id=1, source_target_pairs={{0,4},{4,0},{8,12},{12,8},{16,20},{20,16},{24,28},{28,24},{1,5},{5... | collective-permute-start | bytes 442376 | tf_op jit(solution)/shard_map/ppermute | solution.py:154
  7.8 0.5 %collective-permute-start.6 = (bf16[6,96,128]{2,1,0:T(8,128)(2,1)S(1)}, bf16[6,96,128]{2,1,0:T(8,128)(2,1)S(1)}, u32[]{:S(2)}, u32[]{:S(2)}) collective-permute-start(bf16[6,96,128]{2,1,0:T(8,128)(2,1)S(1)} %get-tuple-element.34), channel_id=1, source_target_pairs={{0,4},{4,0},{8,12},{12,8},{16,20},{20,16},{24,28},{28,24},{1,5},{5... | collective-permute-start | bytes 442376 | tf_op jit(solution)/shard_map/ppermute | solution.py:154
  8.3 0.1 pack.1
  8.5 1.6 %collective-permute-start.1 = (bf16[6,192,128]{2,1,0:T(8,128)(2,1)S(1)}, bf16[6,192,128]{2,1,0:T(8,128)(2,1)S(1)}, u32[]{:S(2)}, u32[]{:S(2)}) collective-permute-start(bf16[6,192,128]{2,1,0:T(8,128)(2,1)S(1)} %get-tuple-element.26), channel_id=1, source_target_pairs={{0,4},{4,0},{8,12},{12,8},{16,20},{20,16},{24,28},{28,24},{1,5},{5... | collective-permute-start | bytes 884744 | tf_op jit(solution)/shard_map/ppermute | solution.py:154
  10.1 3.6 %collective-permute-start = (bf16[6,192,128]{2,1,0:T(8,128)(2,1)S(1)}, bf16[6,192,128]{2,1,0:T(8,128)(2,1)S(1)}, u32[]{:S(2)}, u32[]{:S(2)}) collective-permute-start(bf16[6,192,128]{2,1,0:T(8,128)(2,1)S(1)} %get-tuple-element.25), channel_id=1, source_target_pairs={{0,24},{4,12},{8,0},{12,20},{16,8},{20,28},{24,16},{28,4},{1,25},{... | collective-permute-start | bytes 884744 | tf_op jit(solution)/shard_map/ppermute | solution.py:154
  13.7 1.8 %collective-permute-done.4 = bf16[8,192,128]{2,1,0:T(8,128)(2,1)S(1)} collective-permute-done((bf16[8,192,128]{2,1,0:T(8,128)(2,1)S(1)}, bf16[8,192,128]{2,1,0:T(8,128)(2,1)S(1)}, u32[]{:S(2)}, u32[]{:S(2)}) %collective-permute-start.4) | collective-permute-done | bytes 393248 | tf_op jit(solution)/shard_map/ppermute | solution.py:158
  15.5 0.1 collective-permute-start.5
  15.6 0.0 collective-permute-done.2
  15.6 1.9 %collective-permute-start.3 = (bf16[6,96,128]{2,1,0:T(8,128)(2,1)S(1)}, bf16[6,96,128]{2,1,0:T(8,128)(2,1)S(1)}, u32[]{:S(2)}, u32[]{:S(2)}) collective-permute-start(bf16[6,96,128]{2,1,0:T(8,128)(2,1)S(1)} %add_convert_fusion.1), channel_id=1, source_target_pairs={{0,8},{4,28},{8,16},{12,4},{16,24},{20,12},{24,0},{28,20},{1,9},{5... | collective-permute-start | bytes 442376 | tf_op jit(solution)/shard_map/ppermute | solution.py:154
  17.5 0.0 collective-permute-done.6
  17.6 1.6 %collective-permute-start.7 = (bf16[6,96,128]{2,1,0:T(8,128)(2,1)S(1)}, bf16[6,96,128]{2,1,0:T(8,128)(2,1)S(1)}, u32[]{:S(2)}, u32[]{:S(2)}) collective-permute-start(bf16[6,96,128]{2,1,0:T(8,128)(2,1)S(1)} %add_convert_fusion), channel_id=1, source_target_pairs={{0,8},{4,28},{8,16},{12,4},{16,24},{20,12},{24,0},{28,20},{1,9},{5... | collective-permute-start | bytes 442376 | tf_op jit(solution)/shard_map/ppermute | solution.py:154
  19.2 5.1 %collective-permute-done.3.refs_4_ = bf16[6,96,128]{2,1,0:T(8,128)(2,1)S(1)} collective-permute-done((bf16[6,96,128]{2,1,0:T(8,128)(2,1)S(1)}, bf16[6,96,128]{2,1,0:T(8,128)(2,1)S(1)}, u32[]{:S(2)}, u32[]{:S(2)}) %collective-permute-start.3) | collective-permute-done | bytes 147488 | tf_op jit(solution)/shard_map/ppermute | solution.py:154
  24.3 0.0 collective-permute-done.1.refs_3_
  24.3 0.0 collective-permute-done.refs_2_
  24.3 0.0 collective-permute-done.5.refs_6_
  24.3 0.0 copy-done
  24.3 0.3 update.2
  24.6 2.6 %collective-permute-done.7.refs_4_ = bf16[6,96,128]{2,1,0:T(8,128)(2,1)S(1)} collective-permute-done((bf16[6,96,128]{2,1,0:T(8,128)(2,1)S(1)}, bf16[6,96,128]{2,1,0:T(8,128)(2,1)S(1)}, u32[]{:S(2)}, u32[]{:S(2)}) %collective-permute-start.7) | collective-permute-done | bytes 147488 | tf_op jit(solution)/shard_map/ppermute | solution.py:154
  27.2 0.3 update.3
  27.5 0.1 collective-permute-start.8
  27.6 1.6 %collective-permute-start.9 = (bf16[192,128]{1,0:T(8,128)(2,1)S(1)}, bf16[192,128]{1,0:T(8,128)(2,1)S(1)}, u32[]{:S(2)}, u32[]{:S(2)}) collective-permute-start(bf16[192,128]{1,0:T(8,128)(2,1)S(1)} %get-tuple-element.42), channel_id=1, source_target_pairs={{0,2},{1,3},{2,0},{3,1},{4,6},{5,7},{6,4},{7,5},{8,10},{9,11},{10,... | collective-permute-start | bytes 147464 | tf_op jit(solution)/shard_map/ppermute | solution.py:225
  29.2 0.3 collective-permute-start.10
  29.5 0.9 %pad_maximum_fusion = f32[4,192,192]{2,1,0:T(8,128)} fusion(f32[4,96,192]{2,1,0:T(8,128)S(1)} %get-tuple-element.39, f32[4,96,192]{2,1,0:T(8,128)S(1)} %get-tuple-element.32), kind=kLoop, calls=%fused_computation | loop fusion | flops 147456 | bytes 1179648 | tf_op jit(solution)/shard_map/concatenate | solution.py:226
  30.4 0.0 collective-permute-done.8
  30.4 1.4 %collective-permute-done.9 = bf16[192,128]{1,0:T(8,128)(2,1)S(1)} collective-permute-done((bf16[192,128]{1,0:T(8,128)(2,1)S(1)}, bf16[192,128]{1,0:T(8,128)(2,1)S(1)}, u32[]{:S(2)}, u32[]{:S(2)}) %collective-permute-start.9) | collective-permute-done | bytes 49184 | tf_op jit(solution)/shard_map/ppermute | solution.py:225
  31.8 1.1 %collective-permute-done.10 = bf16[192,128]{1,0:T(8,128)(2,1)S(1)} collective-permute-done((bf16[192,128]{1,0:T(8,128)(2,1)S(1)}, bf16[192,128]{1,0:T(8,128)(2,1)S(1)}, u32[]{:S(2)}, u32[]{:S(2)}) %collective-permute-start.10) | collective-permute-done | bytes 49184 | tf_op jit(solution)/shard_map/ppermute | solution.py:225
  32.9 0.7 %convert_add_fusion = f32[192,128]{1,0:T(8,128)} fusion(bf16[192,128]{1,0:T(8,128)(2,1)S(1)} %collective-permute-done.10, bf16[192,128]{1,0:T(8,128)(2,1)S(1)} %collective-permute-done.9, f32[192,128]{1,0:T(8,128)S(1)} %get-tuple-element.40, bf16[192,128]{1,0:T(8,128)(2,1)S(1)} %collective-permute-done.8), kind=kLoop, calls=%fused_computation.4 | loop fusion | flops 147456 | bytes 344064 | tf_op jit(solution)/shard_map/add | solution.py:225
  (4 shorter events, 0.1 us)
Async XLA Ops:
  0.6 23.6 %copy-start = (f32[4,192,192]{2,1,0:T(8,128)S(1)}, f32[4,192,192]{2,1,0:T(8,128)}, u32[]{:S(2)}) copy-start(f32[4,192,192]{2,1,0:T(8,128)} %refs_0_.3) | copy-start | bytes 1769476
  3.3 12.1 %collective-permute-start.4 = (bf16[8,192,128]{2,1,0:T(8,128)(2,1)S(1)}, bf16[8,192,128]{2,1,0:T(8,128)(2,1)S(1)}, u32[]{:S(2)}, u32[]{:S(2)}) collective-permute-start(bf16[8,192,128]{2,1,0:T(8,128)(2,1)S(1)} %get-tuple-element.31), channel_id=1, source_target_pairs={{0,2},{1,3},{2,0},{3,1},{4,6},{5,7},{6,4},{7,5},{8,10},{9,11},{10,... | collective-permute-start | bytes 1179656 | tf_op jit(solution)/shard_map/ppermute | solution.py:158
  6.3 9.3 %collective-permute-start.2 = (bf16[6,96,128]{2,1,0:T(8,128)(2,1)S(1)}, bf16[6,96,128]{2,1,0:T(8,128)(2,1)S(1)}, u32[]{:S(2)}, u32[]{:S(2)}) collective-permute-start(bf16[6,96,128]{2,1,0:T(8,128)(2,1)S(1)} %get-tuple-element.28), channel_id=1, source_target_pairs={{0,4},{4,0},{8,12},{12,8},{16,20},{20,16},{24,28},{28,24},{1,5},{5... | collective-permute-start | bytes 442376 | tf_op jit(solution)/shard_map/ppermute | solution.py:154
  7.8 9.7 %collective-permute-start.6 = (bf16[6,96,128]{2,1,0:T(8,128)(2,1)S(1)}, bf16[6,96,128]{2,1,0:T(8,128)(2,1)S(1)}, u32[]{:S(2)}, u32[]{:S(2)}) collective-permute-start(bf16[6,96,128]{2,1,0:T(8,128)(2,1)S(1)} %get-tuple-element.34), channel_id=1, source_target_pairs={{0,4},{4,0},{8,12},{12,8},{16,20},{20,16},{24,28},{28,24},{1,5},{5... | collective-permute-start | bytes 442376 | tf_op jit(solution)/shard_map/ppermute | solution.py:154
  8.5 15.8 %collective-permute-start.1 = (bf16[6,192,128]{2,1,0:T(8,128)(2,1)S(1)}, bf16[6,192,128]{2,1,0:T(8,128)(2,1)S(1)}, u32[]{:S(2)}, u32[]{:S(2)}) collective-permute-start(bf16[6,192,128]{2,1,0:T(8,128)(2,1)S(1)} %get-tuple-element.26), channel_id=1, source_target_pairs={{0,4},{4,0},{8,12},{12,8},{16,20},{20,16},{24,28},{28,24},{1,5},{5... | collective-permute-start | bytes 884744 | tf_op jit(solution)/shard_map/ppermute | solution.py:154
  10.1 14.2 %collective-permute-start = (bf16[6,192,128]{2,1,0:T(8,128)(2,1)S(1)}, bf16[6,192,128]{2,1,0:T(8,128)(2,1)S(1)}, u32[]{:S(2)}, u32[]{:S(2)}) collective-permute-start(bf16[6,192,128]{2,1,0:T(8,128)(2,1)S(1)} %get-tuple-element.25), channel_id=1, source_target_pairs={{0,24},{4,12},{8,0},{12,20},{16,8},{20,28},{24,16},{28,4},{1,25},{... | collective-permute-start | bytes 884744 | tf_op jit(solution)/shard_map/ppermute | solution.py:154
  15.5 8.8 %collective-permute-start.5 = (bf16[8,192,128]{2,1,0:T(8,128)(2,1)S(1)}, bf16[8,192,128]{2,1,0:T(8,128)(2,1)S(1)}, u32[]{:S(2)}, u32[]{:S(2)}) collective-permute-start(bf16[8,192,128]{2,1,0:T(8,128)(2,1)S(1)} %pad_maximum_fusion.1), channel_id=1, source_target_pairs={{0,1},{1,0},{2,3},{3,2},{4,5},{5,4},{6,7},{7,6},{8,9},{9,8},{10,11... | collective-permute-start | bytes 1179656 | tf_op jit(solution)/shard_map/ppermute | solution.py:161
  15.6 8.6 %collective-permute-start.3 = (bf16[6,96,128]{2,1,0:T(8,128)(2,1)S(1)}, bf16[6,96,128]{2,1,0:T(8,128)(2,1)S(1)}, u32[]{:S(2)}, u32[]{:S(2)}) collective-permute-start(bf16[6,96,128]{2,1,0:T(8,128)(2,1)S(1)} %add_convert_fusion.1), channel_id=1, source_target_pairs={{0,8},{4,28},{8,16},{12,4},{16,24},{20,12},{24,0},{28,20},{1,9},{5... | collective-permute-start | bytes 442376 | tf_op jit(solution)/shard_map/ppermute | solution.py:154
  17.6 9.6 %collective-permute-start.7 = (bf16[6,96,128]{2,1,0:T(8,128)(2,1)S(1)}, bf16[6,96,128]{2,1,0:T(8,128)(2,1)S(1)}, u32[]{:S(2)}, u32[]{:S(2)}) collective-permute-start(bf16[6,96,128]{2,1,0:T(8,128)(2,1)S(1)} %add_convert_fusion), channel_id=1, source_target_pairs={{0,8},{4,28},{8,16},{12,4},{16,24},{20,12},{24,0},{28,20},{1,9},{5... | collective-permute-start | bytes 442376 | tf_op jit(solution)/shard_map/ppermute | solution.py:154
  27.5 2.9 %collective-permute-start.8 = (bf16[192,128]{1,0:T(8,128)(2,1)S(1)}, bf16[192,128]{1,0:T(8,128)(2,1)S(1)}, u32[]{:S(2)}, u32[]{:S(2)}) collective-permute-start(bf16[192,128]{1,0:T(8,128)(2,1)S(1)} %get-tuple-element.41), channel_id=1, source_target_pairs={{0,1},{1,0},{2,3},{3,2},{4,5},{5,4},{6,7},{7,6},{8,9},{9,8},{10,11... | collective-permute-start | bytes 147464 | tf_op jit(solution)/shard_map/ppermute | solution.py:225
  27.6 4.2 %collective-permute-start.9 = (bf16[192,128]{1,0:T(8,128)(2,1)S(1)}, bf16[192,128]{1,0:T(8,128)(2,1)S(1)}, u32[]{:S(2)}, u32[]{:S(2)}) collective-permute-start(bf16[192,128]{1,0:T(8,128)(2,1)S(1)} %get-tuple-element.42), channel_id=1, source_target_pairs={{0,2},{1,3},{2,0},{3,1},{4,6},{5,7},{6,4},{7,5},{8,10},{9,11},{10,... | collective-permute-start | bytes 147464 | tf_op jit(solution)/shard_map/ppermute | solution.py:225
  29.2 3.7 %collective-permute-start.10 = (bf16[192,128]{1,0:T(8,128)(2,1)S(1)}, bf16[192,128]{1,0:T(8,128)(2,1)S(1)}, u32[]{:S(2)}, u32[]{:S(2)}) collective-permute-start(bf16[192,128]{1,0:T(8,128)(2,1)S(1)} %get-tuple-element.43), channel_id=1, source_target_pairs={{0,3},{1,2},{2,1},{3,0},{4,7},{5,6},{6,5},{7,4},{8,11},{9,10},{10,... | collective-permute-start | bytes 147464 | tf_op jit(solution)/shard_map/ppermute | solution.py:225

commit v7 on v6

--- a/solution.py
+++ b/solution.py
@@ -218,11 +218,19 @@
             name="update",
         )(*inputs, *sums)
         updated.append(fresh)
+        if chunk == 0:
+            early = [to_peer(sums[2 * shift + 1][: rows[0]]) for shift in range(1, outer_count)]
     kept, *parts = sums
     for at, piece in enumerate(parts, 1):
         shift, cross = divmod(at, 2)
         moves = [(i, ((i // 2 - shift) % outer_count) * 2 + (i % 2 ^ cross)) for i in range(pair_count)]
-        kept = kept + lax.ppermute(piece, "pair", moves).astype(jnp.float32)
+        if shift and cross:
+            piece = piece[rows[0] :]
+        elif shift:
+            first = piece[: rows[0]].astype(jnp.float32) + early[shift - 1].astype(jnp.float32)
+            piece = jnp.concatenate([first.astype(piece.dtype), piece[rows[0] :]], axis=0)
+        back = lax.ppermute(piece, "pair", moves).astype(jnp.float32)
+        kept = kept + jnp.pad(back, ((skeleton - back.shape[0], 0), (0, 0)))
     return (jnp.concatenate(updated, axis=1), kept)
 
 

time: 33.7 us -> 34.2 us (1.015)
  starting transfers between devices: 15.7 us -> 16.2 us
    ppermute x3, starting transfers between devices: 1.92 us -> 2.27 us  [body(): back = lax.ppermute(piece, 'pair', moves).astype(jnp.float32)]
  transfers between devices with their start and end apart: 11 -> 12, of which waited for: 5 -> 5; matrix products, arithmetic and copies ran while one was open for 3% -> 3% of each run, Pallas kernels for 1% -> 2%
where the time goes in v7:
time: 34.2 us; the launch traced here: 34.1 us
  starting transfers between devices  16.2 us (47%)
  waiting for transfers between devices  12 us (35%)
  Pallas kernels  3.43 us (10%)
  other arithmetic  1.73 us (5%)
  between operations  0.77 us (2%)
    ppermute x6, starting transfers between devices, to_tile(): return lax.ppermute(piece, 'surf', moves)  10.7 us
    ppermute x6, waiting for transfers between devices, to_tile(): return lax.ppermute(piece, 'surf', moves)  7.57 us
    ppermute x1, starting transfers between devices, to_outer(): return lax.ppermute(piece, 'pair', moves)  3.03 us
    pallas_call x1, Pallas kernels, body(): pl.pallas_call(functools.partial(terms_kernel, surf_count, pair_count), o...  2.63 us
    ppermute x3, waiting for transfers between devices, body(): back = lax.ppermute(piece, 'pair', moves).astype(jnp.float32)  2.62 us
    ppermute x3, starting transfers between devices, body(): back = lax.ppermute(piece, 'pair', moves).astype(jnp.float32)  2.27 us
    ppermute x1, waiting for transfers between devices, to_outer(): return lax.ppermute(piece, 'pair', moves)  1.76 us
    concatenate x1, other arithmetic, body(): return (jnp.concatenate(updated, axis=1), kept)  0.93 us
  transfers between devices with their start and end apart: 12, of which 5 were waited for; matrix products, arithmetic and copies ran while one was open for 3% of the time, Pallas kernels for 2%

profile of v7, /device:TPU:0, one launch (start us, length us, event | category | flops | bytes accessed | tf_op | source)
XLA Modules:
  0.0 34.1 jit_solution(4663219678908500812)
XLA Ops:
  0.6 0.0 copy-start
  0.6 2.6 %terms.1 = (f32[20,192,256]{2,1,0:T(8,128)S(1)}, bf16[6,192,128]{2,1,0:T(8,128)(2,1)S(1)}, bf16[6,96,128]{2,1,0:T(8,128)(2,1)S(1)}, bf16[6,96,128]{2,1,0:T(8,128...) custom-call(bf16[2,4,192,128]{3,2,1,0:T(8,128)(2,1)} %bitcast.2, ...), custom_call_target="tpu_custom_call" | custom-call | tf_op jit(solution)/shard_map/terms/pallas_call | solution.py:170
  3.3 3.0 %collective-permute-start.4 = (bf16[8,192,128]{2,1,0:T(8,128)(2,1)S(1)}, bf16[8,192,128]{2,1,0:T(8,128)(2,1)S(1)}, u32[]{:S(2)}, u32[]{:S(2)}) collective-permute-start(bf16[8,192,128]{2,1,0:T(8,128)(2,1)S(1)} %get-tuple-element.31), channel_id=1, source_target_pairs={{0,2},{1,3},{2,0},{3,1},{4,6},{5,7},{6,4},{7,5},{8,10},{9,11},{10,... | collective-permute-start | bytes 1179656 | tf_op jit(solution)/shard_map/ppermute | solution.py:158
  6.3 1.5 %collective-permute-start.2 = (bf16[6,96,128]{2,1,0:T(8,128)(2,1)S(1)}, bf16[6,96,128]{2,1,0:T(8,128)(2,1)S(1)}, u32[]{:S(2)}, u32[]{:S(2)}) collective-permute-start(bf16[6,96,128]{2,1,0:T(8,128)(2,1)S(1)} %get-tuple-element.28), channel_id=1, source_target_pairs={{0,4},{4,0},{8,12},{12,8},{16,20},{20,16},{24,28},{28,24},{1,5},{5... | collective-permute-start | bytes 442376 | tf_op jit(solution)/shard_map/ppermute | solution.py:154
  7.8 0.5 %collective-permute-start.6 = (bf16[6,96,128]{2,1,0:T(8,128)(2,1)S(1)}, bf16[6,96,128]{2,1,0:T(8,128)(2,1)S(1)}, u32[]{:S(2)}, u32[]{:S(2)}) collective-permute-start(bf16[6,96,128]{2,1,0:T(8,128)(2,1)S(1)} %get-tuple-element.34), channel_id=1, source_target_pairs={{0,4},{4,0},{8,12},{12,8},{16,20},{20,16},{24,28},{28,24},{1,5},{5... | collective-permute-start | bytes 442376 | tf_op jit(solution)/shard_map/ppermute | solution.py:154
  8.3 0.1 pack.1
  8.5 1.6 %collective-permute-start.1 = (bf16[6,192,128]{2,1,0:T(8,128)(2,1)S(1)}, bf16[6,192,128]{2,1,0:T(8,128)(2,1)S(1)}, u32[]{:S(2)}, u32[]{:S(2)}) collective-permute-start(bf16[6,192,128]{2,1,0:T(8,128)(2,1)S(1)} %get-tuple-element.26), channel_id=1, source_target_pairs={{0,4},{4,0},{8,12},{12,8},{16,20},{20,16},{24,28},{28,24},{1,5},{5... | collective-permute-start | bytes 884744 | tf_op jit(solution)/shard_map/ppermute | solution.py:154
  10.1 3.6 %collective-permute-start = (bf16[6,192,128]{2,1,0:T(8,128)(2,1)S(1)}, bf16[6,192,128]{2,1,0:T(8,128)(2,1)S(1)}, u32[]{:S(2)}, u32[]{:S(2)}) collective-permute-start(bf16[6,192,128]{2,1,0:T(8,128)(2,1)S(1)} %get-tuple-element.25), channel_id=1, source_target_pairs={{0,24},{4,12},{8,0},{12,20},{16,8},{20,28},{24,16},{28,4},{1,25},{... | collective-permute-start | bytes 884744 | tf_op jit(solution)/shard_map/ppermute | solution.py:154
  13.7 1.8 %collective-permute-done.4 = bf16[8,192,128]{2,1,0:T(8,128)(2,1)S(1)} collective-permute-done((bf16[8,192,128]{2,1,0:T(8,128)(2,1)S(1)}, bf16[8,192,128]{2,1,0:T(8,128)(2,1)S(1)}, u32[]{:S(2)}, u32[]{:S(2)}) %collective-permute-start.4) | collective-permute-done | bytes 393248 | tf_op jit(solution)/shard_map/ppermute | solution.py:158
  15.5 0.1 collective-permute-start.5
  15.6 0.0 collective-permute-done.2
  15.6 1.9 %collective-permute-start.3 = (bf16[6,96,128]{2,1,0:T(8,128)(2,1)S(1)}, bf16[6,96,128]{2,1,0:T(8,128)(2,1)S(1)}, u32[]{:S(2)}, u32[]{:S(2)}) collective-permute-start(bf16[6,96,128]{2,1,0:T(8,128)(2,1)S(1)} %add_convert_fusion.1), channel_id=1, source_target_pairs={{0,8},{4,28},{8,16},{12,4},{16,24},{20,12},{24,0},{28,20},{1,9},{5... | collective-permute-start | bytes 442376 | tf_op jit(solution)/shard_map/ppermute | solution.py:154
  17.5 0.0 collective-permute-done.6
  17.6 1.6 %collective-permute-start.7 = (bf16[6,96,128]{2,1,0:T(8,128)(2,1)S(1)}, bf16[6,96,128]{2,1,0:T(8,128)(2,1)S(1)}, u32[]{:S(2)}, u32[]{:S(2)}) collective-permute-start(bf16[6,96,128]{2,1,0:T(8,128)(2,1)S(1)} %add_convert_fusion), channel_id=1, source_target_pairs={{0,8},{4,28},{8,16},{12,4},{16,24},{20,12},{24,0},{28,20},{1,9},{5... | collective-permute-start | bytes 442376 | tf_op jit(solution)/shard_map/ppermute | solution.py:154
  19.2 5.1 %collective-permute-done.3.refs_4_ = bf16[6,96,128]{2,1,0:T(8,128)(2,1)S(1)} collective-permute-done((bf16[6,96,128]{2,1,0:T(8,128)(2,1)S(1)}, bf16[6,96,128]{2,1,0:T(8,128)(2,1)S(1)}, u32[]{:S(2)}, u32[]{:S(2)}) %collective-permute-start.3) | collective-permute-done | bytes 147488 | tf_op jit(solution)/shard_map/ppermute | solution.py:154
  24.3 0.0 collective-permute-done.1.refs_3_
  24.3 0.0 collective-permute-done.refs_2_
  24.3 0.0 collective-permute-done.5.refs_6_
  24.3 0.0 copy-done
  24.3 0.3 update.2
  24.6 0.1 collective-permute-start.9
  24.7 2.5 %collective-permute-done.7.refs_4_ = bf16[6,96,128]{2,1,0:T(8,128)(2,1)S(1)} collective-permute-done((bf16[6,96,128]{2,1,0:T(8,128)(2,1)S(1)}, bf16[6,96,128]{2,1,0:T(8,128)(2,1)S(1)}, u32[]{:S(2)}, u32[]{:S(2)}) %collective-permute-start.7) | collective-permute-done | bytes 147488 | tf_op jit(solution)/shard_map/ppermute | solution.py:154
  27.2 0.3 update.3
  27.6 0.9 %collective-permute-start.11 = (bf16[96,128]{1,0:T(8,128)(2,1)S(1)}, bf16[96,128]{1,0:T(8,128)(2,1)S(1)}, u32[]{:S(2)}, u32[]{:S(2)}) collective-permute-start(bf16[96,128]{1,0:T(8,128)(2,1)S(1)} %slice.23), channel_id=1, source_target_pairs={{0,3},{1,2},{2,1},{3,0},{4,7},{5,6},{6,5},{7,4},{8,11},{9,10},{10,... | collective-permute-start | bytes 73736 | tf_op jit(solution)/shard_map/ppermute | solution.py:232
  28.4 0.8 %collective-permute-start.8 = (bf16[192,128]{1,0:T(8,128)(2,1)S(1)}, bf16[192,128]{1,0:T(8,128)(2,1)S(1)}, u32[]{:S(2)}, u32[]{:S(2)}) collective-permute-start(bf16[192,128]{1,0:T(8,128)(2,1)S(1)} %get-tuple-element.41), channel_id=1, source_target_pairs={{0,1},{1,0},{2,3},{3,2},{4,5},{5,4},{6,7},{7,6},{8,9},{9,8},{10,11... | collective-permute-start | bytes 147464 | tf_op jit(solution)/shard_map/ppermute | solution.py:232
  29.2 0.0 collective-permute-done.9
  29.3 0.6 %collective-permute-start.10 = (bf16[192,128]{1,0:T(8,128)(2,1)S(1)}, bf16[192,128]{1,0:T(8,128)(2,1)S(1)}, u32[]{:S(2)}, u32[]{:S(2)}) collective-permute-start(bf16[192,128]{1,0:T(8,128)(2,1)S(1)} %pad_maximum_fusion.2), channel_id=1, source_target_pairs={{0,2},{1,3},{2,0},{3,1},{4,6},{5,7},{6,4},{7,5},{8,10},{9,11},{10,... | collective-permute-start | bytes 147464 | tf_op jit(solution)/shard_map/ppermute | solution.py:232
  29.9 0.9 %pad_maximum_fusion = f32[4,192,192]{2,1,0:T(8,128)} fusion(f32[4,96,192]{2,1,0:T(8,128)S(1)} %get-tuple-element.39, f32[4,96,192]{2,1,0:T(8,128)S(1)} %get-tuple-element.32), kind=kLoop, calls=%fused_computation | loop fusion | flops 147456 | bytes 1179648 | tf_op jit(solution)/shard_map/concatenate | solution.py:234
  30.8 0.3 collective-permute-done.11
  31.1 0.0 collective-permute-done.8
  31.1 2.4 %collective-permute-done.10 = bf16[192,128]{1,0:T(8,128)(2,1)S(1)} collective-permute-done((bf16[192,128]{1,0:T(8,128)(2,1)S(1)}, bf16[192,128]{1,0:T(8,128)(2,1)S(1)}, u32[]{:S(2)}, u32[]{:S(2)}) %collective-permute-start.10) | collective-permute-done | bytes 49184 | tf_op jit(solution)/shard_map/ppermute | solution.py:232
  33.4 0.7 %convert_add_fusion = f32[192,128]{1,0:T(8,128)} fusion(bf16[192,128]{1,0:T(8,128)(2,1)S(1)} %collective-permute-done.10, f32[192,128]{1,0:T(8,128)S(1)} %get-tuple-element.40, bf16[192,128]{1,0:T(8,128)(2,1)S(1)} %collective-permute-done.8, bf16[96,128]{1,0:T(8,128)(2,1)S(1)} %collective-permute-done.11), kind=kLoop, calls=%fused_computation.4 | loop fusion | flops 147456 | bytes 319488 | tf_op jit(solution)/shard_map/add | solution.py:233
  (9 shorter events, 0.2 us)
Async XLA Ops:
  0.6 23.6 %copy-start = (f32[4,192,192]{2,1,0:T(8,128)S(1)}, f32[4,192,192]{2,1,0:T(8,128)}, u32[]{:S(2)}) copy-start(f32[4,192,192]{2,1,0:T(8,128)} %refs_0_.3) | copy-start | bytes 1769476
  3.3 12.1 %collective-permute-start.4 = (bf16[8,192,128]{2,1,0:T(8,128)(2,1)S(1)}, bf16[8,192,128]{2,1,0:T(8,128)(2,1)S(1)}, u32[]{:S(2)}, u32[]{:S(2)}) collective-permute-start(bf16[8,192,128]{2,1,0:T(8,128)(2,1)S(1)} %get-tuple-element.31), channel_id=1, source_target_pairs={{0,2},{1,3},{2,0},{3,1},{4,6},{5,7},{6,4},{7,5},{8,10},{9,11},{10,... | collective-permute-start | bytes 1179656 | tf_op jit(solution)/shard_map/ppermute | solution.py:158
  6.3 9.3 %collective-permute-start.2 = (bf16[6,96,128]{2,1,0:T(8,128)(2,1)S(1)}, bf16[6,96,128]{2,1,0:T(8,128)(2,1)S(1)}, u32[]{:S(2)}, u32[]{:S(2)}) collective-permute-start(bf16[6,96,128]{2,1,0:T(8,128)(2,1)S(1)} %get-tuple-element.28), channel_id=1, source_target_pairs={{0,4},{4,0},{8,12},{12,8},{16,20},{20,16},{24,28},{28,24},{1,5},{5... | collective-permute-start | bytes 442376 | tf_op jit(solution)/shard_map/ppermute | solution.py:154
  7.8 9.7 %collective-permute-start.6 = (bf16[6,96,128]{2,1,0:T(8,128)(2,1)S(1)}, bf16[6,96,128]{2,1,0:T(8,128)(2,1)S(1)}, u32[]{:S(2)}, u32[]{:S(2)}) collective-permute-start(bf16[6,96,128]{2,1,0:T(8,128)(2,1)S(1)} %get-tuple-element.34), channel_id=1, source_target_pairs={{0,4},{4,0},{8,12},{12,8},{16,20},{20,16},{24,28},{28,24},{1,5},{5... | collective-permute-start | bytes 442376 | tf_op jit(solution)/shard_map/ppermute | solution.py:154
  8.5 15.8 %collective-permute-start.1 = (bf16[6,192,128]{2,1,0:T(8,128)(2,1)S(1)}, bf16[6,192,128]{2,1,0:T(8,128)(2,1)S(1)}, u32[]{:S(2)}, u32[]{:S(2)}) collective-permute-start(bf16[6,192,128]{2,1,0:T(8,128)(2,1)S(1)} %get-tuple-element.26), channel_id=1, source_target_pairs={{0,4},{4,0},{8,12},{12,8},{16,20},{20,16},{24,28},{28,24},{1,5},{5... | collective-permute-start | bytes 884744 | tf_op jit(solution)/shard_map/ppermute | solution.py:154
  10.1 14.2 %collective-permute-start = (bf16[6,192,128]{2,1,0:T(8,128)(2,1)S(1)}, bf16[6,192,128]{2,1,0:T(8,128)(2,1)S(1)}, u32[]{:S(2)}, u32[]{:S(2)}) collective-permute-start(bf16[6,192,128]{2,1,0:T(8,128)(2,1)S(1)} %get-tuple-element.25), channel_id=1, source_target_pairs={{0,24},{4,12},{8,0},{12,20},{16,8},{20,28},{24,16},{28,4},{1,25},{... | collective-permute-start | bytes 884744 | tf_op jit(solution)/shard_map/ppermute | solution.py:154
  15.5 8.8 %collective-permute-start.5 = (bf16[8,192,128]{2,1,0:T(8,128)(2,1)S(1)}, bf16[8,192,128]{2,1,0:T(8,128)(2,1)S(1)}, u32[]{:S(2)}, u32[]{:S(2)}) collective-permute-start(bf16[8,192,128]{2,1,0:T(8,128)(2,1)S(1)} %pad_maximum_fusion.1), channel_id=1, source_target_pairs={{0,1},{1,0},{2,3},{3,2},{4,5},{5,4},{6,7},{7,6},{8,9},{9,8},{10,11... | collective-permute-start | bytes 1179656 | tf_op jit(solution)/shard_map/ppermute | solution.py:161
  15.6 8.6 %collective-permute-start.3 = (bf16[6,96,128]{2,1,0:T(8,128)(2,1)S(1)}, bf16[6,96,128]{2,1,0:T(8,128)(2,1)S(1)}, u32[]{:S(2)}, u32[]{:S(2)}) collective-permute-start(bf16[6,96,128]{2,1,0:T(8,128)(2,1)S(1)} %add_convert_fusion.1), channel_id=1, source_target_pairs={{0,8},{4,28},{8,16},{12,4},{16,24},{20,12},{24,0},{28,20},{1,9},{5... | collective-permute-start | bytes 442376 | tf_op jit(solution)/shard_map/ppermute | solution.py:154
  17.6 9.6 %collective-permute-start.7 = (bf16[6,96,128]{2,1,0:T(8,128)(2,1)S(1)}, bf16[6,96,128]{2,1,0:T(8,128)(2,1)S(1)}, u32[]{:S(2)}, u32[]{:S(2)}) collective-permute-start(bf16[6,96,128]{2,1,0:T(8,128)(2,1)S(1)} %add_convert_fusion), channel_id=1, source_target_pairs={{0,8},{4,28},{8,16},{12,4},{16,24},{20,12},{24,0},{28,20},{1,9},{5... | collective-permute-start | bytes 442376 | tf_op jit(solution)/shard_map/ppermute | solution.py:154
  24.6 4.6 %collective-permute-start.9 = (bf16[96,128]{1,0:T(8,128)(2,1)S(1)}, bf16[96,128]{1,0:T(8,128)(2,1)S(1)}, u32[]{:S(2)}, u32[]{:S(2)}) collective-permute-start(bf16[96,128]{1,0:T(8,128)(2,1)S(1)} %slice.21), channel_id=1, source_target_pairs={{0,1},{1,0},{2,3},{3,2},{4,5},{5,4},{6,7},{7,6},{8,9},{9,8},{10,11... | collective-permute-start | bytes 73736 | tf_op jit(solution)/shard_map/ppermute | solution.py:161
  27.6 3.5 %collective-permute-start.11 = (bf16[96,128]{1,0:T(8,128)(2,1)S(1)}, bf16[96,128]{1,0:T(8,128)(2,1)S(1)}, u32[]{:S(2)}, u32[]{:S(2)}) collective-permute-start(bf16[96,128]{1,0:T(8,128)(2,1)S(1)} %slice.23), channel_id=1, source_target_pairs={{0,3},{1,2},{2,1},{3,0},{4,7},{5,6},{6,5},{7,4},{8,11},{9,10},{10,... | collective-permute-start | bytes 73736 | tf_op jit(solution)/shard_map/ppermute | solution.py:232
  28.4 2.6 %collective-permute-start.8 = (bf16[192,128]{1,0:T(8,128)(2,1)S(1)}, bf16[192,128]{1,0:T(8,128)(2,1)S(1)}, u32[]{:S(2)}, u32[]{:S(2)}) collective-permute-start(bf16[192,128]{1,0:T(8,128)(2,1)S(1)} %get-tuple-element.41), channel_id=1, source_target_pairs={{0,1},{1,0},{2,3},{3,2},{4,5},{5,4},{6,7},{7,6},{8,9},{9,8},{10,11... | collective-permute-start | bytes 147464 | tf_op jit(solution)/shard_map/ppermute | solution.py:232
  29.3 4.2 %collective-permute-start.10 = (bf16[192,128]{1,0:T(8,128)(2,1)S(1)}, bf16[192,128]{1,0:T(8,128)(2,1)S(1)}, u32[]{:S(2)}, u32[]{:S(2)}) collective-permute-start(bf16[192,128]{1,0:T(8,128)(2,1)S(1)} %pad_maximum_fusion.2), channel_id=1, source_target_pairs={{0,2},{1,3},{2,0},{3,1},{4,6},{5,7},{6,4},{7,5},{8,10},{9,11},{10,... | collective-permute-start | bytes 147464 | tf_op jit(solution)/shard_map/ppermute | solution.py:232

commit v8 on v6

--- a/solution.py
+++ b/solution.py
@@ -105,31 +105,43 @@
 
 
 def update_kernel(chunk, outer_count, *refs):
-    blocks_ref, own_ref, direct_ref, near_ref, comb_ref, kept_w, peer_w = refs[:7]
-    outer_w = refs[7 : 6 + outer_count]
+    count = 7 if chunk == 0 else 4
+    *whole_refs, comb_ref, kept_w, peer_w = refs[:count]
+    outer_w = refs[count : count + outer_count - 1]
     updated_ref, kept_ref, *part_refs = refs[-1 - 2 * outer_count :]
-    slots, skeleton, _ = own_ref.shape
+    slots, skeleton, _ = whole_refs[0].shape
     span = slice(*chunk_rows(skeleton)[chunk])
     tail = skeleton - LANES
 
-    def received(row):
-        return near_ref[row, span].astype(jnp.float32) + direct_ref[row, span].astype(jnp.float32) + comb_ref[row].astype(jnp.float32)
+    def unpack(read, two, half):
+        tails = read(slots + two)[:, half * tail : (half + 1) * tail]
+        return jnp.concatenate([read(2 * two + half), tails], axis=1)
+
+    def remaining(two, half, where):
+        slot = 2 * two + half
+        if chunk:
+            return whole_refs[0][slot, where]
+        blocks_ref, own_ref, direct_ref, near_ref = whole_refs
+        both = unpack(lambda row: near_ref[row, where].astype(jnp.float32) + direct_ref[row, where].astype(jnp.float32), two, half)
+        return blocks_ref[slot, where] - own_ref[slot, where] - both
 
     panels = [((kept_w, 0), (peer_w, 0))]
     panels += [((outer_w[shift - 1], 0), (peer_w, shift * slots)) for shift in range(1, outer_count)]
     total = [None] * len(panels)
     for two in range(slots // 2):
-        tails = received(slots + two)
         for half in range(2):
             slot = 2 * two + half
-            gone = jnp.concatenate([received(slot), tails[:, half * tail : (half + 1) * tail]], axis=1)
-            updated = blocks_ref[slot, span] - own_ref[slot, span] - gone
+            updated = remaining(two, half, span) - unpack(lambda row: comb_ref[row].astype(jnp.float32), two, half)
             updated_ref[slot] = updated
             rounded = updated.astype(jnp.bfloat16)
             for at, pair in enumerate(panels):
                 panel = jnp.concatenate([ref[base + slot] for ref, base in pair], axis=1)
                 part = jnp.dot(rounded, panel, preferred_element_type=jnp.float32)
                 total[at] = part if total[at] is None else total[at] + part
+    if chunk == 0:
+        rest = slice(span.stop, skeleton)
+        for slot in range(slots):
+            refs[-2 - 2 * outer_count][slot, rest] = remaining(slot // 2, slot % 2, rest)
     columns = kept_ref.shape[-1]
     for at, ref in enumerate((kept_ref, *part_refs)):
         ref[span] = total[at // 2][:, at % 2 * columns : (at % 2 + 1) * columns].astype(ref.dtype)
@@ -204,19 +216,22 @@
         merged = (comb[chunk].astype(jnp.float32) + far[chunk].astype(jnp.float32)).astype(jnp.bfloat16)
         comb[chunk] = to_tile(merged, 2, -2)
 
-    updated, sums = [], []
+    updated, sums, base = [], [], None
     for chunk in range(CHUNKS):
-        inputs = [blocks, own, direct, near, comb[chunk], kept_w, peer_w, *outer_w]
-        fresh, *sums = pl.pallas_call(
+        inputs = [*([base] if chunk else [blocks, own, direct, near]), comb[chunk], kept_w, peer_w, *outer_w]
+        extra = [] if chunk else [shape(*blocks.shape, dtype=jnp.float32)]
+        out = pl.pallas_call(
             functools.partial(update_kernel, chunk, outer_count),
-            out_shape=[shape(slots, rows[chunk], skeleton, dtype=jnp.float32), shape(skeleton, columns, dtype=jnp.float32)]
+            out_shape=extra + [shape(slots, rows[chunk], skeleton, dtype=jnp.float32), shape(skeleton, columns, dtype=jnp.float32)]
             + [shape(skeleton, columns)] * (pair_count - 1),
             in_specs=[vmem] * (len(inputs) + len(sums)),
-            out_specs=[vmem] * (1 + pair_count),
+            out_specs=[vmem] * (len(extra) + 1 + pair_count),
             input_output_aliases={len(inputs) + at: 1 + at for at in range(len(sums))},
             compiler_params=pltpu.CompilerParams(vmem_limit_bytes=8 << 20),
             name="update",
         )(*inputs, *sums)
+        base = base if chunk else out[0]
+        fresh, *sums = out[len(extra) :]
         updated.append(fresh)
     kept, *parts = sums
     for at, piece in enumerate(parts, 1):

time: 33.7 us -> 33.7 us (level)
  no operation moved by 1% of the time
where the time goes in v8:
time: 33.7 us; the launch traced here: 33.5 us
  starting transfers between devices  15.7 us (47%)
  waiting for transfers between devices  11.9 us (35%)
  Pallas kernels  3.4 us (10%)
  other arithmetic  1.72 us (5%)
  between operations  0.73 us (2%)
    ppermute x6, starting transfers between devices, to_tile(): return lax.ppermute(piece, 'surf', moves)  10.7 us
    ppermute x6, waiting for transfers between devices, to_tile(): return lax.ppermute(piece, 'surf', moves)  7.67 us
    ppermute x1, starting transfers between devices, to_outer(): return lax.ppermute(piece, 'pair', moves)  3.03 us
    pallas_call x1, Pallas kernels, body(): pl.pallas_call(functools.partial(terms_kernel, surf_count, pair_count), o...  2.63 us
    ppermute x3, waiting for transfers between devices, body(): kept = kept + lax.ppermute(piece, 'pair', moves).astype(jnp.float32)  2.48 us
    ppermute x3, starting transfers between devices, body(): kept = kept + lax.ppermute(piece, 'pair', moves).astype(jnp.float32)  1.92 us
    ppermute x1, waiting for transfers between devices, to_outer(): return lax.ppermute(piece, 'pair', moves)  1.76 us
    concatenate x1, other arithmetic, body(): return (jnp.concatenate(updated, axis=1), kept)  0.93 us
  transfers between devices with their start and end apart: 11, of which 5 were waited for; matrix products, arithmetic and copies ran while one was open for 3% of the time, Pallas kernels for 1%

profile of v8, /device:TPU:0, one launch (start us, length us, event | category | flops | bytes accessed | tf_op | source)
XLA Modules:
  0.0 33.5 jit_solution(16926182860002754352)
XLA Ops:
  0.6 0.0 copy-start
  0.6 2.6 %terms.1 = (f32[20,192,256]{2,1,0:T(8,128)S(1)}, bf16[6,192,128]{2,1,0:T(8,128)(2,1)S(1)}, bf16[6,96,128]{2,1,0:T(8,128)(2,1)S(1)}, bf16[6,96,128]{2,1,0:T(8,128...) custom-call(bf16[2,4,192,128]{3,2,1,0:T(8,128)(2,1)} %bitcast.2, ...), custom_call_target="tpu_custom_call" | custom-call | tf_op jit(solution)/shard_map/terms/pallas_call | solution.py:182
  3.3 3.0 %collective-permute-start.4 = (bf16[8,192,128]{2,1,0:T(8,128)(2,1)S(1)}, bf16[8,192,128]{2,1,0:T(8,128)(2,1)S(1)}, u32[]{:S(2)}, u32[]{:S(2)}) collective-permute-start(bf16[8,192,128]{2,1,0:T(8,128)(2,1)S(1)} %get-tuple-element.32), channel_id=1, source_target_pairs={{0,2},{1,3},{2,0},{3,1},{4,6},{5,7},{6,4},{7,5},{8,10},{9,11},{10,... | collective-permute-start | bytes 1179656 | tf_op jit(solution)/shard_map/ppermute | solution.py:170
  6.3 1.5 %collective-permute-start.2 = (bf16[6,96,128]{2,1,0:T(8,128)(2,1)S(1)}, bf16[6,96,128]{2,1,0:T(8,128)(2,1)S(1)}, u32[]{:S(2)}, u32[]{:S(2)}) collective-permute-start(bf16[6,96,128]{2,1,0:T(8,128)(2,1)S(1)} %get-tuple-element.29), channel_id=1, source_target_pairs={{0,4},{4,0},{8,12},{12,8},{16,20},{20,16},{24,28},{28,24},{1,5},{5... | collective-permute-start | bytes 442376 | tf_op jit(solution)/shard_map/ppermute | solution.py:166
  7.8 0.5 %collective-permute-start.6 = (bf16[6,96,128]{2,1,0:T(8,128)(2,1)S(1)}, bf16[6,96,128]{2,1,0:T(8,128)(2,1)S(1)}, u32[]{:S(2)}, u32[]{:S(2)}) collective-permute-start(bf16[6,96,128]{2,1,0:T(8,128)(2,1)S(1)} %get-tuple-element.36), channel_id=1, source_target_pairs={{0,4},{4,0},{8,12},{12,8},{16,20},{20,16},{24,28},{28,24},{1,5},{5... | collective-permute-start | bytes 442376 | tf_op jit(solution)/shard_map/ppermute | solution.py:166
  8.3 0.1 pack.1
  8.5 1.6 %collective-permute-start.1 = (bf16[6,192,128]{2,1,0:T(8,128)(2,1)S(1)}, bf16[6,192,128]{2,1,0:T(8,128)(2,1)S(1)}, u32[]{:S(2)}, u32[]{:S(2)}) collective-permute-start(bf16[6,192,128]{2,1,0:T(8,128)(2,1)S(1)} %get-tuple-element.27), channel_id=1, source_target_pairs={{0,4},{4,0},{8,12},{12,8},{16,20},{20,16},{24,28},{28,24},{1,5},{5... | collective-permute-start | bytes 884744 | tf_op jit(solution)/shard_map/ppermute | solution.py:166
  10.1 3.6 %collective-permute-start = (bf16[6,192,128]{2,1,0:T(8,128)(2,1)S(1)}, bf16[6,192,128]{2,1,0:T(8,128)(2,1)S(1)}, u32[]{:S(2)}, u32[]{:S(2)}) collective-permute-start(bf16[6,192,128]{2,1,0:T(8,128)(2,1)S(1)} %get-tuple-element.26), channel_id=1, source_target_pairs={{0,24},{4,12},{8,0},{12,20},{16,8},{20,28},{24,16},{28,4},{1,25},{... | collective-permute-start | bytes 884744 | tf_op jit(solution)/shard_map/ppermute | solution.py:166
  13.7 1.8 %collective-permute-done.4 = bf16[8,192,128]{2,1,0:T(8,128)(2,1)S(1)} collective-permute-done((bf16[8,192,128]{2,1,0:T(8,128)(2,1)S(1)}, bf16[8,192,128]{2,1,0:T(8,128)(2,1)S(1)}, u32[]{:S(2)}, u32[]{:S(2)}) %collective-permute-start.4) | collective-permute-done | bytes 393248 | tf_op jit(solution)/shard_map/ppermute | solution.py:170
  15.5 0.1 collective-permute-start.5
  15.6 0.0 collective-permute-done.2
  15.6 1.9 %collective-permute-start.3 = (bf16[6,96,128]{2,1,0:T(8,128)(2,1)S(1)}, bf16[6,96,128]{2,1,0:T(8,128)(2,1)S(1)}, u32[]{:S(2)}, u32[]{:S(2)}) collective-permute-start(bf16[6,96,128]{2,1,0:T(8,128)(2,1)S(1)} %add_convert_fusion.1), channel_id=1, source_target_pairs={{0,8},{4,28},{8,16},{12,4},{16,24},{20,12},{24,0},{28,20},{1,9},{5... | collective-permute-start | bytes 442376 | tf_op jit(solution)/shard_map/ppermute | solution.py:166
  17.5 0.0 collective-permute-done.6
  17.6 1.6 %collective-permute-start.7 = (bf16[6,96,128]{2,1,0:T(8,128)(2,1)S(1)}, bf16[6,96,128]{2,1,0:T(8,128)(2,1)S(1)}, u32[]{:S(2)}, u32[]{:S(2)}) collective-permute-start(bf16[6,96,128]{2,1,0:T(8,128)(2,1)S(1)} %add_convert_fusion), channel_id=1, source_target_pairs={{0,8},{4,28},{8,16},{12,4},{16,24},{20,12},{24,0},{28,20},{1,9},{5... | collective-permute-start | bytes 442376 | tf_op jit(solution)/shard_map/ppermute | solution.py:166
  19.2 5.1 %collective-permute-done.3.refs_4_ = bf16[6,96,128]{2,1,0:T(8,128)(2,1)S(1)} collective-permute-done((bf16[6,96,128]{2,1,0:T(8,128)(2,1)S(1)}, bf16[6,96,128]{2,1,0:T(8,128)(2,1)S(1)}, u32[]{:S(2)}, u32[]{:S(2)}) %collective-permute-start.3) | collective-permute-done | bytes 147488 | tf_op jit(solution)/shard_map/ppermute | solution.py:166
  24.3 0.0 collective-permute-done.1.refs_3_
  24.3 0.0 collective-permute-done.refs_2_
  24.3 0.0 collective-permute-done.5.refs_6_.refs_3_
  24.3 0.0 copy-done
  24.3 0.3 update.2
  24.6 2.6 %collective-permute-done.7.refs_1_ = bf16[6,96,128]{2,1,0:T(8,128)(2,1)S(1)} collective-permute-done((bf16[6,96,128]{2,1,0:T(8,128)(2,1)S(1)}, bf16[6,96,128]{2,1,0:T(8,128)(2,1)S(1)}, u32[]{:S(2)}, u32[]{:S(2)}) %collective-permute-start.7) | collective-permute-done | bytes 147488 | tf_op jit(solution)/shard_map/ppermute | solution.py:166
  27.2 0.3 update.3
  27.5 0.1 collective-permute-start.8
  27.6 1.6 %collective-permute-start.9 = (bf16[192,128]{1,0:T(8,128)(2,1)S(1)}, bf16[192,128]{1,0:T(8,128)(2,1)S(1)}, u32[]{:S(2)}, u32[]{:S(2)}) collective-permute-start(bf16[192,128]{1,0:T(8,128)(2,1)S(1)} %get-tuple-element.44), channel_id=1, source_target_pairs={{0,2},{1,3},{2,0},{3,1},{4,6},{5,7},{6,4},{7,5},{8,10},{9,11},{10,... | collective-permute-start | bytes 147464 | tf_op jit(solution)/shard_map/ppermute | solution.py:240
  29.2 0.3 collective-permute-start.10
  29.5 0.9 %pad_maximum_fusion = f32[4,192,192]{2,1,0:T(8,128)} fusion(f32[4,96,192]{2,1,0:T(8,128)S(1)} %get-tuple-element.41, f32[4,96,192]{2,1,0:T(8,128)S(1)} %get-tuple-element.33), kind=kLoop, calls=%fused_computation | loop fusion | flops 147456 | bytes 1179648 | tf_op jit(solution)/shard_map/concatenate | solution.py:241
  30.4 0.0 collective-permute-done.8
  30.4 1.4 %collective-permute-done.9 = bf16[192,128]{1,0:T(8,128)(2,1)S(1)} collective-permute-done((bf16[192,128]{1,0:T(8,128)(2,1)S(1)}, bf16[192,128]{1,0:T(8,128)(2,1)S(1)}, u32[]{:S(2)}, u32[]{:S(2)}) %collective-permute-start.9) | collective-permute-done | bytes 49184 | tf_op jit(solution)/shard_map/ppermute | solution.py:240
  31.8 1.1 %collective-permute-done.10 = bf16[192,128]{1,0:T(8,128)(2,1)S(1)} collective-permute-done((bf16[192,128]{1,0:T(8,128)(2,1)S(1)}, bf16[192,128]{1,0:T(8,128)(2,1)S(1)}, u32[]{:S(2)}, u32[]{:S(2)}) %collective-permute-start.10) | collective-permute-done | bytes 49184 | tf_op jit(solution)/shard_map/ppermute | solution.py:240
  32.9 0.7 %convert_add_fusion = f32[192,128]{1,0:T(8,128)} fusion(bf16[192,128]{1,0:T(8,128)(2,1)S(1)} %collective-permute-done.10, bf16[192,128]{1,0:T(8,128)(2,1)S(1)} %collective-permute-done.9, f32[192,128]{1,0:T(8,128)S(1)} %get-tuple-element.42, bf16[192,128]{1,0:T(8,128)(2,1)S(1)} %collective-permute-done.8), kind=kLoop, calls=%fused_computation.4 | loop fusion | flops 147456 | bytes 344064 | tf_op jit(solution)/shard_map/add | solution.py:240
  (4 shorter events, 0.1 us)
Async XLA Ops:
  0.6 23.6 %copy-start = (f32[4,192,192]{2,1,0:T(8,128)S(1)}, f32[4,192,192]{2,1,0:T(8,128)}, u32[]{:S(2)}) copy-start(f32[4,192,192]{2,1,0:T(8,128)} %refs_0_.1) | copy-start | bytes 1769476
  3.3 12.1 %collective-permute-start.4 = (bf16[8,192,128]{2,1,0:T(8,128)(2,1)S(1)}, bf16[8,192,128]{2,1,0:T(8,128)(2,1)S(1)}, u32[]{:S(2)}, u32[]{:S(2)}) collective-permute-start(bf16[8,192,128]{2,1,0:T(8,128)(2,1)S(1)} %get-tuple-element.32), channel_id=1, source_target_pairs={{0,2},{1,3},{2,0},{3,1},{4,6},{5,7},{6,4},{7,5},{8,10},{9,11},{10,... | collective-permute-start | bytes 1179656 | tf_op jit(solution)/shard_map/ppermute | solution.py:170
  6.3 9.3 %collective-permute-start.2 = (bf16[6,96,128]{2,1,0:T(8,128)(2,1)S(1)}, bf16[6,96,128]{2,1,0:T(8,128)(2,1)S(1)}, u32[]{:S(2)}, u32[]{:S(2)}) collective-permute-start(bf16[6,96,128]{2,1,0:T(8,128)(2,1)S(1)} %get-tuple-element.29), channel_id=1, source_target_pairs={{0,4},{4,0},{8,12},{12,8},{16,20},{20,16},{24,28},{28,24},{1,5},{5... | collective-permute-start | bytes 442376 | tf_op jit(solution)/shard_map/ppermute | solution.py:166
  7.8 9.7 %collective-permute-start.6 = (bf16[6,96,128]{2,1,0:T(8,128)(2,1)S(1)}, bf16[6,96,128]{2,1,0:T(8,128)(2,1)S(1)}, u32[]{:S(2)}, u32[]{:S(2)}) collective-permute-start(bf16[6,96,128]{2,1,0:T(8,128)(2,1)S(1)} %get-tuple-element.36), channel_id=1, source_target_pairs={{0,4},{4,0},{8,12},{12,8},{16,20},{20,16},{24,28},{28,24},{1,5},{5... | collective-permute-start | bytes 442376 | tf_op jit(solution)/shard_map/ppermute | solution.py:166
  8.5 15.8 %collective-permute-start.1 = (bf16[6,192,128]{2,1,0:T(8,128)(2,1)S(1)}, bf16[6,192,128]{2,1,0:T(8,128)(2,1)S(1)}, u32[]{:S(2)}, u32[]{:S(2)}) collective-permute-start(bf16[6,192,128]{2,1,0:T(8,128)(2,1)S(1)} %get-tuple-element.27), channel_id=1, source_target_pairs={{0,4},{4,0},{8,12},{12,8},{16,20},{20,16},{24,28},{28,24},{1,5},{5... | collective-permute-start | bytes 884744 | tf_op jit(solution)/shard_map/ppermute | solution.py:166
  10.1 14.2 %collective-permute-start = (bf16[6,192,128]{2,1,0:T(8,128)(2,1)S(1)}, bf16[6,192,128]{2,1,0:T(8,128)(2,1)S(1)}, u32[]{:S(2)}, u32[]{:S(2)}) collective-permute-start(bf16[6,192,128]{2,1,0:T(8,128)(2,1)S(1)} %get-tuple-element.26), channel_id=1, source_target_pairs={{0,24},{4,12},{8,0},{12,20},{16,8},{20,28},{24,16},{28,4},{1,25},{... | collective-permute-start | bytes 884744 | tf_op jit(solution)/shard_map/ppermute | solution.py:166
  15.5 8.8 %collective-permute-start.5 = (bf16[8,192,128]{2,1,0:T(8,128)(2,1)S(1)}, bf16[8,192,128]{2,1,0:T(8,128)(2,1)S(1)}, u32[]{:S(2)}, u32[]{:S(2)}) collective-permute-start(bf16[8,192,128]{2,1,0:T(8,128)(2,1)S(1)} %pad_maximum_fusion.1), channel_id=1, source_target_pairs={{0,1},{1,0},{2,3},{3,2},{4,5},{5,4},{6,7},{7,6},{8,9},{9,8},{10,11... | collective-permute-start | bytes 1179656 | tf_op jit(solution)/shard_map/ppermute | solution.py:173
  15.6 8.6 %collective-permute-start.3 = (bf16[6,96,128]{2,1,0:T(8,128)(2,1)S(1)}, bf16[6,96,128]{2,1,0:T(8,128)(2,1)S(1)}, u32[]{:S(2)}, u32[]{:S(2)}) collective-permute-start(bf16[6,96,128]{2,1,0:T(8,128)(2,1)S(1)} %add_convert_fusion.1), channel_id=1, source_target_pairs={{0,8},{4,28},{8,16},{12,4},{16,24},{20,12},{24,0},{28,20},{1,9},{5... | collective-permute-start | bytes 442376 | tf_op jit(solution)/shard_map/ppermute | solution.py:166
  17.6 9.6 %collective-permute-start.7 = (bf16[6,96,128]{2,1,0:T(8,128)(2,1)S(1)}, bf16[6,96,128]{2,1,0:T(8,128)(2,1)S(1)}, u32[]{:S(2)}, u32[]{:S(2)}) collective-permute-start(bf16[6,96,128]{2,1,0:T(8,128)(2,1)S(1)} %add_convert_fusion), channel_id=1, source_target_pairs={{0,8},{4,28},{8,16},{12,4},{16,24},{20,12},{24,0},{28,20},{1,9},{5... | collective-permute-start | bytes 442376 | tf_op jit(solution)/shard_map/ppermute | solution.py:166
  27.5 2.9 %collective-permute-start.8 = (bf16[192,128]{1,0:T(8,128)(2,1)S(1)}, bf16[192,128]{1,0:T(8,128)(2,1)S(1)}, u32[]{:S(2)}, u32[]{:S(2)}) collective-permute-start(bf16[192,128]{1,0:T(8,128)(2,1)S(1)} %get-tuple-element.43), channel_id=1, source_target_pairs={{0,1},{1,0},{2,3},{3,2},{4,5},{5,4},{6,7},{7,6},{8,9},{9,8},{10,11... | collective-permute-start | bytes 147464 | tf_op jit(solution)/shard_map/ppermute | solution.py:240
  27.6 4.2 %collective-permute-start.9 = (bf16[192,128]{1,0:T(8,128)(2,1)S(1)}, bf16[192,128]{1,0:T(8,128)(2,1)S(1)}, u32[]{:S(2)}, u32[]{:S(2)}) collective-permute-start(bf16[192,128]{1,0:T(8,128)(2,1)S(1)} %get-tuple-element.44), channel_id=1, source_target_pairs={{0,2},{1,3},{2,0},{3,1},{4,6},{5,7},{6,4},{7,5},{8,10},{9,11},{10,... | collective-permute-start | bytes 147464 | tf_op jit(solution)/shard_map/ppermute | solution.py:240
  29.2 3.7 %collective-permute-start.10 = (bf16[192,128]{1,0:T(8,128)(2,1)S(1)}, bf16[192,128]{1,0:T(8,128)(2,1)S(1)}, u32[]{:S(2)}, u32[]{:S(2)}) collective-permute-start(bf16[192,128]{1,0:T(8,128)(2,1)S(1)} %get-tuple-element.45), channel_id=1, source_target_pairs={{0,3},{1,2},{2,1},{3,0},{4,7},{5,6},{6,5},{7,4},{8,11},{9,10},{10,... | collective-permute-start | bytes 147464 | tf_op jit(solution)/shard_map/ppermute | solution.py:240
